TPU v7x, 512 devices: a whole 4x4x16 slice. The times are simulated.
512 devices in a mesh: grp: 16 (over z), cand: 32 (over y, x, core).
Axes of the slice: x: 4, y: 4, z: 16, core: 2. Of those that a mesh axis runs over, the one named last changes fastest.
Arguments:
- embeddings: bfloat16 [384, 1024, 1024], P('grp', 'cand'), may hold values from -6 to 6
- hidden_weight: bfloat16 [2048, 1024], P('cand'), may hold values from -0.1875 to 0.1875
- score_weight: bfloat16 [2048], replicated, may hold values from -0.5 to 0.5
- relevance: int32 [384, 1024], P('grp', 'cand'), may hold values from 0 to 4
- rank_pos: int32 [384, 1024], P('grp', 'cand'), may hold values from 0 to 1023, as said below
- ideal_dcg: float32 [384], P('grp'), may hold values from 32 to 128
Outputs:
- grad_hidden: float32 [2048, 1024], P('cand')
- lambdas: float32 [384, 1024], P('grp', 'cand')
Inputs may be any that keep to these rules, and one draw needn't show every extreme that they name: `rank_pos`: in each group the rank positions are a permutation of 0 to 1023.
All inputs are finite; a program needn't handle non-finite values.
Results may differ from a plain program's by a relative error of at most 0.006.
Values may be sent and summed in bfloat16 or wider, within the bound.
No kernel may reach another device: no remote copies, remote signals or barrier semaphores. Data moves between devices by JAX's collectives and lax.ppermute only.
A program may use at most 64 MiB of HBM per device.

v0:
```python
import jax
import jax.numpy as jnp
from jax import lax
from jax.sharding import PartitionSpec as P

EPS = 1e-06


def turned_gather(arrays, axis, dims):
    turned = [jnp.moveaxis(a, dim, 0) for a, dim in zip(arrays, dims)]
    widths = [t[0].size for t in turned]
    both = jnp.concatenate([t.reshape(-1, w) for t, w in zip(turned, widths)], axis=1)
    result = lax.all_gather(both, axis, axis=0, tiled=True)
    parts = jnp.split(result, [sum(widths[:k]) for k in range(1, len(widths))], axis=1)
    return tuple(
        (
            jnp.moveaxis(b.reshape(-1, *t.shape[1:]), 0, dim)
            for b, t, dim in zip(parts, turned, dims)
        )
    )


def copy_for_each(value, axis):
    copies = jnp.broadcast_to(value, (lax.axis_size(axis), *value.shape))
    return lax.all_to_all(copies, axis, split_axis=0, concat_axis=0, tiled=True)


def joined_along(parts, dim):
    parts = jnp.moveaxis(parts, 0, dim)
    shape = parts.shape
    return parts.reshape(*shape[:dim], shape[dim] * shape[dim + 1], *shape[dim + 2 :])


def gathered_copies(value, axis, dim):
    parts = copy_for_each(value, axis)
    return joined_along(parts, dim)


def over_copies(value, axis):
    return copy_for_each(value, axis).sum(axis=0)


def pair_lambdas(own_score, own_gain, own_disc, far_score, far_gain, far_disc, ideal):
    gain_diff = far_gain[..., None, :] - own_gain[..., :, None]
    toward = jnp.sign(gain_diff)
    weight = (
        jnp.abs(gain_diff)
        * jnp.abs(far_disc[..., None, :] - own_disc[..., :, None])
        / ideal[..., None, None]
    )
    margin = own_score[..., :, None] - far_score[..., None, :]
    return jnp.sum(weight * toward * jax.nn.sigmoid(toward * margin), axis=-1)


def gain_of(labels):
    return jnp.exp2(labels.astype(jnp.float32)) - 1.0


def discount_of(positions):
    return 1.0 / jnp.log2(2.0 + positions.astype(jnp.float32))


def per_device(embeddings, hidden_weight, score_weight, relevance, rank_pos, ideal_dcg):
    grp_count, local, width = embeddings.shape
    cand_rows = embeddings.reshape(grp_count * local, width)
    all_labels, all_ranks = turned_gather((relevance, rank_pos), "cand", (1, 1))
    all_gain = gain_of(all_labels)
    all_disc = discount_of(all_ranks)
    pre_act = lax.dot_general(
        cand_rows,
        lax.all_gather(hidden_weight, "cand", axis=0, tiled=True),
        (((1,), (1,)), ((), ())),
        preferred_element_type=jnp.float32,
    )
    acts, pull = jax.vjp(jax.nn.gelu, pre_act)
    scores = jnp.dot(
        acts.astype(jnp.bfloat16), score_weight, preferred_element_type=jnp.float32
    ).reshape(grp_count, local)
    gain_vals = gain_of(relevance)
    discount = discount_of(rank_pos)
    lambdas = pair_lambdas(
        scores,
        gain_vals,
        discount,
        gathered_copies(scores, "cand", 1),
        all_gain,
        all_disc,
        ideal_dcg,
    )
    upstream = (
        lambdas.reshape(grp_count * local)[:, None] * score_weight.astype(jnp.float32)[None, :]
    )
    grad_pre = pull(upstream)[0].astype(jnp.bfloat16)
    owned = lax.psum_scatter(
        lax.dot_general(
            grad_pre, cand_rows, (((0,), (0,)), ((), ())), preferred_element_type=jnp.float32
        ).astype(jnp.bfloat16),
        "cand",
        scatter_dimension=0,
        tiled=True,
    ).astype(jnp.float32)
    summed = lax.psum(owned, "grp")
    squares = over_copies(jnp.sum(summed * summed), "cand")
    entries = summed.shape[0] * summed.shape[1] * lax.axis_size("cand")
    scale = lax.rsqrt(squares / entries + EPS)
    return (summed * scale, lambdas)


def solution(mesh):
    return jax.shard_map(
        per_device,
        mesh=mesh,
        in_specs=(
            P("grp", "cand", None),
            P("cand", None),
            P(),
            P("grp", "cand"),
            P("grp", "cand"),
            P("grp"),
        ),
        out_specs=(P("cand", None), P("grp", "cand")),
        check_vma=False,
    )
```

profile of v0, /device:TPU:1, one launch (start us, length us, event | category | flops | bytes accessed | tf_op | source)
XLA Modules:
  0.0 302.9 jit_solution(5547443069772350048)
XLA Ops:
  7.2 0.0 copy-start
  7.2 0.0 all-gather.2.cloned.1.call-start
  7.2 0.7 all-gather.2.cloned.1.call-update
  7.9 0.7 reshape.20
  8.6 0.8 copy.28
  9.4 0.8 copy.29
  10.2 0.1 pad_add_fusion
  10.2 28.5 %all_gather.6 = s32[1024,48]{1,0:T(8,128)S(1)} all-gather(s32[32,48]{1,0:T(8,128)S(1)} %pad_add_fusion), channel_id=1, replica_groups=mesh['grp'=16,'cand'=32] {'cand'}, dimensions={0}, use_global_device_ids=true | all-gather | bytes 202752 | tf_op jit(solution)/shard_map/all_gather | solution.py:13
  38.7 0.2 fusion.33
  38.9 0.2 copy.35
  39.1 0.2 copy.36
  39.3 0.1 divide_bitcast_fusion
  39.3 38.9 %all-gather.2.cloned.1.call-done = bf16[2048,1024]{1,0:T(8,128)(2,1)} async-done(((bf16[64,1024]{1,0:T(8,128)(2,1)}), bf16[2048,1024]{1,0:T(8,128)(2,1)}) %all-gather.2.cloned.1.call-update) | async-done | bytes 4194320 | tf_op jit(solution)/shard_map/all_gather | solution.py:71
  78.2 0.0 copy-done
  78.2 5.3 %fusion.34 = f32[768,2048]{1,0:T(8,128)S(1)} fusion(bf16[768,1024]{1,0:T(8,128)(2,1)S(1)} %bitcast.12, bf16[2048,1024]{1,0:T(8,128)(2,1)} %all-gather.2.cloned.1.call-done), kind=kOutput, calls=%fused_computation.48 | convolution fusion | flops 3221225472 | bytes 12058624 | tf_op jit(solution)/shard_map/dot_general | solution.py:69
  83.5 0.0 copy-start.6
  83.5 2.7 copy-done.6
  86.1 0.0 copy-start.1
  86.1 0.0 copy-start.2
  86.1 0.0 copy-start.5
  86.1 2.2 fusion.22
  88.4 0.1 sub.63
  88.5 0.8 reshape.24
  89.3 5.3 %all-to-all-start = ((f32[32,1,768]{2,1,0:T(1,128)}), f32[32,1,768]{2,1,0:T(1,128)S(1)}, u32[]{:S(2)}, u32[]{:S(2)}) async-start(f32[32,1,768]{2,1,0:T(1,128)} %reshape.24), calls=%async_computation | async-start | bytes 196608 | tf_op jit(solution)/shard_map/all_to_all | solution.py:25
  94.6 0.0 reduce-scatter.2.cloned.1.call-start
  94.7 0.0 copy-done.1
  94.7 0.0 copy-done.2
  94.7 0.0 copy-done.3
  94.7 7.3 %all-to-all-done = f32[32,1,768]{2,1,0:T(1,128)S(1)} async-done(((f32[32,1,768]{2,1,0:T(1,128)}), f32[32,1,768]{2,1,0:T(1,128)S(1)}, u32[]{:S(2)}, u32[]{:S(2)}) %all-to-all-start) | async-done | bytes 98336 | tf_op jit(solution)/shard_map/all_to_all | solution.py:25
  102.0 0.5 broadcast.84
  102.5 0.9 reduce.3
  103.4 0.1 reshape.25
  103.6 0.1 copy.32
  103.6 0.2 sub.65
  103.8 0.0 copy-done.5
  103.8 3.0 fusion.13
  106.8 0.0 copy-start.4
  106.8 0.1 mul.88
  106.9 10.4 %convolution_convert_fusion = bf16[2048,1024]{1,0:T(8,128)(2,1)} fusion(bf16[768,1024]{1,0:T(8,128)(2,1)S(1)} %bitcast.13, f32[768,2048]{1,0:T(8,128)} %copy-done.6, f32[2048]{0:T(1024)S(1)} %convert_element_type.34, f32[768]{0:T(1024)S(1)} %mul.88), kind=kOutput, calls=%fused_computation.19 | convolution fusion | flops 3256352768 | bytes 12069888 | tf_op jit(solution)/shard_map/dot_general | solution.py:95
  117.3 0.0 copy-done.4
  117.3 0.0 reduce-scatter.2.cloned.1.call-update
  117.3 101.5 %reduce-scatter.2.cloned.1.call-done = bf16[64,1024]{1,0:T(8,128)(2,1)} async-done(((bf16[2048,1024]{1,0:T(8,128)(2,1)}), bf16[64,1024]{1,0:T(8,128)(2,1)}) %reduce-scatter.2.cloned.1.call-update) | async-done | bytes 131088 | tf_op jit(solution)/shard_map/reduce_scatter | solution.py:94
  218.8 46.8 %all-reduce.1 = f32[64,1024]{1,0:T(8,128)S(1)} all-reduce(bf16[64,1024]{1,0:T(8,128)(2,1)} %reduce-scatter.2.cloned.1.call-done), channel_id=1, replica_groups=mesh['grp'=16,'cand'=32] {'grp'}, use_global_device_ids=true, to_apply=%region_2.0 | all-reduce | flops 65536 | bytes 393216 | tf_op jit(solution)/shard_map/psum | solution.py:102
  265.6 0.7 multiply_reduce_fusion
  266.2 0.7 broadcast_in_dim.5
  266.9 27.1 %all_to_all.11 = f32[32,1,1]{2,1,0:T(1,128)S(1)} all-to-all(f32[32,1,1]{2,1,0:T(1,128)S(1)} %broadcast_in_dim.5), channel_id=1, replica_groups=mesh['grp'=16,'cand'=32] {'cand'}, dimensions={0} | all-to-all | bytes 256 | tf_op jit(solution)/shard_map/all_to_all | solution.py:25
  294.0 0.6 reduce_sum.29
  295.4 0.7 broadcast_multiply_fusion
  (4 shorter events, 0.1 us)
Async XLA Ops:
  7.2 71.0 %copy-start = (bf16[24,32,1024]{2,1,0:T(8,128)(2,1)S(1)}, bf16[24,32,1024]{2,1,0:T(8,128)(2,1)}, u32[]{:S(2)}) copy-start(bf16[24,32,1024]{2,1,0:T(8,128)(2,1)} %param.6) | copy-start | bytes 4718596
  7.2 71.0 %all-gather.2.cloned.1.call-start = ((), (), s32[]{:S(2)}) async-start(), calls=%async_computation.3 | async-start | bytes 4325376 | tf_op jit(solution)/shard_map/all_gather | solution.py:71
  83.5 2.7 copy-start.6
  86.1 8.6 %copy-start.1 = (s32[24,32]{1,0:T(8,128)S(1)}, s32[24,32]{1,0:T(8,128)}, u32[]{:S(2)}) copy-start(s32[24,32]{1,0:T(8,128)} %param.10) | copy-start | bytes 9220
  86.1 8.6 %copy-start.2 = (s32[24,32]{1,0:T(8,128)S(1)}, s32[24,32]{1,0:T(8,128)}, u32[]{:S(2)}) copy-start(s32[24,32]{1,0:T(8,128)} %param.9) | copy-start | bytes 9220
  86.1 8.6 %copy-start.3 = (bf16[2048]{0:T(1024)(128)(2,1)S(1)}, bf16[2048]{0:T(1024)(128)(2,1)}, u32[]{:S(2)}) copy-start(bf16[2048]{0:T(1024)(128)(2,1)} %param.8) | copy-start | bytes 12292
  86.1 17.7 %copy-start.5 = (f32[24]{0:T(128)S(1)}, f32[24]{0:T(128)}, u32[]{:S(2)}) copy-start(f32[24]{0:T(128)} %param.11) | copy-start | bytes 292
  89.3 12.7 %all-to-all-start = ((f32[32,1,768]{2,1,0:T(1,128)}), f32[32,1,768]{2,1,0:T(1,128)S(1)}, u32[]{:S(2)}, u32[]{:S(2)}) async-start(f32[32,1,768]{2,1,0:T(1,128)} %reshape.24), calls=%async_computation | async-start | bytes 196608 | tf_op jit(solution)/shard_map/all_to_all | solution.py:25
  94.6 124.2 %reduce-scatter.2.cloned.1.call-start = ((), (), s32[]{:S(2)}) async-start(), calls=%async_computation.4 | async-start | bytes 4325376 | tf_op jit(solution)/shard_map/reduce_scatter | solution.py:94
  106.8 10.5 %copy-start.4 = (f32[24,32]{1,0:T(8,128)}, f32[24,32]{1,0:T(8,128)S(1)}, u32[]{:S(2)}) copy-start(f32[24,32]{1,0:T(8,128)S(1)} %fusion.13) | copy-start | bytes 9220
Sparse Core Ops, SparseCore 0:
  11.1 67.0 all-gather.1
  117.5 101.2 reduce-scatter.1
where the time goes:
time: 303 us
  waiting for transfers between devices  148 us (49%)
  blocking collectives  102 us (34%)
  matrix products  17.9 us (6%)
  between operations  14.9 us (5%)
  local copies, waits for them, and re-layouts  8.06 us (3%)
  other arithmetic  6.06 us (2%)
  starting transfers between devices  5.38 us (2%)
    reduce_scatter x1, waiting for transfers between devices, per_device(): lax.psum_scatter(lax.dot_general(grad_pre, cand_rows, (((0,), (0,)), ((),...  101 us
    psum x1, blocking collectives, per_device(): summed = lax.psum(owned, 'grp')  46.8 us
    all_gather x1, waiting for transfers between devices, per_device(): lax.all_gather(hidden_weight, 'cand', axis=0, tiled=True)  38.9 us
    all_gather x1, blocking collectives, turned_gather(): result = lax.all_gather(both, axis, axis=0, tiled=True)  28.5 us
    all_to_all x1, blocking collectives, copy_for_each(): return lax.all_to_all(copies, axis, split_axis=0, concat_axis=0, tiled=True)  27.1 us
    dot_general x1, matrix products, per_device(): lax.dot_general(grad_pre, cand_rows, (((0,), (0,)), ((), ())), preferred_...  10.4 us
    all_to_all x1, waiting for transfers between devices, copy_for_each(): return lax.all_to_all(copies, axis, split_axis=0, concat_axis=0, tiled=True)  7.27 us
    unnamed x21, local copies, waits for them, and re-layouts  6.27 us
  transfers between devices with their start and end apart: 3, of which 3 were waited for; matrix products, arithmetic and copies ran while one was open for 1% of the time, Pallas kernels for 0%

commit v1 on v0

v1 whole, which is shorter than its diff:
```python
import jax
import jax.numpy as jnp
from jax import lax
from jax.sharding import Mesh
from jax.sharding import PartitionSpec as P

EPS = 1e-06
GELU_A = 0.7978845608028654
GELU_B = 0.044715
CHIPS = ("y", "x")
CAND = ("y", "x", "c")


def spread(value, axis, size):
    copies = jnp.broadcast_to(value[None], (size, *value.shape))
    return lax.all_to_all(copies, axis, split_axis=0, concat_axis=0, tiled=True)


def per_device(embeddings, hidden_weight, score_weight, relevance, rank_pos, ideal_dcg):
    groups, local, width = embeddings.shape
    owned_rows = hidden_weight.shape[0]
    cores = lax.axis_size("c")
    chips = lax.axis_size("y") * lax.axis_size("x")
    planes = lax.axis_size("z")
    core = lax.axis_index("c")
    chip = lax.axis_index("y") * lax.axis_size("x") + lax.axis_index("x")
    own = embeddings.reshape(groups * local, width)

    other = lax.ppermute(own, "c", [(0, 1), (1, 0)])
    labels = spread(jnp.stack([relevance, rank_pos]), CAND, chips * cores)
    weight = spread(hidden_weight, CHIPS, chips).reshape(chips * owned_rows, width)

    labels = labels.reshape(chips, cores, 2, groups, local).transpose(2, 3, 0, 1, 4)
    own_labels = lax.dynamic_index_in_dim(labels, chip, 2, keepdims=False)
    labels = labels.reshape(2, groups, chips * cores * local)
    own_labels = own_labels.reshape(2, groups, cores * local)
    gain = lambda v: jnp.exp2(v.astype(jnp.float32)) - 1.0
    disc = lambda v: 1.0 / jnp.log2(2.0 + v.astype(jnp.float32))
    gain_diff = gain(labels[0])[:, None, :] - gain(own_labels[0])[:, :, None]
    disc_diff = jnp.abs(disc(labels[1])[:, None, :] - disc(own_labels[1])[:, :, None])
    pull = gain_diff * disc_diff / ideal_dcg[:, None, None]

    both = jnp.concatenate([own, other], axis=0)
    unit_weight = lax.dynamic_index_in_dim(
        score_weight.reshape(chips, cores, owned_rows), core, 1, keepdims=False
    ).reshape(chips * owned_rows).astype(jnp.float32)
    pre = lax.dot_general(
        weight, both, (((1,), (1,)), ((), ())), preferred_element_type=jnp.float32
    )
    tanh = jnp.tanh(GELU_A * (pre + GELU_B * pre * pre * pre))
    acts = (0.5 * pre * (1.0 + tanh)).astype(jnp.bfloat16).astype(jnp.float32)
    slope = 0.5 * (1.0 + tanh) + 0.5 * pre * (1.0 - tanh * tanh) * (
        GELU_A * (1.0 + 3.0 * GELU_B * pre * pre)
    )
    part = jnp.sum(acts * unit_weight[:, None], axis=0).reshape(2, groups, local)
    part = jnp.where(core == 0, part, part[::-1])
    pair = lax.psum(part, "c")
    scores = spread(pair, CHIPS, chips)
    scores = scores.transpose(2, 0, 1, 3).reshape(groups, chips * cores * local)
    own_scores = pair.transpose(1, 0, 2).reshape(groups, cores * local)
    margin = own_scores[:, :, None] - scores[:, None, :]
    pair_lam = jnp.sum(
        pull * jax.nn.sigmoid(jnp.where(gain_diff < 0.0, -margin, margin)), axis=-1
    )
    pair_lam = pair_lam.reshape(groups, cores, local).transpose(1, 0, 2)
    pair_lam = jnp.where(core == 0, pair_lam, pair_lam[::-1])
    lambdas = pair_lam[0]

    upstream = pair_lam.reshape(-1)[None, :] * unit_weight[:, None]
    grad_pre = (upstream * slope).astype(jnp.bfloat16)
    term = lax.dot_general(
        grad_pre, both, (((1,), (0,)), ((), ())), preferred_element_type=jnp.float32
    ).astype(jnp.bfloat16)
    terms = lax.all_to_all(
        term.reshape(chips, owned_rows, width), CHIPS, split_axis=0, concat_axis=0, tiled=True
    )
    owned = jnp.sum(terms.astype(jnp.float32), axis=0)
    pieces = lax.all_to_all(
        owned.reshape(planes, owned_rows // planes, width), "z", split_axis=0, concat_axis=0, tiled=True
    )
    piece = jnp.sum(pieces, axis=0)
    total = spread(piece, "z", planes).reshape(owned_rows, width)
    squares = jnp.sum(spread(jnp.sum(total * total), CAND, chips * cores))
    entries = owned_rows * width * chips * cores
    return total * lax.rsqrt(squares / entries + EPS), lambdas


def solution(mesh):
    fine = Mesh(mesh.devices.reshape(mesh.devices.shape[0], 4, 4, 2), ("z", "y", "x", "c"))
    return jax.shard_map(
        per_device,
        mesh=fine,
        in_specs=(
            P("z", CAND, None),
            P(CAND, None),
            P(),
            P("z", CAND),
            P("z", CAND),
            P("z"),
        ),
        out_specs=(P(CAND, None), P("z", CAND)),
        check_vma=False,
    )
```

time: 303 us -> 203 us (0.67)
  waiting for transfers between devices: 148 us -> 39.5 us
  starting transfers between devices: 5.38 us -> 19.9 us
  between operations: 14.9 us -> 1.6 us
  other arithmetic: 6.06 us -> 9.92 us
  local copies, waits for them, and re-layouts: 8.06 us -> 11.2 us
    reduce_scatter x1 -> x0, waiting for transfers between devices: 101 us -> none  [per_device(): lax.psum_scatter(lax.dot_general(grad_pre, cand_rows, (((0,), (0,)), ((),...]
    all_to_all x1 -> x4, blocking collectives: 27.1 us -> 97.5 us  [the longest x2 41.1 us: spread(): return lax.all_to_all(copies, axis, split_axis=0, concat_axis=0, tiled=True)]
    psum x1, blocking collectives: 46.8 us -> 4.39 us  [per_device(): pair = lax.psum(part, 'c')]
    all_gather x1 -> x0, waiting for transfers between devices: 38.9 us -> none  [per_device(): lax.all_gather(hidden_weight, 'cand', axis=0, tiled=True)]
    all_to_all x1 -> x3, waiting for transfers between devices: 7.27 us -> 39 us  [spread(): return lax.all_to_all(copies, axis, split_axis=0, concat_axis=0, tiled=True)]
    all_gather x1 -> x0, blocking collectives: 28.5 us -> none  [turned_gather(): result = lax.all_gather(both, axis, axis=0, tiled=True)]
    all_to_all x1 -> x3, starting transfers between devices: 5.3 us -> 17.8 us  [spread(): return lax.all_to_all(copies, axis, split_axis=0, concat_axis=0, tiled=True)]
    unnamed x21 -> x13, local copies, waits for them, and re-layouts: 6.27 us -> 2.07 us
  transfers between devices with their start and end apart: 3 -> 4, of which waited for: 3 -> 4; matrix products, arithmetic and copies ran while one was open for 1% -> 3% of each run, Pallas kernels for 0% -> 0%
where the time goes in v1:
time: 203 us; the launch traced here: 202 us
  blocking collectives  102 us (50%)
  waiting for transfers between devices  39.5 us (19%)
  starting transfers between devices  19.9 us (10%)
  matrix products  17.9 us (9%)
  local copies, waits for them, and re-layouts  11.2 us (6%)
  other arithmetic  9.92 us (5%)
    all_to_all x2, blocking collectives, spread(): return lax.all_to_all(copies, axis, split_axis=0, concat_axis=0, tiled=True)  41.1 us
    all_to_all x3, waiting for transfers between devices, spread(): return lax.all_to_all(copies, axis, split_axis=0, concat_axis=0, tiled=True)  39 us
    all_to_all x1, blocking collectives, per_device(): lax.all_to_all(term.reshape(chips, owned_rows, width), CHIPS, split_axis=...  30.2 us
    all_to_all x1, blocking collectives, per_device(): lax.all_to_all(owned.reshape(planes, owned_rows // planes, width), 'z', s...  26.2 us
    all_to_all x3, starting transfers between devices, spread(): return lax.all_to_all(copies, axis, split_axis=0, concat_axis=0, tiled=True)  17.8 us
    dot_general x1, matrix products, per_device(): lax.dot_general(weight, both, (((1,), (1,)), ((), ())), preferred_element...  9.28 us
    dot_general x1, matrix products, per_device(): lax.dot_general(grad_pre, both, (((1,), (0,)), ((), ())), preferred_eleme...  8.66 us
    psum x1, blocking collectives, per_device(): pair = lax.psum(part, 'c')  4.39 us
  transfers between devices with their start and end apart: 4, of which 4 were waited for; matrix products, arithmetic and copies ran while one was open for 3% of the time, Pallas kernels for 0%

profile of v1, /device:TPU:1, one launch (start us, length us, event | category | flops | bytes accessed | tf_op | source)
XLA Modules:
  0.0 202.0 jit_solution(17117614926168994607)
XLA Ops:
  0.6 0.7 pad_add_fusion
  1.4 0.3 reshape.142
  1.8 17.8 %all_to_all.36 = s32[32,1,1536]{2,1,0:T(1,128)S(1)} all-to-all(s32[32,1,1536]{2,1,0:T(1,128)S(1)} %reshape.142), channel_id=1, replica_groups=mesh['z'=16,'y'=4,'x'=4,'c'=2] {'y','x','c'}, dimensions={0} | all-to-all | bytes 393216 | tf_op jit(solution)/shard_map/all_to_all | solution.py:16
  19.6 2.5 %broadcast_in_dim.11 = bf16[16,64,1024]{2,1,0:T(8,128)(2,1)} broadcast(bf16[64,1024]{1,0:T(8,128)(2,1)} %param.7), dimensions={1,2} | broadcast | bytes 2228224 | tf_op jit(solution)/shard_map/broadcast_in_dim | solution.py:15
  22.1 3.7 %all-to-all-start.1 = ((bf16[16,64,1024]{2,1,0:T(8,128)(2,1)}), bf16[16,64,1024]{2,1,0:T(8,128)(2,1)S(1)}, u32[]{:S(2)}, u32[]{:S(2)}) async-start(bf16[16,64,1024]{2,1,0:T(8,128)(2,1)} %broadcast_in_dim.11), calls=%async_computation.1 | async-start | bytes 4194304 | tf_op jit(solution)/shard_map/all_to_all | solution.py:16
  25.8 2.1 %collective-permute-start = (bf16[768,1024]{1,0:T(8,128)(2,1)}, bf16[768,1024]{1,0:T(8,128)(2,1)}, u32[]{:S(2)}, u32[]{:S(2)}) collective-permute-start(bf16[768,1024]{1,0:T(8,128)(2,1)} %bitcast.56), channel_id=1, source_target_pairs={{0,1},{1,0},{2,3},{3,2},{4,5},{5,4},{6,7},{7,6},{8,9},{9,8},{10,11... | collective-permute-start | bytes 4718600 | tf_op jit(solution)/shard_map/ppermute | solution.py:29
  27.9 0.1 reshape.123
  28.1 0.5 broadcast.131
  28.6 1.1 reduce.7
  29.8 0.2 reshape.143
  30.0 0.9 fusion.27
  30.9 0.6 collective-permute-done
  31.5 27.8 %all-to-all-done.1 = bf16[16,64,1024]{2,1,0:T(8,128)(2,1)S(1)} async-done(((bf16[16,64,1024]{2,1,0:T(8,128)(2,1)}), bf16[16,64,1024]{2,1,0:T(8,128)(2,1)S(1)}, u32[]{:S(2)}, u32[]{:S(2)}) %all-to-all-start.1) | async-done | bytes 2097184 | tf_op jit(solution)/shard_map/all_to_all | solution.py:16
  59.3 9.3 %multiply_reduce_fusion = (f32[1536]{0:T(1024)S(1)}, f32[1536,1024]{0,1:T(8,128)}) fusion(f32[1024]{0:T(1024)S(1)} %reshape.132, bf16[1024,1024]{1,0:T(8,128)(2,1)S(1)} %bitcast.49, bf16[768,1024]{1,0:T(8,128)(2,1)} %collective-permute-done, bf16[768,1024]{1,0:T(8,128)(2,1)} %bitcast.57), kind=kOutput, calls=%fused_computation.20 | convolution fusion | flops 3246389760 | bytes 11544576 | tf_op jit(solution)/shard_map/dot_general | solution.py:47
  68.6 0.1 reshape.124
  68.7 4.4 %psum.7 = f32[2,24,32]{2,1,0:T(8,128)S(1)} all-reduce(f32[2,24,32]{2,1,0:T(8,128)S(1)} %reverse_select_fusion.1), channel_id=1, replica_groups=mesh['z'=16,'y'=4,'x'=4,'c'=2] {'c'}, use_global_device_ids=true, to_apply=%region_1.2 | all-reduce | flops 1536 | bytes 12288 | tf_op jit(solution)/shard_map/psum | solution.py:57
  73.1 0.1 broadcast_bitcast_fusion
  73.2 1.1 reshape.140
  74.3 3.7 %all-to-all-start.2 = ((f32[16,1,1536]{2,1,0:T(1,128)}), f32[16,1,1536]{2,1,0:T(1,128)S(1)}, u32[]{:S(2)}, u32[]{:S(2)}) async-start(f32[16,1,1536]{2,1,0:T(1,128)} %reshape.140), calls=%async_computation.2 | async-start | bytes 196608 | tf_op jit(solution)/shard_map/all_to_all | solution.py:16
  78.0 0.1 reshape.131
  78.1 0.1 sub.60
  78.2 0.2 copy.52
  78.4 0.5 reshape.129
  78.9 0.2 copy.50
  79.1 0.5 sub.57
  79.7 0.1 sub.66
  79.7 4.7 %all-to-all-done.2 = f32[16,1,1536]{2,1,0:T(1,128)S(1)} async-done(((f32[16,1,1536]{2,1,0:T(1,128)}), f32[16,1,1536]{2,1,0:T(1,128)S(1)}, u32[]{:S(2)}, u32[]{:S(2)}) %all-to-all-start.2) | async-done | bytes 98336 | tf_op jit(solution)/shard_map/all_to_all | solution.py:16
  84.4 0.5 broadcast.130
  85.0 0.9 reduce.6
  85.8 0.3 reshape.141
  86.2 0.2 copy.56
  86.4 0.5 sub.68
  86.9 4.4 %fusion.14 = f32[24,64]{1,0:T(8,128)S(1)} fusion(f32[24,1024]{1,0:T(8,128)S(1)} %sub.68, f32[24,64]{1,0:T(8,128)S(1)} %sub.66, f32[24]{0:T(128)S(1)} %copy-done.3, f32[24,64]{1,0:T(8,128)S(1)} %reshape.131, f32[24,1024]{1,0:T(8,128)S(1)} %reshape.129, f32[24,64]{1,0:T(8,128)S(1)} %sub.60, f32[24,1024]{1,0:T(8,128)S(1)} %sub.57), kind=kLoop, calls=%fused_computation.22 | loop fusion | flops 22018560 | bytes 319584 | tf_op jit(solution)/shard_map/reduce_sum | solution.py:62
  91.3 0.1 reshape.125
  91.4 0.1 mul.104
  91.5 8.7 %fusion.18 = bf16[1024,1024]{1,0:T(8,128)(2,1)S(1)} fusion(bf16[768,1024]{1,0:T(8,128)(2,1)} %collective-permute-done, bf16[768,1024]{1,0:T(8,128)(2,1)S(1)} %bitcast.58, f32[1536,1024]{0,1:T(8,128)} %get-tuple-element.7, f32[1536]{0:T(1024)S(1)} %mul.104, f32[1024]{0:T(1024)S(1)} %reshape.132), kind=kOutput, calls=%fused_computation.27 | convolution fusion | flops 3260022784 | bytes 11544576 | tf_op jit(solution)/shard_map/dot_general | solution.py:71
  100.2 30.2 %all_to_all.37 = bf16[16,64,1024]{2,1,0:T(8,128)(2,1)S(1)} all-to-all(bf16[16,64,1024]{2,1,0:T(8,128)(2,1)S(1)} %bitcast.50), channel_id=1, replica_groups=mesh['z'=16,'y'=4,'x'=4,'c'=2] {'y','x'}, dimensions={0} | all-to-all | bytes 4194304 | tf_op jit(solution)/shard_map/all_to_all | solution.py:74
  130.4 0.4 convert_reduce_fusion
  130.8 0.1 reshape.127
  130.9 26.2 %all_to_all.38 = f32[16,4,1024]{2,1,0:T(4,128)S(1)} all-to-all(f32[16,4,1024]{2,1,0:T(4,128)S(1)} %reshape.127), channel_id=1, replica_groups=mesh['z'=16,'y'=4,'x'=4,'c'=2] {'z'}, dimensions={0} | all-to-all | bytes 524288 | tf_op jit(solution)/shard_map/all_to_all | solution.py:78
  157.2 23.2 %all_to_all.39 = f32[16,4,1024]{2,1,0:T(4,128)S(1)} all-to-all(f32[16,4,1024]{2,1,0:T(4,128)S(1)} %broadcast_in_dim.13), channel_id=1, replica_groups=mesh['z'=16,'y'=4,'x'=4,'c'=2] {'z'}, dimensions={0} | all-to-all | bytes 524288 | tf_op jit(solution)/shard_map/all_to_all | solution.py:16
  180.5 0.7 multiply_reduce_fusion.1
  181.2 1.3 broadcast_in_dim.14
  182.5 10.4 %all-to-all-start.6 = ((f32[32,1,1]{2,1,0:T(1,128)}), f32[32,1,1]{2,1,0:T(1,128)S(1)}, u32[]{:S(2)}, u32[]{:S(2)}) async-start(f32[32,1,1]{2,1,0:T(1,128)} %broadcast_in_dim.14), calls=%async_computation.6 | async-start | bytes 32768 | tf_op jit(solution)/shard_map/all_to_all | solution.py:16
  192.9 0.6 slice_bitcast_fusion
  193.5 6.4 %all-to-all-done.6 = f32[32,1,1]{2,1,0:T(1,128)S(1)} async-done(((f32[32,1,1]{2,1,0:T(1,128)}), f32[32,1,1]{2,1,0:T(1,128)S(1)}, u32[]{:S(2)}, u32[]{:S(2)}) %all-to-all-start.6) | async-done | bytes 160 | tf_op jit(solution)/shard_map/all_to_all | solution.py:16
  199.9 0.6 reduce_sum.59
  201.2 0.8 mul.119
  (24 shorter events, 0.4 us)
Async XLA Ops:
  0.6 27.3 %copy-start.1 = (bf16[2048]{0:T(1024)(128)(2,1)S(1)}, bf16[2048]{0:T(1024)(128)(2,1)}, u32[]{:S(2)}) copy-start(bf16[2048]{0:T(1024)(128)(2,1)} %param.8) | copy-start | bytes 12292
  22.1 37.2 %all-to-all-start.1 = ((bf16[16,64,1024]{2,1,0:T(8,128)(2,1)}), bf16[16,64,1024]{2,1,0:T(8,128)(2,1)S(1)}, u32[]{:S(2)}, u32[]{:S(2)}) async-start(bf16[16,64,1024]{2,1,0:T(8,128)(2,1)} %broadcast_in_dim.11), calls=%async_computation.1 | async-start | bytes 4194304 | tf_op jit(solution)/shard_map/all_to_all | solution.py:16
  25.8 5.6 %collective-permute-start = (bf16[768,1024]{1,0:T(8,128)(2,1)}, bf16[768,1024]{1,0:T(8,128)(2,1)}, u32[]{:S(2)}, u32[]{:S(2)}) collective-permute-start(bf16[768,1024]{1,0:T(8,128)(2,1)} %bitcast.56), channel_id=1, source_target_pairs={{0,1},{1,0},{2,3},{3,2},{4,5},{5,4},{6,7},{7,6},{8,9},{9,8},{10,11... | collective-permute-start | bytes 4718600 | tf_op jit(solution)/shard_map/ppermute | solution.py:29
  59.3 18.9 %copy-start = (f32[1,24,16,2,32]{4,1,0,3,2:T(8,128)S(1)}, f32[1,24,16,2,32]{4,1,0,3,2:T(8,128)}, u32[]{:S(2)}) copy-start(f32[1,24,16,2,32]{4,1,0,3,2:T(8,128)} %get-tuple-element.3) | copy-start | bytes 294916
  68.6 18.3 %copy-start.3 = (f32[24]{0:T(128)S(1)}, f32[24]{0:T(128)}, u32[]{:S(2)}) copy-start(f32[24]{0:T(128)} %param.11) | copy-start | bytes 292
  68.6 22.9 %copy-start.2 = (bf16[24,32,1024]{2,1,0:T(8,128)(2,1)S(1)}, bf16[24,32,1024]{2,1,0:T(8,128)(2,1)}, u32[]{:S(2)}) copy-start(bf16[24,32,1024]{2,1,0:T(8,128)(2,1)} %param.6) | copy-start | bytes 4718596
  74.3 10.1 %all-to-all-start.2 = ((f32[16,1,1536]{2,1,0:T(1,128)}), f32[16,1,1536]{2,1,0:T(1,128)S(1)}, u32[]{:S(2)}, u32[]{:S(2)}) async-start(f32[16,1,1536]{2,1,0:T(1,128)} %reshape.140), calls=%async_computation.2 | async-start | bytes 196608 | tf_op jit(solution)/shard_map/all_to_all | solution.py:16
  182.5 17.4 %all-to-all-start.6 = ((f32[32,1,1]{2,1,0:T(1,128)}), f32[32,1,1]{2,1,0:T(1,128)S(1)}, u32[]{:S(2)}, u32[]{:S(2)}) async-start(f32[32,1,1]{2,1,0:T(1,128)} %broadcast_in_dim.14), calls=%async_computation.6 | async-start | bytes 32768 | tf_op jit(solution)/shard_map/all_to_all | solution.py:16

commit v2 on v1

--- a/solution.py
+++ b/solution.py
@@ -3,6 +3,7 @@
 from jax import lax
 from jax.sharding import Mesh
 from jax.sharding import PartitionSpec as P
+
 
 EPS = 1e-06
 GELU_A = 0.7978845608028654
@@ -23,17 +24,14 @@
     chips = lax.axis_size("y") * lax.axis_size("x")
     planes = lax.axis_size("z")
     core = lax.axis_index("c")
-    chip = lax.axis_index("y") * lax.axis_size("x") + lax.axis_index("x")
     own = embeddings.reshape(groups * local, width)
 
+    weight = spread(hidden_weight, CHIPS, chips).reshape(chips * owned_rows, width)
     other = lax.ppermute(own, "c", [(0, 1), (1, 0)])
-    labels = spread(jnp.stack([relevance, rank_pos]), CAND, chips * cores)
-    weight = spread(hidden_weight, CHIPS, chips).reshape(chips * owned_rows, width)
-
-    labels = labels.reshape(chips, cores, 2, groups, local).transpose(2, 3, 0, 1, 4)
-    own_labels = lax.dynamic_index_in_dim(labels, chip, 2, keepdims=False)
-    labels = labels.reshape(2, groups, chips * cores * local)
-    own_labels = own_labels.reshape(2, groups, cores * local)
+    own_labels = lax.all_gather(jnp.stack([relevance, rank_pos]), "c")
+    labels = lax.all_gather(lax.all_gather(own_labels, "x"), "y")
+    own_labels = own_labels.transpose(1, 2, 0, 3).reshape(2, groups, cores * local)
+    labels = labels.transpose(3, 4, 0, 1, 2, 5).reshape(2, groups, chips * cores * local)
     gain = lambda v: jnp.exp2(v.astype(jnp.float32)) - 1.0
     disc = lambda v: 1.0 / jnp.log2(2.0 + v.astype(jnp.float32))
     gain_diff = gain(labels[0])[:, None, :] - gain(own_labels[0])[:, :, None]
@@ -76,10 +74,10 @@
     )
     owned = jnp.sum(terms.astype(jnp.float32), axis=0)
     pieces = lax.all_to_all(
-        owned.reshape(planes, owned_rows // planes, width), "z", split_axis=0, concat_axis=0, tiled=True
+        owned.astype(jnp.bfloat16).reshape(planes, owned_rows // planes, width), "z", split_axis=0, concat_axis=0, tiled=True
     )
-    piece = jnp.sum(pieces, axis=0)
-    total = spread(piece, "z", planes).reshape(owned_rows, width)
+    piece = jnp.sum(pieces.astype(jnp.float32), axis=0).astype(jnp.bfloat16)
+    total = spread(piece, "z", planes).reshape(owned_rows, width).astype(jnp.float32)
     squares = jnp.sum(spread(jnp.sum(total * total), CAND, chips * cores))
     entries = owned_rows * width * chips * cores
     return total * lax.rsqrt(squares / entries + EPS), lambdas

time: 203 us -> 197 us (0.970)
  waiting for transfers between devices: 39.5 us -> 11.7 us
  blocking collectives: 102 us -> 122 us
  starting transfers between devices: 19.9 us -> 24.8 us
  other arithmetic: 9.92 us -> 7.83 us
    all_gather x0 -> x3, blocking collectives: none -> 38.9 us  [the longest x2 35.8 us: per_device(): labels = lax.all_gather(lax.all_gather(own_labels, 'x'), 'y')]
    all_to_all x3, waiting for transfers between devices: 39 us -> 11.7 us  [spread(): return lax.all_to_all(copies, axis, split_axis=0, concat_axis=0, tiled=True)]
    all_to_all x2 -> x1, blocking collectives: 41.1 us -> 15.8 us  [spread(): return lax.all_to_all(copies, axis, split_axis=0, concat_axis=0, tiled=True)]
    psum x1, blocking collectives: 4.39 us -> 7.8 us  [per_device(): pair = lax.psum(part, 'c')]
    ppermute x1, starting transfers between devices: 2.07 us -> 4.89 us  [per_device(): other = lax.ppermute(own, 'c', [(0, 1), (1, 0)])]
    all_to_all x1, blocking collectives: 26.2 us -> 29 us  [per_device(): lax.all_to_all(owned.astype(jnp.bfloat16).reshape(planes, owned_rows // p...]
    all_to_all x3, starting transfers between devices: 17.8 us -> 19.9 us  [spread(): return lax.all_to_all(copies, axis, split_axis=0, concat_axis=0, tiled=True)]
  transfers between devices with their start and end apart: 4 -> 4, of which waited for: 4 -> 2; matrix products, arithmetic and copies ran while one was open for 3% -> 2% of each run, Pallas kernels for 0% -> 0%
where the time goes in v2:
time: 197 us; the launch traced here: 196 us
  blocking collectives  122 us (62%)
  starting transfers between devices  24.8 us (13%)
  matrix products  18.4 us (9%)
  waiting for transfers between devices  11.7 us (6%)
  local copies, waits for them, and re-layouts  10.1 us (5%)
  other arithmetic  7.83 us (4%)
    all_gather x2, blocking collectives, per_device(): labels = lax.all_gather(lax.all_gather(own_labels, 'x'), 'y')  35.8 us
    all_to_all x1, blocking collectives, per_device(): lax.all_to_all(term.reshape(chips, owned_rows, width), CHIPS, split_axis=...  30.2 us
    all_to_all x1, blocking collectives, per_device(): lax.all_to_all(owned.astype(jnp.bfloat16).reshape(planes, owned_rows // p...  29 us
    all_to_all x3, starting transfers between devices, spread(): return lax.all_to_all(copies, axis, split_axis=0, concat_axis=0, tiled=True)  19.9 us
    all_to_all x1, blocking collectives, spread(): return lax.all_to_all(copies, axis, split_axis=0, concat_axis=0, tiled=True)  15.8 us
    all_to_all x3, waiting for transfers between devices, spread(): return lax.all_to_all(copies, axis, split_axis=0, concat_axis=0, tiled=True)  11.7 us
    dot_general x1, matrix products, per_device(): lax.dot_general(weight, both, (((1,), (1,)), ((), ())), preferred_element...  9.28 us
    dot_general x1, matrix products, per_device(): lax.dot_general(grad_pre, both, (((1,), (0,)), ((), ())), preferred_eleme...  9.16 us
  transfers between devices with their start and end apart: 4, of which 2 were waited for; matrix products, arithmetic and copies ran while one was open for 2% of the time, Pallas kernels for 0%

profile of v2, /device:TPU:1, one launch (start us, length us, event | category | flops | bytes accessed | tf_op | source)
XLA Modules:
  0.0 196.3 jit_solution(7336687265999819340)
XLA Ops:
  0.7 2.5 %broadcast_in_dim.8 = bf16[16,64,1024]{2,1,0:T(8,128)(2,1)} broadcast(bf16[64,1024]{1,0:T(8,128)(2,1)} %param.7), dimensions={1,2} | broadcast | bytes 2228224 | tf_op jit(solution)/shard_map/broadcast_in_dim | solution.py:16
  3.2 7.6 %all-to-all-start = ((bf16[16,64,1024]{2,1,0:T(8,128)(2,1)}), bf16[16,64,1024]{2,1,0:T(8,128)(2,1)S(1)}, u32[]{:S(2)}, u32[]{:S(2)}) async-start(bf16[16,64,1024]{2,1,0:T(8,128)(2,1)} %broadcast_in_dim.8), calls=%async_computation | async-start | bytes 4194304 | tf_op jit(solution)/shard_map/all_to_all | solution.py:17
  10.8 4.9 %collective-permute-start = (bf16[768,1024]{1,0:T(8,128)(2,1)}, bf16[768,1024]{1,0:T(8,128)(2,1)}, u32[]{:S(2)}, u32[]{:S(2)}) collective-permute-start(bf16[768,1024]{1,0:T(8,128)(2,1)} %bitcast.58), channel_id=1, source_target_pairs={{0,1},{1,0},{2,3},{3,2},{4,5},{5,4},{6,7},{7,6},{8,9},{9,8},{10,11... | collective-permute-start | bytes 4718600 | tf_op jit(solution)/shard_map/ppermute | solution.py:30
  15.7 0.0 copy-done.2
  15.7 0.1 reshape.118
  15.8 0.1 reshape.127
  15.9 3.1 %all-gather = s32[4,24,32]{2,1,0:T(8,128)S(1)} all-gather(s32[2,24,32]{2,1,0:T(8,128)S(1)} %pad_add_fusion), channel_id=2, replica_groups=mesh['z'=16,'y'=4,'x'=4,'c'=2] {'c'}, dimensions={0}, use_global_device_ids=true | all-gather | bytes 18432 | tf_op jit(solution)/shard_map/all_gather | solution.py:31
  19.0 23.8 %all-gather.1 = s32[8,2,24,32]{3,2,1,0:T(8,128)S(1)} all-gather(s32[2,2,24,32]{3,2,1,0:T(8,128)S(1)} %bitcast.52), channel_id=3, replica_groups=mesh['z'=16,'y'=4,'x'=4,'c'=2] {'x'}, dimensions={0}, use_global_device_ids=true | all-gather | bytes 61440 | tf_op jit(solution)/shard_map/all_gather | solution.py:32
  42.9 11.9 %all-gather.2 = s32[16,2,2,24,32]{4,3,2,1,0:T(8,128)S(1)} all-gather(s32[4,2,2,24,32]{4,3,2,1,0:T(8,128)S(1)} %bitcast.51), channel_id=4, replica_groups=mesh['z'=16,'y'=4,'x'=4,'c'=2] {'y'}, dimensions={0}, use_global_device_ids=true | all-gather | bytes 245760 | tf_op jit(solution)/shard_map/all_gather | solution.py:32
  54.8 0.4 copy.64
  55.2 0.6 fusion.27
  55.9 0.0 collective-permute-done
  55.9 0.0 all-to-all-done
  55.9 0.0 copy-start.3
  55.9 9.3 %multiply_reduce_fusion = (f32[1536]{0:T(1024)S(1)}, f32[1536,1024]{0,1:T(8,128)}) fusion(f32[1024]{0:T(1024)S(1)} %reshape.127, bf16[1024,1024]{1,0:T(8,128)(2,1)S(1)} %bitcast.47, bf16[768,1024]{1,0:T(8,128)(2,1)} %collective-permute-done, bf16[768,1024]{1,0:T(8,128)(2,1)} %bitcast.59), kind=kOutput, calls=%fused_computation.20 | convolution fusion | flops 3246389760 | bytes 11544576 | tf_op jit(solution)/shard_map/dot_general | solution.py:45
  65.2 0.1 reshape.119
  65.3 7.8 %psum.7 = f32[2,24,32]{2,1,0:T(8,128)S(1)} all-reduce(f32[2,24,32]{2,1,0:T(8,128)S(1)} %reverse_select_fusion.1), channel_id=1, replica_groups=mesh['z'=16,'y'=4,'x'=4,'c'=2] {'c'}, use_global_device_ids=true, to_apply=%region_1.2 | all-reduce | flops 1536 | bytes 12288 | tf_op jit(solution)/shard_map/psum | solution.py:55
  73.1 0.1 broadcast_bitcast_fusion
  73.2 1.0 reshape.138
  74.3 3.9 %all-to-all-start.1 = ((f32[16,1,1536]{2,1,0:T(1,128)}), f32[16,1,1536]{2,1,0:T(1,128)S(1)}, u32[]{:S(2)}, u32[]{:S(2)}) async-start(f32[16,1,1536]{2,1,0:T(1,128)} %reshape.138), calls=%async_computation.1 | async-start | bytes 196608 | tf_op jit(solution)/shard_map/all_to_all | solution.py:17
  78.2 0.5 reshape.124
  78.7 0.5 sub.57
  79.3 0.1 reshape.126
  79.4 0.1 sub.60
  79.5 0.1 sub.66
  79.5 5.3 %all-to-all-done.1 = f32[16,1,1536]{2,1,0:T(1,128)S(1)} async-done(((f32[16,1,1536]{2,1,0:T(1,128)}), f32[16,1,1536]{2,1,0:T(1,128)S(1)}, u32[]{:S(2)}, u32[]{:S(2)}) %all-to-all-start.1) | async-done | bytes 98336 | tf_op jit(solution)/shard_map/all_to_all | solution.py:17
  84.8 0.5 broadcast.129
  85.4 0.9 reduce.8
  86.2 0.3 reshape.139
  86.6 0.2 copy.56
  86.8 0.5 sub.68
  87.3 4.4 %fusion.14 = f32[24,64]{1,0:T(8,128)S(1)} fusion(f32[24,1024]{1,0:T(8,128)S(1)} %sub.68, f32[24,64]{1,0:T(8,128)S(1)} %sub.66, f32[24]{0:T(128)S(1)} %copy-done.3, f32[24,64]{1,0:T(8,128)S(1)} %reshape.126, f32[24,1024]{1,0:T(8,128)S(1)} %reshape.124, f32[24,64]{1,0:T(8,128)S(1)} %sub.60, f32[24,1024]{1,0:T(8,128)S(1)} %sub.57), kind=kLoop, calls=%fused_computation.22 | loop fusion | flops 22018560 | bytes 319584 | tf_op jit(solution)/shard_map/reduce_sum | solution.py:60
  91.7 0.1 reshape.120
  91.8 0.1 mul.100
  91.9 9.2 %fusion.18 = bf16[1024,1024]{1,0:T(8,128)(2,1)S(1)} fusion(bf16[768,1024]{1,0:T(8,128)(2,1)} %collective-permute-done, bf16[768,1024]{1,0:T(8,128)(2,1)} %bitcast.60, f32[1536,1024]{0,1:T(8,128)} %get-tuple-element.7, f32[1536]{0:T(1024)S(1)} %mul.100, f32[1024]{0:T(1024)S(1)} %reshape.127), kind=kOutput, calls=%fused_computation.26 | convolution fusion | flops 3260022784 | bytes 11544576 | tf_op jit(solution)/shard_map/dot_general | solution.py:69
  101.1 30.2 %all_to_all.31 = bf16[16,64,1024]{2,1,0:T(8,128)(2,1)S(1)} all-to-all(bf16[16,64,1024]{2,1,0:T(8,128)(2,1)S(1)} %bitcast.48), channel_id=1, replica_groups=mesh['z'=16,'y'=4,'x'=4,'c'=2] {'y','x'}, dimensions={0} | all-to-all | bytes 4194304 | tf_op jit(solution)/shard_map/all_to_all | solution.py:72
  131.3 0.4 reduce_sum.62
  131.7 0.1 reshape.122
  131.8 29.0 %all_to_all.32 = bf16[16,4,1024]{2,1,0:T(4,128)(2,1)S(1)} all-to-all(bf16[16,4,1024]{2,1,0:T(4,128)(2,1)S(1)} %reshape.122), channel_id=1, replica_groups=mesh['z'=16,'y'=4,'x'=4,'c'=2] {'z'}, dimensions={0} | all-to-all | bytes 262144 | tf_op jit(solution)/shard_map/all_to_all | solution.py:76
  160.8 0.1 reduce_sum.63
  160.9 15.8 %all_to_all.33 = bf16[16,4,1024]{2,1,0:T(4,128)(2,1)S(1)} all-to-all(bf16[16,4,1024]{2,1,0:T(4,128)(2,1)S(1)} %broadcast_in_dim.10), channel_id=1, replica_groups=mesh['z'=16,'y'=4,'x'=4,'c'=2] {'z'}, dimensions={0} | all-to-all | bytes 262144 | tf_op jit(solution)/shard_map/all_to_all | solution.py:17
  176.7 0.7 fusion.28
  177.5 1.3 broadcast_in_dim.11
  178.7 8.4 %all-to-all-start.5 = ((f32[32,1,1]{2,1,0:T(1,128)}), f32[32,1,1]{2,1,0:T(1,128)S(1)}, u32[]{:S(2)}, u32[]{:S(2)}) async-start(f32[32,1,1]{2,1,0:T(1,128)} %broadcast_in_dim.11), calls=%async_computation.5 | async-start | bytes 32768 | tf_op jit(solution)/shard_map/all_to_all | solution.py:17
  187.2 0.6 slice_bitcast_fusion
  187.8 6.4 %all-to-all-done.5 = f32[32,1,1]{2,1,0:T(1,128)S(1)} async-done(((f32[32,1,1]{2,1,0:T(1,128)}), f32[32,1,1]{2,1,0:T(1,128)S(1)}, u32[]{:S(2)}, u32[]{:S(2)}) %all-to-all-start.5) | async-done | bytes 160 | tf_op jit(solution)/shard_map/all_to_all | solution.py:17
  194.2 0.6 reduce_sum.65
  195.5 0.8 mul.115
  (19 shorter events, 0.2 us)
Async XLA Ops:
  0.6 15.1 %copy-start.2 = (bf16[2048]{0:T(1024)(128)(2,1)S(1)}, bf16[2048]{0:T(1024)(128)(2,1)}, u32[]{:S(2)}) copy-start(bf16[2048]{0:T(1024)(128)(2,1)} %param.8) | copy-start | bytes 12292
  0.6 15.2 %copy-start.1 = (s32[24,32]{1,0:T(8,128)S(1)}, s32[24,32]{1,0:T(8,128)}, u32[]{:S(2)}) copy-start(s32[24,32]{1,0:T(8,128)} %param.9) | copy-start | bytes 9220
  0.7 15.2 %copy-start = (s32[24,32]{1,0:T(8,128)S(1)}, s32[24,32]{1,0:T(8,128)}, u32[]{:S(2)}) copy-start(s32[24,32]{1,0:T(8,128)} %param.10) | copy-start | bytes 9220
  3.2 52.7 %all-to-all-start = ((bf16[16,64,1024]{2,1,0:T(8,128)(2,1)}), bf16[16,64,1024]{2,1,0:T(8,128)(2,1)S(1)}, u32[]{:S(2)}, u32[]{:S(2)}) async-start(bf16[16,64,1024]{2,1,0:T(8,128)(2,1)} %broadcast_in_dim.8), calls=%async_computation | async-start | bytes 4194304 | tf_op jit(solution)/shard_map/all_to_all | solution.py:17
  10.8 45.1 %collective-permute-start = (bf16[768,1024]{1,0:T(8,128)(2,1)}, bf16[768,1024]{1,0:T(8,128)(2,1)}, u32[]{:S(2)}, u32[]{:S(2)}) collective-permute-start(bf16[768,1024]{1,0:T(8,128)(2,1)} %bitcast.58), channel_id=1, source_target_pairs={{0,1},{1,0},{2,3},{3,2},{4,5},{5,4},{6,7},{7,6},{8,9},{9,8},{10,11... | collective-permute-start | bytes 4718600 | tf_op jit(solution)/shard_map/ppermute | solution.py:30
  55.9 31.4 %copy-start.3 = (f32[24]{0:T(128)S(1)}, f32[24]{0:T(128)}, u32[]{:S(2)}) copy-start(f32[24]{0:T(128)} %param.11) | copy-start | bytes 292
  74.3 10.6 %all-to-all-start.1 = ((f32[16,1,1536]{2,1,0:T(1,128)}), f32[16,1,1536]{2,1,0:T(1,128)S(1)}, u32[]{:S(2)}, u32[]{:S(2)}) async-start(f32[16,1,1536]{2,1,0:T(1,128)} %reshape.138), calls=%async_computation.1 | async-start | bytes 196608 | tf_op jit(solution)/shard_map/all_to_all | solution.py:17
  178.7 15.5 %all-to-all-start.5 = ((f32[32,1,1]{2,1,0:T(1,128)}), f32[32,1,1]{2,1,0:T(1,128)S(1)}, u32[]{:S(2)}, u32[]{:S(2)}) async-start(f32[32,1,1]{2,1,0:T(1,128)} %broadcast_in_dim.11), calls=%async_computation.5 | async-start | bytes 32768 | tf_op jit(solution)/shard_map/all_to_all | solution.py:17

commit v3 on v2

v3 whole, which is shorter than its diff:
```python
import jax
import jax.numpy as jnp
from jax import lax
from jax.experimental import pallas as pl
from jax.experimental.pallas import tpu as pltpu
from jax.sharding import Mesh
from jax.sharding import PartitionSpec as P

EPS = 1e-06
GELU_A = 0.7978845608028654
GELU_B = 0.044715
CHIPS = ("y", "x")
CAND = ("y", "x", "c")
MIB = 1 << 20
f32 = jnp.float32
bf16 = jnp.bfloat16


def spread(value, axis, size):
    copies = jnp.broadcast_to(value[None], (size, *value.shape))
    return lax.all_to_all(copies, axis, split_axis=0, concat_axis=0, tiled=True)


def score_kernel(weight_ref, own_ref, other_ref, unit_ref, pre_ref, part_ref):
    @pl.when(pl.program_id(0) == 0)
    def _():
        part_ref[...] = jnp.zeros_like(part_ref)

    weight = weight_ref[...]
    unit = unit_ref[...]
    cut = 256
    for half, rows_ref in enumerate((own_ref, other_ref)):
        count = rows_ref.shape[0]
        for first in range(0, count, cut):
            pre = lax.dot_general(
                weight,
                rows_ref[first : first + cut, :],
                (((1,), (1,)), ((), ())),
                preferred_element_type=f32,
            )
            cols = slice(half * count + first, half * count + first + cut)
            pre_ref[:, cols] = pre
            tanh = jnp.tanh(pre * (GELU_A + (GELU_A * GELU_B) * (pre * pre)))
            part = 0.5 * pre
            acts = (part + part * tanh).astype(bf16).astype(f32)
            part_ref[:, cols] += jnp.sum(acts * unit, axis=0, keepdims=True)


def score(weight, own, other, unit):
    units, width = weight.shape
    count = own.shape[0]
    block = units // 2
    return pl.pallas_call(
        score_kernel,
        grid=(units // block,),
        in_specs=[
            pl.BlockSpec((block, width), lambda i: (i, 0)),
            pl.BlockSpec((count, width), lambda i: (0, 0)),
            pl.BlockSpec((count, width), lambda i: (0, 0)),
            pl.BlockSpec((block, 1), lambda i: (i, 0)),
        ],
        out_specs=[
            pl.BlockSpec((block, 2 * count), lambda i: (i, 0)),
            pl.BlockSpec((1, 2 * count), lambda i: (0, 0)),
        ],
        out_shape=[
            pltpu.HBM((units, 2 * count), f32),
            jax.ShapeDtypeStruct((1, 2 * count), f32),
        ],
        compiler_params=pltpu.CompilerParams(vmem_limit_bytes=32 * MIB),
        cost_estimate=pl.CostEstimate(
            flops=4 * units * width * count,
            bytes_accessed=12 * MIB,
            transcendentals=2 * units * count,
        ),
        name="score",
    )(weight, own, other, unit)


def slope_kernel(pre_ref, unit_ref, slope_ref):
    pre = pre_ref[...]
    square = pre * pre
    tanh = jnp.tanh(pre * (GELU_A + (GELU_A * GELU_B) * square))
    slope_ref[...] = (0.5 * unit_ref[...]) * (
        (1.0 + tanh)
        + pre * (1.0 - tanh * tanh) * (GELU_A + (3.0 * GELU_A * GELU_B) * square)
    )


def slopes(pre, unit):
    units, count = pre.shape
    block = 128
    return pl.pallas_call(
        slope_kernel,
        grid=(units // block,),
        in_specs=[
            pl.BlockSpec((block, count), lambda i: (i, 0)),
            pl.BlockSpec((block, 1), lambda i: (i, 0)),
        ],
        out_specs=pl.BlockSpec((block, count), lambda i: (i, 0)),
        out_shape=pltpu.HBM((units, count), f32),
        compiler_params=pltpu.CompilerParams(vmem_limit_bytes=16 * MIB),
        cost_estimate=pl.CostEstimate(
            flops=2000 * units * count,
            bytes_accessed=12 * MIB,
            transcendentals=units * count,
        ),
        name="slopes",
    )(pre, unit)


def term_kernel(slope_ref, lam_ref, own_ref, other_ref, out_ref):
    count = own_ref.shape[0]
    grad_pre = (slope_ref[...] * lam_ref[...]).astype(bf16)
    out_ref[...] = (
        jnp.dot(grad_pre[:, :count], own_ref[...], preferred_element_type=f32)
        + jnp.dot(grad_pre[:, count:], other_ref[...], preferred_element_type=f32)
    ).astype(bf16)


def gradient_term(slope, lam, own, other):
    units, both = slope.shape
    count, width = own.shape
    block = units // 2
    return pl.pallas_call(
        term_kernel,
        grid=(units // block,),
        in_specs=[
            pl.BlockSpec((block, both), lambda i: (i, 0)),
            pl.BlockSpec((1, both), lambda i: (0, 0)),
            pl.BlockSpec((count, width), lambda i: (0, 0)),
            pl.BlockSpec((count, width), lambda i: (0, 0)),
        ],
        out_specs=pl.BlockSpec((block, width), lambda i: (i, 0)),
        out_shape=jax.ShapeDtypeStruct((units, width), bf16),
        compiler_params=pltpu.CompilerParams(vmem_limit_bytes=32 * MIB),
        cost_estimate=pl.CostEstimate(
            flops=2 * units * width * both, bytes_accessed=12 * MIB, transcendentals=0
        ),
        name="gradient_term",
    )(slope, lam, own, other)


def per_device(embeddings, hidden_weight, score_weight, relevance, rank_pos, ideal_dcg):
    groups, local, width = embeddings.shape
    owned_rows = hidden_weight.shape[0]
    cores = lax.axis_size("c")
    chips = lax.axis_size("y") * lax.axis_size("x")
    planes = lax.axis_size("z")
    core = lax.axis_index("c")
    chip = lax.axis_index("y") * lax.axis_size("x") + lax.axis_index("x")
    own = embeddings.reshape(groups * local, width)

    weight = spread(hidden_weight, CHIPS, chips).reshape(chips * owned_rows, width)
    other = lax.ppermute(own, "c", [(0, 1), (1, 0)])
    unit = lax.dynamic_index_in_dim(
        score_weight.reshape(chips, cores, owned_rows), core, 1, keepdims=False
    ).reshape(chips * owned_rows, 1).astype(f32)
    code = (8 * rank_pos + relevance).astype(f32)

    pre, part = score(weight, own, other, unit)
    message = jnp.concatenate([part.reshape(2, groups, local), code[None]], axis=0)
    heard = spread(message, CAND, chips * cores)
    slope = slopes(pre, unit)

    heard = heard.reshape(chips, cores, 3, groups, local)
    scores = heard[:, :, 0] + heard[:, ::-1, 1]
    rank = jnp.floor(heard[:, :, 2] * 0.125)
    gain = jnp.exp2(heard[:, :, 2] - 8.0 * rank) - 1.0
    disc = 1.0 / jnp.log2(2.0 + rank)
    facts = jnp.stack([0.5 * scores, gain, disc]).transpose(0, 3, 1, 2, 4)
    mine = lax.dynamic_index_in_dim(facts, chip, 2, keepdims=False)
    mine = mine.reshape(3, groups, cores * local)[:, :, :, None]
    facts = facts.reshape(3, groups, chips * cores * local)[:, :, None, :]
    pull = (facts[1] - mine[1]) * jnp.abs(facts[2] - mine[2])
    pair_lam = jnp.sum(pull + jnp.abs(pull) * jnp.tanh(mine[0] - facts[0]), axis=-1)
    pair_lam = (pair_lam * (0.5 / ideal_dcg)[:, None]).reshape(groups, cores, local)
    pair_lam = pair_lam.transpose(1, 0, 2)
    pair_lam = jnp.where(core == 0, pair_lam, pair_lam[::-1])
    lambdas = pair_lam[0]

    term = gradient_term(slope, pair_lam.reshape(1, -1), own, other)
    terms = lax.all_to_all(
        term.reshape(chips, owned_rows, width), CHIPS, split_axis=0, concat_axis=0, tiled=True
    )
    owned = jnp.sum(terms.astype(f32), axis=0).astype(bf16)
    pieces = lax.all_to_all(
        owned.reshape(planes, owned_rows // planes, width), "z", split_axis=0, concat_axis=0, tiled=True
    )
    piece = jnp.sum(pieces.astype(f32), axis=0).astype(bf16)
    total = spread(piece, "z", planes).reshape(owned_rows, width).astype(f32)
    squares = jnp.sum(spread(jnp.sum(total * total), CAND, chips * cores))
    entries = owned_rows * width * chips * cores
    return total * lax.rsqrt(squares / entries + EPS), lambdas


def solution(mesh):
    fine = Mesh(mesh.devices.reshape(mesh.devices.shape[0], 4, 4, 2), ("z", "y", "x", "c"))
    return jax.shard_map(
        per_device,
        mesh=fine,
        in_specs=(
            P("z", CAND, None),
            P(CAND, None),
            P(),
            P("z", CAND),
            P("z", CAND),
            P("z"),
        ),
        out_specs=(P(CAND, None), P("z", CAND)),
        check_vma=False,
    )
```

time: 197 us -> 183 us (0.929)
  blocking collectives: 122 us -> 79.5 us
  Pallas kernels: 0 us -> 20.5 us
  matrix products: 18.4 us -> 0 us
  waiting for transfers between devices: 11.7 us -> 26 us
  local copies, waits for them, and re-layouts: 10.1 us -> 17.8 us
  starting transfers between devices: 24.8 us -> 30.1 us
    all_gather x3 -> x0, blocking collectives: 38.9 us -> none  [the longest x2 35.8 us: per_device(): labels = lax.all_gather(lax.all_gather(own_labels, 'x'), 'y')]
    pallas_call x0 -> x3, Pallas kernels: none -> 20.5 us  [the longest x1 8.39 us: score(): pl.pallas_call(score_kernel, grid=(units // block,), in_specs=[pl.BlockSp...]
    dot_general x2 -> x0, matrix products: 18.4 us -> none  [the longest x1 9.28 us: per_device(): lax.dot_general(weight, both, (((1,), (1,)), ((), ())), preferred_element...]
    all_to_all x3, waiting for transfers between devices: 11.7 us -> 23.3 us  [spread(): return lax.all_to_all(copies, axis, split_axis=0, concat_axis=0, tiled=True)]
    psum x1 -> x0, blocking collectives: 7.8 us -> none  [per_device(): pair = lax.psum(part, 'c')]
    unnamed x11 -> x18, local copies, waits for them, and re-layouts: 1.49 us -> 8.55 us
    all_to_all x3, starting transfers between devices: 19.9 us -> 25.2 us  [spread(): return lax.all_to_all(copies, axis, split_axis=0, concat_axis=0, tiled=True)]
    all_to_all x1, blocking collectives: 30.2 us -> 34.1 us  [per_device(): lax.all_to_all(term.reshape(chips, owned_rows, width), CHIPS, split_axis=...]
  transfers between devices with their start and end apart: 4 -> 4, of which waited for: 2 -> 3; matrix products, arithmetic and copies ran while one was open for 2% -> 1% of each run, Pallas kernels for 0% -> 4%
where the time goes in v3:
time: 183 us; the launch traced here: 182 us
  blocking collectives  79.5 us (43%)
  starting transfers between devices  30.1 us (16%)
  waiting for transfers between devices  26 us (14%)
  Pallas kernels  20.5 us (11%)
  local copies, waits for them, and re-layouts  17.8 us (10%)
  other arithmetic  6.48 us (4%)
    all_to_all x1, blocking collectives, per_device(): lax.all_to_all(term.reshape(chips, owned_rows, width), CHIPS, split_axis=...  34.1 us
    all_to_all x1, blocking collectives, per_device(): lax.all_to_all(owned.reshape(planes, owned_rows // planes, width), 'z', s...  28.3 us
    all_to_all x3, starting transfers between devices, spread(): return lax.all_to_all(copies, axis, split_axis=0, concat_axis=0, tiled=True)  25.2 us
    all_to_all x3, waiting for transfers between devices, spread(): return lax.all_to_all(copies, axis, split_axis=0, concat_axis=0, tiled=True)  23.3 us
    all_to_all x1, blocking collectives, spread(): return lax.all_to_all(copies, axis, split_axis=0, concat_axis=0, tiled=True)  17.1 us
    unnamed x18, local copies, waits for them, and re-layouts  8.55 us
    pallas_call x1, Pallas kernels, score(): pl.pallas_call(score_kernel, grid=(units // block,), in_specs=[pl.BlockSp...  8.39 us
    pallas_call x1, Pallas kernels, slopes(): pl.pallas_call(slope_kernel, grid=(units // block,), in_specs=[pl.BlockSp...  7.15 us
  transfers between devices with their start and end apart: 4, of which 3 were waited for; matrix products, arithmetic and copies ran while one was open for 1% of the time, Pallas kernels for 4%

profile of v3, /device:TPU:1, one launch (start us, length us, event | category | flops | bytes accessed | tf_op | source)
XLA Modules:
  0.0 182.1 jit_solution(14368868090299728661)
XLA Ops:
  0.6 2.5 %broadcast_in_dim.10 = bf16[16,64,1024]{2,1,0:T(8,128)(2,1)} broadcast(bf16[64,1024]{1,0:T(8,128)(2,1)} %param.7), dimensions={1,2} | broadcast | bytes 2228224 | tf_op jit(solution)/shard_map/broadcast_in_dim | solution.py:20
  3.2 7.7 %all-to-all-start = ((bf16[16,64,1024]{2,1,0:T(8,128)(2,1)}), bf16[16,64,1024]{2,1,0:T(8,128)(2,1)S(1)}, u32[]{:S(2)}, u32[]{:S(2)}) async-start(bf16[16,64,1024]{2,1,0:T(8,128)(2,1)} %broadcast_in_dim.10), calls=%async_computation | async-start | bytes 4194304 | tf_op jit(solution)/shard_map/all_to_all | solution.py:21
  10.9 4.9 %collective-permute-start = (bf16[768,1024]{1,0:T(8,128)(2,1)}, bf16[768,1024]{1,0:T(8,128)(2,1)}, u32[]{:S(2)}, u32[]{:S(2)}) collective-permute-start(bf16[768,1024]{1,0:T(8,128)(2,1)} %bitcast.33), channel_id=1, source_target_pairs={{0,1},{1,0},{2,3},{3,2},{4,5},{5,4},{6,7},{7,6},{8,9},{9,8},{10,11... | collective-permute-start | bytes 4718600 | tf_op jit(solution)/shard_map/ppermute | solution.py:155
  15.8 0.1 reshape.156
  15.9 0.5 reshape.163.unit_ref
  16.5 2.7 %collective-permute-done.other_ref = bf16[768,1024]{1,0:T(8,128)(2,1)} collective-permute-done((bf16[768,1024]{1,0:T(8,128)(2,1)}, bf16[768,1024]{1,0:T(8,128)(2,1)}, u32[]{:S(2)}, u32[]{:S(2)}) %collective-permute-start) | collective-permute-done | bytes 1572896 | tf_op jit(solution)/shard_map/ppermute | solution.py:155
  19.1 17.0 %all-to-all-done = bf16[16,64,1024]{2,1,0:T(8,128)(2,1)S(1)} async-done(((bf16[16,64,1024]{2,1,0:T(8,128)(2,1)}), bf16[16,64,1024]{2,1,0:T(8,128)(2,1)S(1)}, u32[]{:S(2)}, u32[]{:S(2)}) %all-to-all-start) | async-done | bytes 2097184 | tf_op jit(solution)/shard_map/all_to_all | solution.py:21
  36.2 1.4 copy-done.2
  37.6 8.4 %score.1 = (f32[1024,1536]{1,0:T(8,128)}, f32[1,1536]{1,0:T(1,128)S(1)}) custom-call(bf16[1024,1024]{1,0:T(8,128)(2,1)S(1)} %bitcast.31, bf16[768,1024]{1,0:T(8,128)(2,1)S(1)} %bitcast.34, bf16[768,1024]{1,0:T(8,128)(2,1)} %collective-permute-done.other_ref, f32[1024,1]{1,0:T(8,128)S(1)} %reshape.163.unit_ref), custom_call_target="tpu_custom_call" | custom-call | flops 3221225472 | bytes 12582912 | tf_op jit(solution)/shard_map/score/pallas_call | solution.py:53
  46.1 0.1 broadcast_in_dim.12
  46.2 1.2 reshape.172
  47.4 9.3 %all-to-all-start.1 = ((f32[32,1,2304]{2,1,0:T(1,128)}), f32[32,1,2304]{2,1,0:T(1,128)S(1)}, u32[]{:S(2)}, u32[]{:S(2)}) async-start(f32[32,1,2304]{2,1,0:T(1,128)} %reshape.172), calls=%async_computation.1 | async-start | bytes 589824 | tf_op jit(solution)/shard_map/all_to_all | solution.py:21
  56.7 2.8 %copy-done.1 = f32[1024,1536]{1,0:T(8,128)S(1)} copy-done((f32[1024,1536]{1,0:T(8,128)S(1)}, f32[1024,1536]{1,0:T(8,128)}, u32[]{:S(2)}) %copy-start.1) | copy-done | bytes 6291480
  59.5 7.2 %slopes.1.slope_ref = f32[1024,1536]{1,0:T(8,128)} custom-call(f32[1024,1536]{1,0:T(8,128)S(1)} %copy-done.1, f32[1024,1]{1,0:T(8,128)S(1)} %reshape.163.unit_ref), custom_call_target="tpu_custom_call" | custom-call | flops 3145728000 | bytes 12582912 | tf_op jit(solution)/shard_map/slopes/pallas_call | solution.py:93
  66.6 0.5 broadcast.93
  67.2 1.3 reduce.9
  68.5 0.4 reshape.173
  68.9 0.1 copy.42
  69.0 0.2 exponential_add_fusion
  69.2 0.2 pad_maximum_fusion
  69.4 0.1 fusion.4
  69.5 0.2 copy.48
  69.7 0.5 sub.78
  70.3 0.1 sub.76
  70.4 0.1 sub.73
  70.4 0.2 copy.45
  70.7 0.5 sub.71
  71.2 0.1 sub.68
  71.2 0.2 copy.43
  71.5 0.5 sub.66
  71.9 2.6 %add_reduce_fusion = f32[24,64]{1,0:T(8,128)S(1)} fusion(f32[24,1024]{1,0:T(8,128)S(1)} %sub.78, f32[24,64]{1,0:T(8,128)S(1)} %sub.76, f32[24,64]{1,0:T(8,128)S(1)} %sub.73, f32[24,1024]{1,0:T(8,128)S(1)} %sub.71, f32[24,64]{1,0:T(8,128)S(1)} %sub.68, f32[24,1024]{1,0:T(8,128)S(1)} %sub.66), kind=kLoop, calls=%fused_computation | loop fusion | flops 14154240 | bytes 319488 | tf_op jit(solution)/shard_map/reduce_sum | solution.py:176
  74.6 0.1 reduce_sum.54
  74.7 0.1 multiply_bitcast_fusion
  74.8 0.1 broadcast_select_fusion
  74.9 0.1 reshape.159.lam_ref
  75.0 2.8 %copy-done = f32[1024,1536]{1,0:T(8,128)S(1)} copy-done((f32[1024,1536]{1,0:T(8,128)S(1)}, f32[1024,1536]{1,0:T(8,128)}, u32[]{:S(2)}) %copy-start) | copy-done | bytes 6291480
  77.8 5.0 %gradient_term.1 = bf16[1024,1024]{1,0:T(8,128)(2,1)S(1)} custom-call(f32[1024,1536]{1,0:T(8,128)S(1)} %copy-done, f32[1,1536]{1,0:T(1,128)S(1)} %reshape.159.lam_ref, bf16[768,1024]{1,0:T(8,128)(2,1)S(1)} %bitcast.35, bf16[768,1024]{1,0:T(8,128)(2,1)} %collective-permute-done.other_ref), custom_call_target="tpu_custom_call" | custom-call | flops 3221225472 | bytes 12582912 | tf_op jit(solution)/shard_map/gradient_term/pallas_call | solution.py:125
  82.8 34.1 %all_to_all.31 = bf16[16,64,1024]{2,1,0:T(8,128)(2,1)S(1)} all-to-all(bf16[16,64,1024]{2,1,0:T(8,128)(2,1)S(1)} %bitcast.32), channel_id=1, replica_groups=mesh['z'=16,'y'=4,'x'=4,'c'=2] {'y','x'}, dimensions={0} | all-to-all | bytes 4194304 | tf_op jit(solution)/shard_map/all_to_all | solution.py:183
  117.0 0.4 reduce_sum.55
  117.4 28.3 %all_to_all.32 = bf16[16,4,1024]{2,1,0:T(4,128)(2,1)S(1)} all-to-all(bf16[16,4,1024]{2,1,0:T(4,128)(2,1)S(1)} %reshape.161), channel_id=1, replica_groups=mesh['z'=16,'y'=4,'x'=4,'c'=2] {'z'}, dimensions={0} | all-to-all | bytes 262144 | tf_op jit(solution)/shard_map/all_to_all | solution.py:187
  145.9 17.1 %all_to_all.33 = bf16[16,4,1024]{2,1,0:T(4,128)(2,1)S(1)} all-to-all(bf16[16,4,1024]{2,1,0:T(4,128)(2,1)S(1)} %broadcast_in_dim.13), channel_id=1, replica_groups=mesh['z'=16,'y'=4,'x'=4,'c'=2] {'z'}, dimensions={0} | all-to-all | bytes 262144 | tf_op jit(solution)/shard_map/all_to_all | solution.py:21
  162.9 0.7 fusion.2
  163.7 1.3 broadcast_in_dim.14
  164.9 8.2 %all-to-all-start.5 = ((f32[32,1,1]{2,1,0:T(1,128)}), f32[32,1,1]{2,1,0:T(1,128)S(1)}, u32[]{:S(2)}, u32[]{:S(2)}) async-start(f32[32,1,1]{2,1,0:T(1,128)} %broadcast_in_dim.14), calls=%async_computation.5 | async-start | bytes 32768 | tf_op jit(solution)/shard_map/all_to_all | solution.py:21
  173.1 0.6 slice.56
  173.7 6.3 %all-to-all-done.5 = f32[32,1,1]{2,1,0:T(1,128)S(1)} async-done(((f32[32,1,1]{2,1,0:T(1,128)}), f32[32,1,1]{2,1,0:T(1,128)S(1)}, u32[]{:S(2)}, u32[]{:S(2)}) %all-to-all-start.5) | async-done | bytes 160 | tf_op jit(solution)/shard_map/all_to_all | solution.py:21
  180.0 0.6 reduce_sum.58
  181.3 0.8 mul.100
  (33 shorter events, 0.6 us)
Async XLA Ops:
  3.1 12.6 %copy-start.6 = (bf16[2048]{0:T(1024)(128)(2,1)S(1)}, bf16[2048]{0:T(1024)(128)(2,1)}, u32[]{:S(2)}) copy-start(bf16[2048]{0:T(1024)(128)(2,1)} %param.8) | copy-start | bytes 12292
  3.1 13.3 %copy-start.7 = (f32[24]{0:T(128)S(1)}, f32[24]{0:T(128)}, u32[]{:S(2)}) copy-start(f32[24]{0:T(128)} %param.11) | copy-start | bytes 292
  3.2 13.3 %copy-start.4 = (s32[24,32]{1,0:T(8,128)S(1)}, s32[24,32]{1,0:T(8,128)}, u32[]{:S(2)}) copy-start(s32[24,32]{1,0:T(8,128)} %param.9) | copy-start | bytes 9220
  3.2 13.3 %copy-start.5 = (s32[24,32]{1,0:T(8,128)S(1)}, s32[24,32]{1,0:T(8,128)}, u32[]{:S(2)}) copy-start(s32[24,32]{1,0:T(8,128)} %param.10) | copy-start | bytes 9220
  3.2 33.0 %all-to-all-start = ((bf16[16,64,1024]{2,1,0:T(8,128)(2,1)}), bf16[16,64,1024]{2,1,0:T(8,128)(2,1)S(1)}, u32[]{:S(2)}, u32[]{:S(2)}) async-start(bf16[16,64,1024]{2,1,0:T(8,128)(2,1)} %broadcast_in_dim.10), calls=%async_computation | async-start | bytes 4194304 | tf_op jit(solution)/shard_map/all_to_all | solution.py:21
  10.9 8.3 %collective-permute-start = (bf16[768,1024]{1,0:T(8,128)(2,1)}, bf16[768,1024]{1,0:T(8,128)(2,1)}, u32[]{:S(2)}, u32[]{:S(2)}) collective-permute-start(bf16[768,1024]{1,0:T(8,128)(2,1)} %bitcast.33), channel_id=1, source_target_pairs={{0,1},{1,0},{2,3},{3,2},{4,5},{5,4},{6,7},{7,6},{8,9},{9,8},{10,11... | collective-permute-start | bytes 4718600 | tf_op jit(solution)/shard_map/ppermute | solution.py:155
  36.2 1.4 copy-start.2
  47.4 19.3 %all-to-all-start.1 = ((f32[32,1,2304]{2,1,0:T(1,128)}), f32[32,1,2304]{2,1,0:T(1,128)S(1)}, u32[]{:S(2)}, u32[]{:S(2)}) async-start(f32[32,1,2304]{2,1,0:T(1,128)} %reshape.172), calls=%async_computation.1 | async-start | bytes 589824 | tf_op jit(solution)/shard_map/all_to_all | solution.py:21
  56.7 2.8 %copy-start.1 = (f32[1024,1536]{1,0:T(8,128)S(1)}, f32[1024,1536]{1,0:T(8,128)}, u32[]{:S(2)}) copy-start(f32[1024,1536]{1,0:T(8,128)} %get-tuple-element.4.pre_ref) | copy-start | bytes 18874372
  71.2 3.8 %copy-start.3 = (bf16[24,32,1024]{2,1,0:T(8,128)(2,1)S(1)}, bf16[24,32,1024]{2,1,0:T(8,128)(2,1)}, u32[]{:S(2)}) copy-start(bf16[24,32,1024]{2,1,0:T(8,128)(2,1)} %param.6) | copy-start | bytes 4718596
  75.0 2.8 %copy-start = (f32[1024,1536]{1,0:T(8,128)S(1)}, f32[1024,1536]{1,0:T(8,128)}, u32[]{:S(2)}) copy-start(f32[1024,1536]{1,0:T(8,128)} %slopes.1.slope_ref) | copy-start | bytes 18874372
  164.9 15.1 %all-to-all-start.5 = ((f32[32,1,1]{2,1,0:T(1,128)}), f32[32,1,1]{2,1,0:T(1,128)S(1)}, u32[]{:S(2)}, u32[]{:S(2)}) async-start(f32[32,1,1]{2,1,0:T(1,128)} %broadcast_in_dim.14), calls=%async_computation.5 | async-start | bytes 32768 | tf_op jit(solution)/shard_map/all_to_all | solution.py:21

commit v4 on v3

v4 whole, which is shorter than its diff:
```python
import functools

import jax
import jax.numpy as jnp
from jax import lax
from jax.experimental import pallas as pl
from jax.experimental.pallas import tpu as pltpu
from jax.sharding import Mesh
from jax.sharding import PartitionSpec as P

EPS = 1e-06
GELU_A = 0.7978845608028654
GELU_B = 0.044715
CHIPS = ("y", "x")
CAND = ("y", "x", "c")
MIB = 1 << 20
LANES = 128
f32 = jnp.float32
bf16 = jnp.bfloat16


def spread(value, axis, size):
    copies = jnp.broadcast_to(value[None], (size, *value.shape))
    return lax.all_to_all(copies, axis, split_axis=0, concat_axis=0, tiled=True)


def score_kernel(weight_ref, own_ref, other_ref, unit_ref, code_ref, slope_ref, message_ref, part_ref):
    step = pl.program_id(0)

    @pl.when(step == 0)
    def _():
        part_ref[...] = jnp.zeros_like(part_ref)

    weight = weight_ref[...]
    unit = unit_ref[...]
    half_unit = 0.5 * unit
    for half, rows_ref in enumerate((own_ref, other_ref)):
        count = rows_ref.shape[0]
        for first in range(0, count, 256):
            pre = lax.dot_general(
                weight,
                rows_ref[first : first + 256, :],
                (((1,), (1,)), ((), ())),
                preferred_element_type=f32,
            )
            cols = slice(half * count + first, half * count + first + 256)
            square = pre * pre
            tanh = jnp.tanh(pre * (GELU_A + (GELU_A * GELU_B) * square))
            upper = 1.0 + tanh
            acts = ((0.5 * pre) * upper).astype(bf16).astype(f32)
            part_ref[:, cols] += jnp.sum(acts * unit, axis=0, keepdims=True)
            slope_ref[:, cols] = half_unit * (
                upper
                + pre * (1.0 - tanh * tanh) * (GELU_A + (3.0 * GELU_A * GELU_B) * square)
            )

    @pl.when(step == pl.num_programs(0) - 1)
    def _():
        row = jnp.concatenate([part_ref[...], code_ref[...]], axis=1)
        for d in range(message_ref.shape[0]):
            message_ref[d] = row


def score(weight, own, other, unit, code, devices):
    units, width = weight.shape
    count = own.shape[0]
    block = units // 2
    whole = lambda i: (0, 0)
    return pl.pallas_call(
        score_kernel,
        grid=(units // block,),
        in_specs=[
            pl.BlockSpec((block, width), lambda i: (i, 0)),
            pl.BlockSpec((count, width), whole),
            pl.BlockSpec((count, width), whole),
            pl.BlockSpec((block, 1), lambda i: (i, 0)),
            pl.BlockSpec((1, count), whole),
        ],
        out_specs=[
            pl.BlockSpec((block, 2 * count), lambda i: (i, 0)),
            pl.BlockSpec((devices, 1, 3 * count), lambda i: (0, 0, 0)),
        ],
        out_shape=[
            pltpu.HBM((units, 2 * count), f32),
            jax.ShapeDtypeStruct((devices, 1, 3 * count), f32),
        ],
        scratch_shapes=[pltpu.VMEM((1, 2 * count), f32)],
        compiler_params=pltpu.CompilerParams(vmem_limit_bytes=40 * MIB),
        cost_estimate=pl.CostEstimate(
            flops=4 * units * width * count,
            bytes_accessed=12 * MIB,
            transcendentals=2 * units * count,
        ),
        name="score",
    )(weight, own, other, unit, code)


def term_kernel(slope_ref, lam_ref, own_ref, other_ref, out_ref):
    count = own_ref.shape[0]
    out = None
    for half, rows_ref in enumerate((own_ref, other_ref)):
        grad_pre = (slope_ref[:, half * count : (half + 1) * count] * lam_ref[half : half + 1, :]).astype(bf16)
        part = jnp.dot(grad_pre, rows_ref[...], preferred_element_type=f32)
        out = part if out is None else out + part
    out_ref[...] = out.astype(bf16)


def gradient_term(slope, lam, own, other):
    units, both = slope.shape
    count, width = own.shape
    block = units // 2
    return pl.pallas_call(
        term_kernel,
        grid=(units // block,),
        in_specs=[
            pl.BlockSpec((block, both), lambda i: (i, 0)),
            pl.BlockSpec((2, count), lambda i: (0, 0)),
            pl.BlockSpec((count, width), lambda i: (0, 0)),
            pl.BlockSpec((count, width), lambda i: (0, 0)),
        ],
        out_specs=pl.BlockSpec((block, width), lambda i: (i, 0)),
        out_shape=jax.ShapeDtypeStruct((units, width), bf16),
        compiler_params=pltpu.CompilerParams(vmem_limit_bytes=32 * MIB),
        cost_estimate=pl.CostEstimate(
            flops=2 * units * width * both, bytes_accessed=12 * MIB, transcendentals=0
        ),
        name="gradient_term",
    )(slope, lam, own, other)


def pair_kernel(place_ref, heard_ref, half_ref, lam_ref, raw_ref, far_ref, own_ref, sum_ref):
    devices, _, size = heard_ref.shape
    width = size // 3
    local = 32
    for d in range(devices):
        raw_ref[d : d + 1, :] = heard_ref[d]
    row = lax.broadcasted_iota(jnp.int32, (devices, width), 0)
    near = raw_ref[:, width : 2 * width]
    near = jnp.where(row % 2 == 0, pltpu.roll(near, devices - 1, 0), pltpu.roll(near, 1, 0))
    code = raw_ref[:, 2 * width :]
    rank = jnp.floor(code * 0.125)
    level = (code - 8.0 * rank).astype(jnp.int32)
    far_ref[0] = 0.5 * (raw_ref[:, :width] + near)
    far_ref[1] = (jnp.left_shift(jnp.ones_like(level), level) - 1).astype(f32)
    far_ref[2] = 0.6931471805599453 / jnp.log(2.0 + rank)

    lane = lax.broadcasted_iota(jnp.int32, (LANES, LANES), 1)
    sub = lax.broadcasted_iota(jnp.int32, (LANES, LANES), 0)
    ones = (lane // local == sub // local).astype(f32)
    pick = lax.broadcasted_iota(jnp.int32, (local, width), 1) % local == lax.broadcasted_iota(
        jnp.int32, (local, width), 0
    )
    for c in range(2):
        mine = row == 2 * place_ref[0] + c
        for k in range(3):
            value = jnp.sum(jnp.where(mine, far_ref[k], 0.0), axis=0, keepdims=True)
            value = jnp.where(pick, value, 0.0)
            for first in range(0, width, LANES):
                at = ((first // LANES * 3 + k) * 2 + c) * local
                own_ref[at : at + local, :] = value[:, first : first + LANES]
    own_ref[...] = jnp.dot(
        own_ref[...], ones, precision=lax.Precision.HIGHEST, preferred_element_type=f32
    )
    pairs = 2 * local
    for first in range(0, width, LANES):
        cols = slice(first, first + LANES)
        at = first // LANES * 3 * pairs
        own_score, own_gain, own_disc = (
            own_ref[at + k * pairs : at + (k + 1) * pairs, :] for k in range(3)
        )

        def step(n, total):
            rows = pl.ds(pl.multiple_of(8 * n, 8), 8)
            score, gain, disc = far_ref[0, rows, cols], far_ref[1, rows, cols], far_ref[2, rows, cols]
            for j in range(8):
                gain_diff = gain[j : j + 1] - own_gain
                disc_diff = jnp.abs(disc[j : j + 1] - own_disc)
                pull = gain_diff * disc_diff
                total += pull + jnp.abs(pull) * jnp.tanh(own_score - score[j : j + 1])
            return total

        at = first // LANES * pairs
        sum_ref[at : at + pairs, :] = lax.fori_loop(0, devices // 8, step, jnp.zeros((pairs, LANES), f32))
    sum_ref[...] = jnp.dot(
        sum_ref[...], ones, precision=lax.Precision.HIGHEST, preferred_element_type=f32
    )
    for first in range(0, width, LANES):
        cols = slice(first, first + LANES)
        at = first // LANES * pairs
        lam = [
            half_ref[:, cols]
            * jnp.sum(
                jnp.where(pick[:, cols], sum_ref[at + c * local : at + (c + 1) * local, :], 0.0), axis=0, keepdims=True
            )
            for c in range(2)
        ]
        south = place_ref[1] == 0
        lam_ref[0:1, cols] = jnp.where(south, lam[0], lam[1])
        lam_ref[1:2, cols] = jnp.where(south, lam[1], lam[0])


def pair_lambdas(heard, half, place):
    devices, _, size = heard.shape
    width = size // 3
    return pl.pallas_call(
        pair_kernel,
        in_specs=[
            pl.BlockSpec(memory_space=pltpu.SMEM),
            pl.BlockSpec(memory_space=pltpu.VMEM),
            pl.BlockSpec(memory_space=pltpu.VMEM),
        ],
        out_specs=pl.BlockSpec(memory_space=pltpu.VMEM),
        out_shape=jax.ShapeDtypeStruct((2, width), f32),
        scratch_shapes=[
            pltpu.VMEM((devices, size), f32),
            pltpu.VMEM((3, devices, width), f32),
            pltpu.VMEM((width // LANES * 6 * 32, LANES), f32),
            pltpu.VMEM((width // LANES * 2 * 32, LANES), f32),
        ],
        compiler_params=pltpu.CompilerParams(vmem_limit_bytes=16 * MIB),
        cost_estimate=pl.CostEstimate(flops=2 * MIB * 10, bytes_accessed=MIB, transcendentals=2 * MIB),
        name="pair_lambdas",
    )(place, heard, half)


def copies_kernel(block_ref, out_ref):
    for k in range(out_ref.shape[0]):
        out_ref[k] = block_ref[...]


def copies(block, count):
    rows, width = block.shape
    step = count // 4
    return pl.pallas_call(
        copies_kernel,
        grid=(count // step,),
        in_specs=[pl.BlockSpec((rows, width), lambda i: (0, 0))],
        out_specs=pl.BlockSpec((step, rows, width), lambda i: (i, 0, 0)),
        out_shape=jax.ShapeDtypeStruct((count, rows, width), block.dtype),
        compiler_params=pltpu.CompilerParams(vmem_limit_bytes=16 * MIB),
        name="copies",
    )(block)


def squares_kernel(total_ref, out_ref):
    total = total_ref[...].astype(f32)
    square = jnp.sum(total * total, axis=0)
    square = jnp.sum(jnp.sum(square, axis=0, keepdims=True), axis=1, keepdims=True)
    row = jnp.broadcast_to(square, (1, LANES))
    for d in range(out_ref.shape[0]):
        out_ref[d] = row


def squares(total, devices):
    return pl.pallas_call(
        squares_kernel,
        in_specs=[pl.BlockSpec(memory_space=pltpu.VMEM)],
        out_specs=pl.BlockSpec(memory_space=pltpu.VMEM),
        out_shape=jax.ShapeDtypeStruct((devices, 1, LANES), f32),
        compiler_params=pltpu.CompilerParams(vmem_limit_bytes=16 * MIB),
        name="squares",
    )(total)


def scaled_kernel(entries, total_ref, heard_ref, out_ref):
    square = jnp.sum(heard_ref[...], axis=0)
    scale = lax.rsqrt(square * (1.0 / entries) + EPS)
    planes, rows, cut = total_ref.shape
    across = out_ref.shape[1] // cut
    scale = jnp.concatenate([scale] * (cut // LANES), axis=1)
    for k in range(planes):
        at, col = k // across * rows, k % across * cut
        out_ref[at : at + rows, col : col + cut] = total_ref[k].astype(f32) * scale


def scaled(total, heard, rows, width, entries):
    return pl.pallas_call(
        functools.partial(scaled_kernel, entries),
        in_specs=[pl.BlockSpec(memory_space=pltpu.VMEM)] * 2,
        out_specs=pl.BlockSpec(memory_space=pltpu.VMEM),
        out_shape=jax.ShapeDtypeStruct((rows, width), f32),
        compiler_params=pltpu.CompilerParams(vmem_limit_bytes=16 * MIB),
        name="scaled",
    )(total, heard)


def per_device(embeddings, hidden_weight, score_weight, relevance, rank_pos, ideal_dcg):
    groups, local, width = embeddings.shape
    owned_rows = hidden_weight.shape[0]
    cores = lax.axis_size("c")
    chips = lax.axis_size("y") * lax.axis_size("x")
    planes = lax.axis_size("z")
    core = lax.axis_index("c")
    chip = lax.axis_index("y") * lax.axis_size("x") + lax.axis_index("x")
    own = embeddings.reshape(groups * local, width)

    weight = lax.all_to_all(
        copies(hidden_weight, chips), CHIPS, split_axis=0, concat_axis=0, tiled=True
    ).reshape(chips * owned_rows, width)
    other = lax.ppermute(own, "c", [(0, 1), (1, 0)])
    unit = lax.dynamic_index_in_dim(
        score_weight.reshape(chips, cores, owned_rows), core, 1, keepdims=False
    ).reshape(chips * owned_rows, 1).astype(f32)
    code = (8 * rank_pos + relevance).astype(f32).reshape(1, groups * local)
    half = jnp.repeat(0.5 / ideal_dcg, local).reshape(1, groups * local)
    place = jnp.stack([chip, core]).astype(jnp.int32)

    slope, message = score(weight, own, other, unit, code, chips * cores)
    heard = lax.all_to_all(message, CAND, split_axis=0, concat_axis=0, tiled=True)
    lam = pair_lambdas(heard, half, place)
    lambdas = lam[0].reshape(groups, local)

    term = gradient_term(slope, lam, own, other)
    terms = lax.all_to_all(
        term.reshape(chips, owned_rows, width), CHIPS, split_axis=0, concat_axis=0, tiled=True
    )
    owned = jnp.sum(terms.astype(f32), axis=0).astype(bf16)
    across = planes * 8 // owned_rows
    owned = owned.reshape(owned_rows // 8, 8, across, width // across).transpose(0, 2, 1, 3)
    pieces = lax.all_to_all(
        owned.reshape(planes, 8, width // across), "z", split_axis=0, concat_axis=0, tiled=True
    )
    piece = jnp.sum(pieces.astype(f32), axis=0).astype(bf16)
    total = spread(piece, "z", planes)
    entries = owned_rows * width * chips * cores
    square = lax.all_to_all(
        squares(total, chips * cores), CAND, split_axis=0, concat_axis=0, tiled=True
    )
    return scaled(total, square, owned_rows, width, entries), lambdas


def solution(mesh):
    fine = Mesh(mesh.devices.reshape(mesh.devices.shape[0], 4, 4, 2), ("z", "y", "x", "c"))
    return jax.shard_map(
        per_device,
        mesh=fine,
        in_specs=(
            P("z", CAND, None),
            P(CAND, None),
            P(),
            P("z", CAND),
            P("z", CAND),
            P("z"),
        ),
        out_specs=(P(CAND, None), P("z", CAND)),
        check_vma=False,
    )
```

time: 183 us -> 172 us (0.940)
  local copies, waits for them, and re-layouts: 17.8 us -> 6.58 us
  waiting for transfers between devices: 26 us -> 34.9 us
  other arithmetic: 6.48 us -> 0.55 us
  blocking collectives: 79.5 us -> 76 us
  Pallas kernels: 20.5 us -> 22.8 us
    all_to_all x3, waiting for transfers between devices: 23.3 us -> 32.3 us  [the longest x1 17 us: per_device(): lax.all_to_all(copies(hidden_weight, chips), CHIPS, split_axis=0, concat_...]
    reduce_sum x3 -> x0, other arithmetic: 3.99 us -> none  [the longest x1 2.62 us: per_device(): jnp.sum(pull + jnp.abs(pull) * jnp.tanh(mine[0] - facts[0]), axis=-1)]
    broadcast_in_dim x4 -> x1, local copies, waits for them, and re-layouts: 3.89 us -> 0.01 us  [spread(): copies = jnp.broadcast_to(value[None], (size, *value.shape))]
    all_to_all x1, blocking collectives: 34.1 us -> 30.6 us  [per_device(): lax.all_to_all(term.reshape(chips, owned_rows, width), CHIPS, split_axis=...]
    unnamed x18 -> x16, local copies, waits for them, and re-layouts: 8.55 us -> 5.1 us
    pallas_call x1, Pallas kernels: 8.39 us -> 10.4 us  [score(): pl.pallas_call(score_kernel, grid=(units // block,), in_specs=[pl.BlockSp...]
    pallas_call x1 -> x4, Pallas kernels: 7.15 us -> 7.42 us  [the longest x1 4.07 us: pair_lambdas(): pl.pallas_call(pair_kernel, in_specs=[pl.BlockSpec(memory_space=pltpu.SME...]
  transfers between devices with their start and end apart: 4 -> 4, of which waited for: 3 -> 4; matrix products, arithmetic and copies ran while one was open for 1% -> 1% of each run, Pallas kernels for 4% -> 0%
where the time goes in v4:
time: 172 us
  blocking collectives  76 us (44%)
  waiting for transfers between devices  34.9 us (20%)
  starting transfers between devices  29.9 us (17%)
  Pallas kernels  22.8 us (13%)
  local copies, waits for them, and re-layouts  6.58 us (4%)
    all_to_all x1, blocking collectives, per_device(): lax.all_to_all(term.reshape(chips, owned_rows, width), CHIPS, split_axis=...  30.6 us
    all_to_all x1, blocking collectives, per_device(): lax.all_to_all(owned.reshape(planes, 8, width // across), 'z', split_axis...  28.3 us
    all_to_all x1, blocking collectives, spread(): return lax.all_to_all(copies, axis, split_axis=0, concat_axis=0, tiled=True)  17.1 us
    all_to_all x1, waiting for transfers between devices, per_device(): lax.all_to_all(copies(hidden_weight, chips), CHIPS, split_axis=0, concat_...  17 us
    pallas_call x1, Pallas kernels, score(): pl.pallas_call(score_kernel, grid=(units // block,), in_specs=[pl.BlockSp...  10.4 us
    all_to_all x1, starting transfers between devices, per_device(): lax.all_to_all(message, CAND, split_axis=0, concat_axis=0, tiled=True)  9.3 us
    all_to_all x1, waiting for transfers between devices, per_device(): lax.all_to_all(message, CAND, split_axis=0, concat_axis=0, tiled=True)  9.04 us
    all_to_all x1, starting transfers between devices, per_device(): lax.all_to_all(squares(total, chips * cores), CAND, split_axis=0, concat_...  8.03 us
  transfers between devices with their start and end apart: 4, of which 4 were waited for; matrix products, arithmetic and copies ran while one was open for 1% of the time, Pallas kernels for 0%

profile of v4, /device:TPU:1, one launch (start us, length us, event | category | flops | bytes accessed | tf_op | source)
XLA Modules:
  0.0 171.6 jit_solution(1503357561867890027)
XLA Ops:
  0.6 0.0 copy-start
  0.6 0.9 copy-done
  1.5 1.9 %copies.1 = bf16[16,64,1024]{2,1,0:T(8,128)(2,1)} custom-call(bf16[64,1024]{1,0:T(8,128)(2,1)S(1)} %copy-done), custom_call_target="tpu_custom_call" | custom-call | tf_op jit(solution)/shard_map/copies/pallas_call | solution.py:234
  3.4 0.0 copy-start.6
  3.4 0.0 copy-start.4
  3.4 0.0 copy-start.5
  3.4 7.7 %all-to-all-start = ((bf16[16,64,1024]{2,1,0:T(8,128)(2,1)}), bf16[16,64,1024]{2,1,0:T(8,128)(2,1)S(1)}, u32[]{:S(2)}, u32[]{:S(2)}) async-start(bf16[16,64,1024]{2,1,0:T(8,128)(2,1)} %copies.1), calls=%async_computation | async-start | bytes 4194304 | tf_op jit(solution)/shard_map/all_to_all | solution.py:297
  11.1 4.9 %collective-permute-start = (bf16[768,1024]{1,0:T(8,128)(2,1)}, bf16[768,1024]{1,0:T(8,128)(2,1)}, u32[]{:S(2)}, u32[]{:S(2)}) collective-permute-start(bf16[768,1024]{1,0:T(8,128)(2,1)} %bitcast.12), channel_id=1, source_target_pairs={{0,1},{1,0},{2,3},{3,2},{4,5},{5,4},{6,7},{7,6},{8,9},{9,8},{10,11... | collective-permute-start | bytes 4718600 | tf_op jit(solution)/shard_map/ppermute | solution.py:300
  16.0 0.0 copy-done.6
  16.0 0.1 reshape.44
  16.2 0.5 reshape.50.unit_ref
  16.6 0.0 copy-done.4
  16.6 0.0 copy-done.5
  16.7 0.1 reshape.45.code_ref
  16.8 2.6 %collective-permute-done.other_ref = bf16[768,1024]{1,0:T(8,128)(2,1)} collective-permute-done((bf16[768,1024]{1,0:T(8,128)(2,1)}, bf16[768,1024]{1,0:T(8,128)(2,1)}, u32[]{:S(2)}, u32[]{:S(2)}) %collective-permute-start) | collective-permute-done | bytes 1572896 | tf_op jit(solution)/shard_map/ppermute | solution.py:300
  19.4 17.0 %all-to-all-done = bf16[16,64,1024]{2,1,0:T(8,128)(2,1)S(1)} async-done(((bf16[16,64,1024]{2,1,0:T(8,128)(2,1)}), bf16[16,64,1024]{2,1,0:T(8,128)(2,1)S(1)}, u32[]{:S(2)}, u32[]{:S(2)}) %all-to-all-start) | async-done | bytes 2097184 | tf_op jit(solution)/shard_map/all_to_all | solution.py:297
  36.4 0.0 copy-start.1
  36.4 1.4 copy-done.1
  37.8 0.0 copy-start.7
  37.8 10.4 %score.1 = (f32[1024,1536]{1,0:T(8,128)}, f32[32,1,2304]{2,1,0:T(1,128)}) custom-call(bf16[1024,1024]{1,0:T(8,128)(2,1)S(1)} %bitcast.10, bf16[768,1024]{1,0:T(8,128)(2,1)S(1)} %bitcast.13, bf16[768,1024]{1,0:T(8,128)(2,1)} %collective-permute-done.other_ref, f32[1024,1]{1,0:T(8,128)S(1)} %reshape.50.unit_ref, f32[1,768]{1,0:T(1,128)S(1)} %reshape.45.code_ref), custom_call_target="tpu_custom_call" | custom-call | flops 3221225472 | bytes 12582912 | tf_op jit(solution)/shard_map/score/pallas_call | solution.py:69
  48.2 9.3 %all-to-all-start.1 = ((f32[32,1,2304]{2,1,0:T(1,128)}), f32[32,1,2304]{2,1,0:T(1,128)S(1)}, u32[]{:S(2)}, u32[]{:S(2)}) async-start(f32[32,1,2304]{2,1,0:T(1,128)} %get-tuple-element.5), calls=%async_computation.1 | async-start | bytes 589824 | tf_op jit(solution)/shard_map/all_to_all | solution.py:309
  57.5 0.0 copy-done.7
  57.5 0.0 copy-start.2
  57.5 0.1 broadcast_in_dim.4
  57.6 0.1 reshape_reshape.3.half_ref
  57.7 0.1 pad_add_fusion.place_ref
  57.8 9.0 %all-to-all-done.1.heard_ref = f32[32,1,2304]{2,1,0:T(1,128)S(1)} async-done(((f32[32,1,2304]{2,1,0:T(1,128)}), f32[32,1,2304]{2,1,0:T(1,128)S(1)}, u32[]{:S(2)}, u32[]{:S(2)}) %all-to-all-start.1) | async-done | bytes 294944 | tf_op jit(solution)/shard_map/all_to_all | solution.py:309
  66.8 4.1 %pair_lambdas.1.lam_ref = f32[2,768]{1,0:T(2,128)S(1)} custom-call(s32[2]{0:T(128)S(1)} %pad_add_fusion.place_ref, f32[32,1,2304]{2,1,0:T(1,128)S(1)} %all-to-all-done.1.heard_ref, f32[1,768]{1,0:T(1,128)S(1)} %reshape_reshape.3.half_ref), custom_call_target="tpu_custom_call" | custom-call | flops 20971520 | bytes 1048576 | tf_op jit(solution)/shard_map/pair_lambdas/pallas_call | solution.py:205
  70.9 0.0 copy-done.2
  70.9 0.0 copy-start.3
  70.9 2.8 %copy-done.3 = f32[1024,1536]{1,0:T(8,128)S(1)} copy-done((f32[1024,1536]{1,0:T(8,128)S(1)}, f32[1024,1536]{1,0:T(8,128)}, u32[]{:S(2)}) %copy-start.3) | copy-done | bytes 6291480
  73.7 5.0 %gradient_term.1 = bf16[1024,1024]{1,0:T(8,128)(2,1)S(1)} custom-call(f32[1024,1536]{1,0:T(8,128)S(1)} %copy-done.3, f32[2,768]{1,0:T(2,128)S(1)} %pair_lambdas.1.lam_ref, bf16[768,1024]{1,0:T(8,128)(2,1)S(1)} %bitcast.14, bf16[768,1024]{1,0:T(8,128)(2,1)} %collective-permute-done.other_ref), custom_call_target="tpu_custom_call" | custom-call | flops 3221225472 | bytes 12582912 | tf_op jit(solution)/shard_map/gradient_term/pallas_call | solution.py:112
  78.7 30.6 %all_to_all.30 = bf16[16,64,1024]{2,1,0:T(8,128)(2,1)S(1)} all-to-all(bf16[16,64,1024]{2,1,0:T(8,128)(2,1)S(1)} %bitcast.11), channel_id=1, replica_groups=mesh['z'=16,'y'=4,'x'=4,'c'=2] {'y','x'}, dimensions={0} | all-to-all | bytes 4194304 | tf_op jit(solution)/shard_map/all_to_all | solution.py:314
  109.3 0.4 reduce_sum.24
  109.7 28.3 %all_to_all.31 = bf16[16,8,512]{2,1,0:T(8,128)(2,1)S(1)} all-to-all(bf16[16,8,512]{2,1,0:T(8,128)(2,1)S(1)} %bitcast.15), channel_id=1, replica_groups=mesh['z'=16,'y'=4,'x'=4,'c'=2] {'z'}, dimensions={0} | all-to-all | bytes 262144 | tf_op jit(solution)/shard_map/all_to_all | solution.py:320
  138.1 17.1 %all_to_all.32.total_ref = bf16[16,8,512]{2,1,0:T(8,128)(2,1)S(1)} all-to-all(bf16[16,8,512]{2,1,0:T(8,128)(2,1)S(1)} %broadcast_in_dim.10), channel_id=1, replica_groups=mesh['z'=16,'y'=4,'x'=4,'c'=2] {'z'}, dimensions={0} | all-to-all | bytes 262144 | tf_op jit(solution)/shard_map/all_to_all | solution.py:24
  155.2 0.7 squares.1
  155.9 8.0 %all-to-all-start.5 = ((f32[32,1,128]{2,1,0:T(1,128)}), f32[32,1,128]{2,1,0:T(1,128)S(1)}, u32[]{:S(2)}, u32[]{:S(2)}) async-start(f32[32,1,128]{2,1,0:T(1,128)} %squares.1), calls=%async_computation.5 | async-start | bytes 32768 | tf_op jit(solution)/shard_map/all_to_all | solution.py:326
  163.9 0.7 reshape_squeeze.3
  164.6 6.2 %all-to-all-done.5.heard_ref = f32[32,1,128]{2,1,0:T(1,128)S(1)} async-done(((f32[32,1,128]{2,1,0:T(1,128)}), f32[32,1,128]{2,1,0:T(1,128)S(1)}, u32[]{:S(2)}, u32[]{:S(2)}) %all-to-all-start.5) | async-done | bytes 16416 | tf_op jit(solution)/shard_map/all_to_all | solution.py:326
  170.8 0.8 scaled.1
  (6 shorter events, 0.1 us)
Async XLA Ops:
  0.6 0.9 copy-start
  3.4 12.6 %copy-start.6 = (bf16[2048]{0:T(1024)(128)(2,1)S(1)}, bf16[2048]{0:T(1024)(128)(2,1)}, u32[]{:S(2)}) copy-start(bf16[2048]{0:T(1024)(128)(2,1)} %param.8) | copy-start | bytes 12292
  3.4 13.2 %copy-start.4 = (s32[24,32]{1,0:T(8,128)S(1)}, s32[24,32]{1,0:T(8,128)}, u32[]{:S(2)}) copy-start(s32[24,32]{1,0:T(8,128)} %param.9) | copy-start | bytes 9220
  3.4 13.2 %copy-start.5 = (s32[24,32]{1,0:T(8,128)S(1)}, s32[24,32]{1,0:T(8,128)}, u32[]{:S(2)}) copy-start(s32[24,32]{1,0:T(8,128)} %param.10) | copy-start | bytes 9220
  3.4 33.0 %all-to-all-start = ((bf16[16,64,1024]{2,1,0:T(8,128)(2,1)}), bf16[16,64,1024]{2,1,0:T(8,128)(2,1)S(1)}, u32[]{:S(2)}, u32[]{:S(2)}) async-start(bf16[16,64,1024]{2,1,0:T(8,128)(2,1)} %copies.1), calls=%async_computation | async-start | bytes 4194304 | tf_op jit(solution)/shard_map/all_to_all | solution.py:297
  11.1 8.3 %collective-permute-start = (bf16[768,1024]{1,0:T(8,128)(2,1)}, bf16[768,1024]{1,0:T(8,128)(2,1)}, u32[]{:S(2)}, u32[]{:S(2)}) collective-permute-start(bf16[768,1024]{1,0:T(8,128)(2,1)} %bitcast.12), channel_id=1, source_target_pairs={{0,1},{1,0},{2,3},{3,2},{4,5},{5,4},{6,7},{7,6},{8,9},{9,8},{10,11... | collective-permute-start | bytes 4718600 | tf_op jit(solution)/shard_map/ppermute | solution.py:300
  36.4 1.4 copy-start.1
  37.8 19.7 %copy-start.7 = (f32[24]{0:T(128)S(1)}, f32[24]{0:T(128)}, u32[]{:S(2)}) copy-start(f32[24]{0:T(128)} %param.11) | copy-start | bytes 292
  48.2 18.6 %all-to-all-start.1 = ((f32[32,1,2304]{2,1,0:T(1,128)}), f32[32,1,2304]{2,1,0:T(1,128)S(1)}, u32[]{:S(2)}, u32[]{:S(2)}) async-start(f32[32,1,2304]{2,1,0:T(1,128)} %get-tuple-element.5), calls=%async_computation.1 | async-start | bytes 589824 | tf_op jit(solution)/shard_map/all_to_all | solution.py:309
  57.5 13.4 %copy-start.2 = (bf16[24,32,1024]{2,1,0:T(8,128)(2,1)S(1)}, bf16[24,32,1024]{2,1,0:T(8,128)(2,1)}, u32[]{:S(2)}) copy-start(bf16[24,32,1024]{2,1,0:T(8,128)(2,1)} %param.6) | copy-start | bytes 4718596
  70.9 2.8 %copy-start.3 = (f32[1024,1536]{1,0:T(8,128)S(1)}, f32[1024,1536]{1,0:T(8,128)}, u32[]{:S(2)}) copy-start(f32[1024,1536]{1,0:T(8,128)} %get-tuple-element.4.slope_ref) | copy-start | bytes 18874372
  155.9 14.9 %all-to-all-start.5 = ((f32[32,1,128]{2,1,0:T(1,128)}), f32[32,1,128]{2,1,0:T(1,128)S(1)}, u32[]{:S(2)}, u32[]{:S(2)}) async-start(f32[32,1,128]{2,1,0:T(1,128)} %squares.1), calls=%async_computation.5 | async-start | bytes 32768 | tf_op jit(solution)/shard_map/all_to_all | solution.py:326

commit v5 on v4

--- a/solution.py
+++ b/solution.py
@@ -19,72 +19,89 @@
 bf16 = jnp.bfloat16
 
 
+def in_hbm(*values):
+    return tuple(pltpu.with_memory_space_constraint(v, pltpu.HBM) for v in values)
+
+
 def spread(value, axis, size):
     copies = jnp.broadcast_to(value[None], (size, *value.shape))
     return lax.all_to_all(copies, axis, split_axis=0, concat_axis=0, tiled=True)
 
 
-def score_kernel(weight_ref, own_ref, other_ref, unit_ref, code_ref, slope_ref, message_ref, part_ref):
-    step = pl.program_id(0)
-
-    @pl.when(step == 0)
-    def _():
-        part_ref[...] = jnp.zeros_like(part_ref)
-
-    weight = weight_ref[...]
-    unit = unit_ref[...]
-    half_unit = 0.5 * unit
-    for half, rows_ref in enumerate((own_ref, other_ref)):
-        count = rows_ref.shape[0]
-        for first in range(0, count, 256):
+def score_kernel(
+    weight_ref, own_hbm, other_hbm, unit_ref, code_ref, slope_hbm, message_ref,
+    rows_ref, slope_ref, part_ref, in_sems, out_sems,
+):
+    count = own_hbm.shape[0]
+    units = weight_ref.shape[0]
+    cut = rows_ref.shape[1]
+    chunks = 2 * count // cut
+
+    def fetch(n):
+        source = own_hbm if n * cut < count else other_hbm
+        first = n * cut % count
+        return pltpu.make_async_copy(source.at[pl.ds(first, cut), :], rows_ref.at[n], in_sems.at[n])
+
+    def put(n):
+        cols = pl.ds(n * cut, cut)
+        return pltpu.make_async_copy(slope_ref.at[:, cols], slope_hbm.at[:, cols], out_sems.at[n])
+
+    for n in range(chunks):
+        fetch(n).start()
+    block = units // 2
+    for n in range(chunks):
+        fetch(n).wait()
+        cols = slice(n * cut, (n + 1) * cut)
+        part = jnp.zeros((1, cut), f32)
+        for first in range(0, units, block):
+            here = slice(first, first + block)
+            unit = unit_ref[here, :]
             pre = lax.dot_general(
-                weight,
-                rows_ref[first : first + 256, :],
+                weight_ref[here, :],
+                rows_ref[n],
                 (((1,), (1,)), ((), ())),
                 preferred_element_type=f32,
             )
-            cols = slice(half * count + first, half * count + first + 256)
             square = pre * pre
             tanh = jnp.tanh(pre * (GELU_A + (GELU_A * GELU_B) * square))
             upper = 1.0 + tanh
             acts = ((0.5 * pre) * upper).astype(bf16).astype(f32)
-            part_ref[:, cols] += jnp.sum(acts * unit, axis=0, keepdims=True)
-            slope_ref[:, cols] = half_unit * (
+            part += jnp.sum(acts * unit, axis=0, keepdims=True)
+            slope_ref[here, cols] = (0.5 * unit) * (
                 upper
                 + pre * (1.0 - tanh * tanh) * (GELU_A + (3.0 * GELU_A * GELU_B) * square)
             )
-
-    @pl.when(step == pl.num_programs(0) - 1)
-    def _():
-        row = jnp.concatenate([part_ref[...], code_ref[...]], axis=1)
-        for d in range(message_ref.shape[0]):
-            message_ref[d] = row
+        part_ref[:, cols] = part
+        put(n).start()
+    row = jnp.concatenate([part_ref[...], code_ref[...]], axis=1)
+    for d in range(message_ref.shape[0]):
+        message_ref[d] = row
+    for n in range(chunks):
+        put(n).wait()
 
 
 def score(weight, own, other, unit, code, devices):
     units, width = weight.shape
     count = own.shape[0]
-    block = units // 2
-    whole = lambda i: (0, 0)
+    cut = 256
+    chunks = 2 * count // cut
+    vmem = pl.BlockSpec(memory_space=pltpu.VMEM)
+    hbm = pl.BlockSpec(memory_space=pltpu.HBM)
     return pl.pallas_call(
         score_kernel,
-        grid=(units // block,),
-        in_specs=[
-            pl.BlockSpec((block, width), lambda i: (i, 0)),
-            pl.BlockSpec((count, width), whole),
-            pl.BlockSpec((count, width), whole),
-            pl.BlockSpec((block, 1), lambda i: (i, 0)),
-            pl.BlockSpec((1, count), whole),
-        ],
-        out_specs=[
-            pl.BlockSpec((block, 2 * count), lambda i: (i, 0)),
-            pl.BlockSpec((devices, 1, 3 * count), lambda i: (0, 0, 0)),
-        ],
+        in_specs=[vmem, hbm, hbm, vmem, vmem],
+        out_specs=[hbm, vmem],
         out_shape=[
             pltpu.HBM((units, 2 * count), f32),
             jax.ShapeDtypeStruct((devices, 1, 3 * count), f32),
         ],
-        scratch_shapes=[pltpu.VMEM((1, 2 * count), f32)],
+        scratch_shapes=[
+            pltpu.VMEM((chunks, cut, width), bf16),
+            pltpu.VMEM((units, 2 * count), f32),
+            pltpu.VMEM((1, 2 * count), f32),
+            pltpu.SemaphoreType.DMA((chunks,)),
+            pltpu.SemaphoreType.DMA((chunks,)),
+        ],
         compiler_params=pltpu.CompilerParams(vmem_limit_bytes=40 * MIB),
         cost_estimate=pl.CostEstimate(
             flops=4 * units * width * count,
@@ -92,43 +109,23 @@
             transcendentals=2 * units * count,
         ),
         name="score",
-    )(weight, own, other, unit, code)
-
-
-def term_kernel(slope_ref, lam_ref, own_ref, other_ref, out_ref):
-    count = own_ref.shape[0]
-    out = None
-    for half, rows_ref in enumerate((own_ref, other_ref)):
-        grad_pre = (slope_ref[:, half * count : (half + 1) * count] * lam_ref[half : half + 1, :]).astype(bf16)
-        part = jnp.dot(grad_pre, rows_ref[...], preferred_element_type=f32)
-        out = part if out is None else out + part
-    out_ref[...] = out.astype(bf16)
-
-
-def gradient_term(slope, lam, own, other):
-    units, both = slope.shape
-    count, width = own.shape
+    )(weight, *in_hbm(own, other), unit, code)
+
+
+def term_kernel(
+    place_ref, heard_ref, half_ref, slope_hbm, own_hbm, other_hbm, lam_ref, term_ref,
+    raw_ref, far_ref, own_ref, sum_ref, slope_ref, rows_ref, sems,
+):
+    count = own_hbm.shape[0]
+    units = slope_hbm.shape[0]
     block = units // 2
-    return pl.pallas_call(
-        term_kernel,
-        grid=(units // block,),
-        in_specs=[
-            pl.BlockSpec((block, both), lambda i: (i, 0)),
-            pl.BlockSpec((2, count), lambda i: (0, 0)),
-            pl.BlockSpec((count, width), lambda i: (0, 0)),
-            pl.BlockSpec((count, width), lambda i: (0, 0)),
-        ],
-        out_specs=pl.BlockSpec((block, width), lambda i: (i, 0)),
-        out_shape=jax.ShapeDtypeStruct((units, width), bf16),
-        compiler_params=pltpu.CompilerParams(vmem_limit_bytes=32 * MIB),
-        cost_estimate=pl.CostEstimate(
-            flops=2 * units * width * both, bytes_accessed=12 * MIB, transcendentals=0
-        ),
-        name="gradient_term",
-    )(slope, lam, own, other)
-
-
-def pair_kernel(place_ref, heard_ref, half_ref, lam_ref, raw_ref, far_ref, own_ref, sum_ref):
+    fetches = [
+        pltpu.make_async_copy(own_hbm, rows_ref.at[0], sems.at[0]),
+        pltpu.make_async_copy(other_hbm, rows_ref.at[1], sems.at[1]),
+        pltpu.make_async_copy(slope_hbm, slope_ref, sems.at[2]),
+    ]
+    for fetch in fetches:
+        fetch.start()
     devices, _, size = heard_ref.shape
     width = size // 3
     local = 32
@@ -197,49 +194,80 @@
         south = place_ref[1] == 0
         lam_ref[0:1, cols] = jnp.where(south, lam[0], lam[1])
         lam_ref[1:2, cols] = jnp.where(south, lam[1], lam[0])
-
-
-def pair_lambdas(heard, half, place):
+    for fetch in fetches:
+        fetch.wait()
+    for first in range(0, units, block):
+        here = slice(first, first + block)
+        term = None
+        for k in range(2):
+            slope = slope_ref[here, k * count : (k + 1) * count]
+            grad_pre = (slope * lam_ref[k : k + 1, :]).astype(bf16)
+            part = jnp.dot(grad_pre, rows_ref[k], preferred_element_type=f32)
+            term = part if term is None else term + part
+        term_ref[here, :] = term.astype(bf16)
+
+
+def gradient_term(heard, half, place, slope, own, other):
     devices, _, size = heard.shape
-    width = size // 3
-    return pl.pallas_call(
-        pair_kernel,
-        in_specs=[
-            pl.BlockSpec(memory_space=pltpu.SMEM),
-            pl.BlockSpec(memory_space=pltpu.VMEM),
-            pl.BlockSpec(memory_space=pltpu.VMEM),
-        ],
-        out_specs=pl.BlockSpec(memory_space=pltpu.VMEM),
-        out_shape=jax.ShapeDtypeStruct((2, width), f32),
+    units = slope.shape[0]
+    count, width = own.shape
+    pairs = 64 * (count // LANES)
+    vmem = pl.BlockSpec(memory_space=pltpu.VMEM)
+    hbm = pl.BlockSpec(memory_space=pltpu.HBM)
+    return pl.pallas_call(
+        term_kernel,
+        in_specs=[pl.BlockSpec(memory_space=pltpu.SMEM), vmem, vmem, hbm, hbm, hbm],
+        out_specs=[vmem, vmem],
+        out_shape=[
+            jax.ShapeDtypeStruct((2, count), f32),
+            jax.ShapeDtypeStruct((units, width), bf16),
+        ],
         scratch_shapes=[
             pltpu.VMEM((devices, size), f32),
-            pltpu.VMEM((3, devices, width), f32),
-            pltpu.VMEM((width // LANES * 6 * 32, LANES), f32),
-            pltpu.VMEM((width // LANES * 2 * 32, LANES), f32),
-        ],
-        compiler_params=pltpu.CompilerParams(vmem_limit_bytes=16 * MIB),
-        cost_estimate=pl.CostEstimate(flops=2 * MIB * 10, bytes_accessed=MIB, transcendentals=2 * MIB),
-        name="pair_lambdas",
-    )(place, heard, half)
-
-
-def copies_kernel(block_ref, out_ref):
-    for k in range(out_ref.shape[0]):
-        out_ref[k] = block_ref[...]
+            pltpu.VMEM((3, devices, count), f32),
+            pltpu.VMEM((3 * pairs, LANES), f32),
+            pltpu.VMEM((pairs, LANES), f32),
+            pltpu.VMEM(slope.shape, f32),
+            pltpu.VMEM((2, count, width), bf16),
+            pltpu.SemaphoreType.DMA((3,)),
+        ],
+        compiler_params=pltpu.CompilerParams(vmem_limit_bytes=40 * MIB),
+        cost_estimate=pl.CostEstimate(
+            flops=4 * units * width * count, bytes_accessed=12 * MIB, transcendentals=2 * MIB
+        ),
+        name="gradient_term",
+    )(place, heard, half, *in_hbm(slope, own, other))
+
+
+def copies_kernel(block_hbm, out_hbm, block_ref, in_sem, out_sems):
+    fetch = pltpu.make_async_copy(block_hbm, block_ref, in_sem)
+    fetch.start()
+    fetch.wait()
+    puts = [
+        pltpu.make_async_copy(block_ref, out_hbm.at[k], out_sems.at[k])
+        for k in range(out_hbm.shape[0])
+    ]
+    for put in puts:
+        put.start()
+    for put in puts:
+        put.wait()
 
 
 def copies(block, count):
-    rows, width = block.shape
-    step = count // 4
+    hbm = pl.BlockSpec(memory_space=pltpu.HBM)
     return pl.pallas_call(
         copies_kernel,
-        grid=(count // step,),
-        in_specs=[pl.BlockSpec((rows, width), lambda i: (0, 0))],
-        out_specs=pl.BlockSpec((step, rows, width), lambda i: (i, 0, 0)),
-        out_shape=jax.ShapeDtypeStruct((count, rows, width), block.dtype),
+        in_specs=[hbm],
+        out_specs=hbm,
+        out_shape=pltpu.HBM((count, *block.shape), block.dtype),
+        scratch_shapes=[
+            pltpu.VMEM(block.shape, block.dtype),
+            pltpu.SemaphoreType.DMA,
+            pltpu.SemaphoreType.DMA((count,)),
+        ],
         compiler_params=pltpu.CompilerParams(vmem_limit_bytes=16 * MIB),
         name="copies",
-    )(block)
+    )(*in_hbm(block))
 
 
 def squares_kernel(total_ref, out_ref):
@@ -307,10 +335,8 @@
 
     slope, message = score(weight, own, other, unit, code, chips * cores)
     heard = lax.all_to_all(message, CAND, split_axis=0, concat_axis=0, tiled=True)
-    lam = pair_lambdas(heard, half, place)
+    lam, term = gradient_term(heard, half, place, slope, own, other)
     lambdas = lam[0].reshape(groups, local)
-
-    term = gradient_term(slope, lam, own, other)
     terms = lax.all_to_all(
         term.reshape(chips, owned_rows, width), CHIPS, split_axis=0, concat_axis=0, tiled=True
     )

time: 172 us -> 167 us (0.971)
  local copies, waits for them, and re-layouts: 6.58 us -> 1.5 us
    unnamed x16 -> x8, local copies, waits for them, and re-layouts: 5.1 us -> 0.02 us
    pallas_call x4 -> x3, Pallas kernels: 21.3 us -> 21.1 us  [the longest x1 10.9 us: score(): pl.pallas_call(score_kernel, in_specs=[vmem, hbm, hbm, vmem, vmem], out_s...]
where the time goes in v5:
time: 167 us; the launch traced here: 166 us
  blocking collectives  76 us (46%)
  waiting for transfers between devices  34.9 us (21%)
  starting transfers between devices  29.9 us (18%)
  Pallas kernels  22.6 us (14%)
    all_to_all x1, blocking collectives, per_device(): lax.all_to_all(term.reshape(chips, owned_rows, width), CHIPS, split_axis=...  30.6 us
    all_to_all x1, blocking collectives, per_device(): lax.all_to_all(owned.reshape(planes, 8, width // across), 'z', split_axis...  28.4 us
    all_to_all x1, blocking collectives, spread(): return lax.all_to_all(copies, axis, split_axis=0, concat_axis=0, tiled=True)  17.1 us
    all_to_all x1, waiting for transfers between devices, per_device(): lax.all_to_all(copies(hidden_weight, chips), CHIPS, split_axis=0, concat_...  17 us
    pallas_call x1, Pallas kernels, score(): pl.pallas_call(score_kernel, in_specs=[vmem, hbm, hbm, vmem, vmem], out_s...  10.9 us
    all_to_all x1, starting transfers between devices, per_device(): lax.all_to_all(message, CAND, split_axis=0, concat_axis=0, tiled=True)  9.3 us
    all_to_all x1, waiting for transfers between devices, per_device(): lax.all_to_all(message, CAND, split_axis=0, concat_axis=0, tiled=True)  9.05 us
    all_to_all x1, starting transfers between devices, per_device(): lax.all_to_all(squares(total, chips * cores), CAND, split_axis=0, concat_...  8.03 us
  transfers between devices with their start and end apart: 4, of which 4 were waited for; matrix products, arithmetic and copies ran while one was open for 1% of the time, Pallas kernels for 0%

profile of v5, /device:TPU:1, one launch (start us, length us, event | category | flops | bytes accessed | tf_op | source)
XLA Modules:
  0.0 166.3 jit_solution(3557243504426961473)
XLA Ops:
  0.6 2.4 %copies.1 = bf16[16,64,1024]{2,1,0:T(8,128)(2,1)} custom-call(bf16[64,1024]{1,0:T(8,128)(2,1)} %block_hbm.1), custom_call_target="tpu_custom_call" | custom-call | tf_op jit(solution)/shard_map/copies/pallas_call | solution.py:258
  3.0 0.0 copy-start.2
  3.0 0.0 copy-start
  3.1 0.0 copy-start.1
  3.1 7.7 %all-to-all-start = ((bf16[16,64,1024]{2,1,0:T(8,128)(2,1)}), bf16[16,64,1024]{2,1,0:T(8,128)(2,1)S(1)}, u32[]{:S(2)}, u32[]{:S(2)}) async-start(bf16[16,64,1024]{2,1,0:T(8,128)(2,1)} %copies.1), calls=%async_computation | async-start | bytes 4194304 | tf_op jit(solution)/shard_map/all_to_all | solution.py:325
  10.8 4.9 %collective-permute-start = (bf16[768,1024]{1,0:T(8,128)(2,1)}, bf16[768,1024]{1,0:T(8,128)(2,1)}, u32[]{:S(2)}, u32[]{:S(2)}) collective-permute-start(bf16[768,1024]{1,0:T(8,128)(2,1)} %bitcast.13), channel_id=1, source_target_pairs={{0,1},{1,0},{2,3},{3,2},{4,5},{5,4},{6,7},{7,6},{8,9},{9,8},{10,11... | collective-permute-start | bytes 4718600 | tf_op jit(solution)/shard_map/ppermute | solution.py:328
  15.7 0.0 copy-done.2
  15.7 0.1 reshape.44
  15.8 0.5 reshape.50.unit_ref
  16.3 0.0 copy-done
  16.3 0.0 copy-done.1
  16.3 0.1 reshape.45.code_ref
  16.4 2.6 %collective-permute-done.other_hbm = bf16[768,1024]{1,0:T(8,128)(2,1)} collective-permute-done((bf16[768,1024]{1,0:T(8,128)(2,1)}, bf16[768,1024]{1,0:T(8,128)(2,1)}, u32[]{:S(2)}, u32[]{:S(2)}) %collective-permute-start) | collective-permute-done | bytes 1572896 | tf_op jit(solution)/shard_map/ppermute | solution.py:328
  19.1 17.0 %all-to-all-done = bf16[16,64,1024]{2,1,0:T(8,128)(2,1)S(1)} async-done(((bf16[16,64,1024]{2,1,0:T(8,128)(2,1)}), bf16[16,64,1024]{2,1,0:T(8,128)(2,1)S(1)}, u32[]{:S(2)}, u32[]{:S(2)}) %all-to-all-start) | async-done | bytes 2097184 | tf_op jit(solution)/shard_map/all_to_all | solution.py:325
  36.1 0.0 copy-start.3
  36.1 10.9 %score.1 = (f32[1024,1536]{1,0:T(8,128)}, f32[32,1,2304]{2,1,0:T(1,128)}) custom-call(bf16[1024,1024]{1,0:T(8,128)(2,1)S(1)} %bitcast.10, bf16[768,1024]{1,0:T(8,128)(2,1)} %bitcast.14, bf16[768,1024]{1,0:T(8,128)(2,1)} %collective-permute-done.other_hbm, f32[1024,1]{1,0:T(8,128)S(1)} %reshape.50.unit_ref, f32[1,768]{1,0:T(1,128)S(1)} %reshape.45.code_ref), custom_call_target="tpu_custom_call" | custom-call | flops 3221225472 | bytes 12582912 | tf_op jit(solution)/shard_map/score/pallas_call | solution.py:90
  47.0 9.3 %all-to-all-start.1 = ((f32[32,1,2304]{2,1,0:T(1,128)}), f32[32,1,2304]{2,1,0:T(1,128)S(1)}, u32[]{:S(2)}, u32[]{:S(2)}) async-start(f32[32,1,2304]{2,1,0:T(1,128)} %get-tuple-element.6), calls=%async_computation.1 | async-start | bytes 589824 | tf_op jit(solution)/shard_map/all_to_all | solution.py:337
  56.3 0.0 copy-done.3
  56.3 0.1 broadcast_in_dim.4
  56.4 0.1 reshape_reshape.3.half_ref
  56.4 0.1 pad_add_fusion.place_ref
  56.5 9.0 %all-to-all-done.1.heard_ref = f32[32,1,2304]{2,1,0:T(1,128)S(1)} async-done(((f32[32,1,2304]{2,1,0:T(1,128)}), f32[32,1,2304]{2,1,0:T(1,128)S(1)}, u32[]{:S(2)}, u32[]{:S(2)}) %all-to-all-start.1) | async-done | bytes 294944 | tf_op jit(solution)/shard_map/all_to_all | solution.py:337
  65.6 7.9 %gradient_term.1 = (f32[2,768]{1,0:T(2,128)S(1)}, bf16[1024,1024]{1,0:T(8,128)(2,1)S(1)}) custom-call(s32[2]{0:T(128)S(1)} %pad_add_fusion.place_ref, f32[32,1,2304]{2,1,0:T(1,128)S(1)} %all-to-all-done.1.heard_ref, f32[1,768]{1,0:T(1,128)S(1)} %reshape_reshape.3.half_ref, f32[1024,1536]{1,0:T(8,128)} %get-tuple-element.7.slope_hbm, ...), custom_call_target="tpu_custom_call" | custom-call | flops 3221225472 | bytes 12582912 | tf_op jit(solution)/shard_map/gradient_term/pallas_call | solution.py:217
  73.5 30.6 %all_to_all.30 = bf16[16,64,1024]{2,1,0:T(8,128)(2,1)S(1)} all-to-all(bf16[16,64,1024]{2,1,0:T(8,128)(2,1)S(1)} %bitcast.11), channel_id=1, replica_groups=mesh['z'=16,'y'=4,'x'=4,'c'=2] {'y','x'}, dimensions={0} | all-to-all | bytes 4194304 | tf_op jit(solution)/shard_map/all_to_all | solution.py:340
  104.0 0.4 reduce_sum.24
  104.4 28.4 %all_to_all.31 = bf16[16,8,512]{2,1,0:T(8,128)(2,1)S(1)} all-to-all(bf16[16,8,512]{2,1,0:T(8,128)(2,1)S(1)} %bitcast.12), channel_id=1, replica_groups=mesh['z'=16,'y'=4,'x'=4,'c'=2] {'z'}, dimensions={0} | all-to-all | bytes 262144 | tf_op jit(solution)/shard_map/all_to_all | solution.py:346
  132.8 17.1 %all_to_all.32.total_ref = bf16[16,8,512]{2,1,0:T(8,128)(2,1)S(1)} all-to-all(bf16[16,8,512]{2,1,0:T(8,128)(2,1)S(1)} %broadcast_in_dim.10), channel_id=1, replica_groups=mesh['z'=16,'y'=4,'x'=4,'c'=2] {'z'}, dimensions={0} | all-to-all | bytes 262144 | tf_op jit(solution)/shard_map/all_to_all | solution.py:28
  149.9 0.7 squares.1
  150.6 8.0 %all-to-all-start.5 = ((f32[32,1,128]{2,1,0:T(1,128)}), f32[32,1,128]{2,1,0:T(1,128)S(1)}, u32[]{:S(2)}, u32[]{:S(2)}) async-start(f32[32,1,128]{2,1,0:T(1,128)} %squares.1), calls=%async_computation.5 | async-start | bytes 32768 | tf_op jit(solution)/shard_map/all_to_all | solution.py:352
  158.7 0.7 reshape_squeeze.3
  159.4 6.2 %all-to-all-done.5.heard_ref = f32[32,1,128]{2,1,0:T(1,128)S(1)} async-done(((f32[32,1,128]{2,1,0:T(1,128)}), f32[32,1,128]{2,1,0:T(1,128)S(1)}, u32[]{:S(2)}, u32[]{:S(2)}) %all-to-all-start.5) | async-done | bytes 16416 | tf_op jit(solution)/shard_map/all_to_all | solution.py:352
  165.6 0.8 scaled.1
  (6 shorter events, 0.1 us)
Async XLA Ops:
  3.0 12.7 %copy-start.2 = (bf16[2048]{0:T(1024)(128)(2,1)S(1)}, bf16[2048]{0:T(1024)(128)(2,1)}, u32[]{:S(2)}) copy-start(bf16[2048]{0:T(1024)(128)(2,1)} %param.8) | copy-start | bytes 12292
  3.0 13.3 %copy-start = (s32[24,32]{1,0:T(8,128)S(1)}, s32[24,32]{1,0:T(8,128)}, u32[]{:S(2)}) copy-start(s32[24,32]{1,0:T(8,128)} %param.9) | copy-start | bytes 9220
  3.1 13.3 %copy-start.1 = (s32[24,32]{1,0:T(8,128)S(1)}, s32[24,32]{1,0:T(8,128)}, u32[]{:S(2)}) copy-start(s32[24,32]{1,0:T(8,128)} %param.10) | copy-start | bytes 9220
  3.1 33.0 %all-to-all-start = ((bf16[16,64,1024]{2,1,0:T(8,128)(2,1)}), bf16[16,64,1024]{2,1,0:T(8,128)(2,1)S(1)}, u32[]{:S(2)}, u32[]{:S(2)}) async-start(bf16[16,64,1024]{2,1,0:T(8,128)(2,1)} %copies.1), calls=%async_computation | async-start | bytes 4194304 | tf_op jit(solution)/shard_map/all_to_all | solution.py:325
  10.8 8.3 %collective-permute-start = (bf16[768,1024]{1,0:T(8,128)(2,1)}, bf16[768,1024]{1,0:T(8,128)(2,1)}, u32[]{:S(2)}, u32[]{:S(2)}) collective-permute-start(bf16[768,1024]{1,0:T(8,128)(2,1)} %bitcast.13), channel_id=1, source_target_pairs={{0,1},{1,0},{2,3},{3,2},{4,5},{5,4},{6,7},{7,6},{8,9},{9,8},{10,11... | collective-permute-start | bytes 4718600 | tf_op jit(solution)/shard_map/ppermute | solution.py:328
  36.1 20.2 %copy-start.3 = (f32[24]{0:T(128)S(1)}, f32[24]{0:T(128)}, u32[]{:S(2)}) copy-start(f32[24]{0:T(128)} %param.11) | copy-start | bytes 292
  47.0 18.6 %all-to-all-start.1 = ((f32[32,1,2304]{2,1,0:T(1,128)}), f32[32,1,2304]{2,1,0:T(1,128)S(1)}, u32[]{:S(2)}, u32[]{:S(2)}) async-start(f32[32,1,2304]{2,1,0:T(1,128)} %get-tuple-element.6), calls=%async_computation.1 | async-start | bytes 589824 | tf_op jit(solution)/shard_map/all_to_all | solution.py:337
  150.6 14.9 %all-to-all-start.5 = ((f32[32,1,128]{2,1,0:T(1,128)}), f32[32,1,128]{2,1,0:T(1,128)S(1)}, u32[]{:S(2)}, u32[]{:S(2)}) async-start(f32[32,1,128]{2,1,0:T(1,128)} %squares.1), calls=%async_computation.5 | async-start | bytes 32768 | tf_op jit(solution)/shard_map/all_to_all | solution.py:352

commit v6 on v5

--- a/solution.py
+++ b/solution.py
@@ -48,31 +48,40 @@
 
     for n in range(chunks):
         fetch(n).start()
-    block = units // 2
-    for n in range(chunks):
-        fetch(n).wait()
+    block = 512
+    tiles = [(n, first) for n in range(chunks) for first in range(0, units, block)]
+
+    def product(n, first):
+        if first == 0:
+            fetch(n).wait()
+        return lax.dot_general(
+            weight_ref[first : first + block, :],
+            rows_ref[n],
+            (((1,), (1,)), ((), ())),
+            preferred_element_type=f32,
+        )
+
+    ahead = product(*tiles[0])
+    for at, (n, first) in enumerate(tiles):
+        pre = ahead
+        if at + 1 < len(tiles):
+            ahead = product(*tiles[at + 1])
+        here = slice(first, first + block)
         cols = slice(n * cut, (n + 1) * cut)
-        part = jnp.zeros((1, cut), f32)
-        for first in range(0, units, block):
-            here = slice(first, first + block)
-            unit = unit_ref[here, :]
-            pre = lax.dot_general(
-                weight_ref[here, :],
-                rows_ref[n],
-                (((1,), (1,)), ((), ())),
-                preferred_element_type=f32,
-            )
-            square = pre * pre
-            tanh = jnp.tanh(pre * (GELU_A + (GELU_A * GELU_B) * square))
-            upper = 1.0 + tanh
-            acts = ((0.5 * pre) * upper).astype(bf16).astype(f32)
-            part += jnp.sum(acts * unit, axis=0, keepdims=True)
-            slope_ref[here, cols] = (0.5 * unit) * (
-                upper
-                + pre * (1.0 - tanh * tanh) * (GELU_A + (3.0 * GELU_A * GELU_B) * square)
-            )
-        part_ref[:, cols] = part
-        put(n).start()
+        half_unit = 0.5 * unit_ref[here, :]
+        line = GELU_A * pre
+        cube = (GELU_B * (pre * pre)) * line
+        inner = line + cube
+        tanh = jnp.tanh(inner)
+        upper = 1.0 + tanh
+        acts = (pre * upper).astype(bf16).astype(f32)
+        part = jnp.sum(acts * half_unit, axis=0, keepdims=True)
+        part_ref[:, cols] = part if first == 0 else part_ref[:, cols] + part
+        slope_ref[here, cols] = half_unit * (
+            upper + (1.0 - tanh * tanh) * (inner + (cube + cube))
+        )
+        if first + block == units:
+            put(n).start()
     row = jnp.concatenate([part_ref[...], code_ref[...]], axis=1)
     for d in range(message_ref.shape[0]):
         message_ref[d] = row

time: 167 us -> 166 us (level)
  no operation moved by 1% of the time
where the time goes in v6:
time: 166 us
  blocking collectives  76 us (46%)
  waiting for transfers between devices  34.9 us (21%)
  starting transfers between devices  30 us (18%)
  Pallas kernels  21.8 us (13%)
    all_to_all x1, blocking collectives, per_device(): lax.all_to_all(term.reshape(chips, owned_rows, width), CHIPS, split_axis=...  30.6 us
    all_to_all x1, blocking collectives, per_device(): lax.all_to_all(owned.reshape(planes, 8, width // across), 'z', split_axis...  28.3 us
    all_to_all x1, blocking collectives, spread(): return lax.all_to_all(copies, axis, split_axis=0, concat_axis=0, tiled=True)  17.1 us
    all_to_all x1, waiting for transfers between devices, per_device(): lax.all_to_all(copies(hidden_weight, chips), CHIPS, split_axis=0, concat_...  17 us
    pallas_call x1, Pallas kernels, score(): pl.pallas_call(score_kernel, in_specs=[vmem, hbm, hbm, vmem, vmem], out_s...  10.1 us
    all_to_all x1, starting transfers between devices, per_device(): lax.all_to_all(message, CAND, split_axis=0, concat_axis=0, tiled=True)  9.32 us
    all_to_all x1, waiting for transfers between devices, per_device(): lax.all_to_all(message, CAND, split_axis=0, concat_axis=0, tiled=True)  9.05 us
    all_to_all x1, starting transfers between devices, per_device(): lax.all_to_all(squares(total, chips * cores), CAND, split_axis=0, concat_...  8.03 us
  transfers between devices with their start and end apart: 4, of which 4 were waited for; matrix products, arithmetic and copies ran while one was open for 1% of the time, Pallas kernels for 0%

profile of v6, /device:TPU:1, one launch (start us, length us, event | category | flops | bytes accessed | tf_op | source)
XLA Modules:
  0.0 165.5 jit_solution(15383232268960828742)
XLA Ops:
  0.6 2.4 %copies.1 = bf16[16,64,1024]{2,1,0:T(8,128)(2,1)} custom-call(bf16[64,1024]{1,0:T(8,128)(2,1)} %block_hbm.1), custom_call_target="tpu_custom_call" | custom-call | tf_op jit(solution)/shard_map/copies/pallas_call | solution.py:267
  3.0 0.0 copy-start.2
  3.0 0.0 copy-start
  3.1 0.0 copy-start.1
  3.1 7.7 %all-to-all-start = ((bf16[16,64,1024]{2,1,0:T(8,128)(2,1)}), bf16[16,64,1024]{2,1,0:T(8,128)(2,1)S(1)}, u32[]{:S(2)}, u32[]{:S(2)}) async-start(bf16[16,64,1024]{2,1,0:T(8,128)(2,1)} %copies.1), calls=%async_computation | async-start | bytes 4194304 | tf_op jit(solution)/shard_map/all_to_all | solution.py:334
  10.8 4.9 %collective-permute-start = (bf16[768,1024]{1,0:T(8,128)(2,1)}, bf16[768,1024]{1,0:T(8,128)(2,1)}, u32[]{:S(2)}, u32[]{:S(2)}) collective-permute-start(bf16[768,1024]{1,0:T(8,128)(2,1)} %bitcast.13), channel_id=1, source_target_pairs={{0,1},{1,0},{2,3},{3,2},{4,5},{5,4},{6,7},{7,6},{8,9},{9,8},{10,11... | collective-permute-start | bytes 4718600 | tf_op jit(solution)/shard_map/ppermute | solution.py:337
  15.7 0.0 copy-done.2
  15.7 0.1 reshape.44
  15.8 0.5 reshape.50.unit_ref
  16.3 0.0 copy-done
  16.3 0.0 copy-done.1
  16.3 0.1 reshape.45.code_ref
  16.4 2.6 %collective-permute-done.other_hbm = bf16[768,1024]{1,0:T(8,128)(2,1)} collective-permute-done((bf16[768,1024]{1,0:T(8,128)(2,1)}, bf16[768,1024]{1,0:T(8,128)(2,1)}, u32[]{:S(2)}, u32[]{:S(2)}) %collective-permute-start) | collective-permute-done | bytes 1572896 | tf_op jit(solution)/shard_map/ppermute | solution.py:337
  19.1 17.0 %all-to-all-done = bf16[16,64,1024]{2,1,0:T(8,128)(2,1)S(1)} async-done(((bf16[16,64,1024]{2,1,0:T(8,128)(2,1)}), bf16[16,64,1024]{2,1,0:T(8,128)(2,1)S(1)}, u32[]{:S(2)}, u32[]{:S(2)}) %all-to-all-start) | async-done | bytes 2097184 | tf_op jit(solution)/shard_map/all_to_all | solution.py:334
  36.1 0.0 copy-start.3
  36.1 10.1 %score.1 = (f32[1024,1536]{1,0:T(8,128)}, f32[32,1,2304]{2,1,0:T(1,128)}) custom-call(bf16[1024,1024]{1,0:T(8,128)(2,1)S(1)} %bitcast.10, bf16[768,1024]{1,0:T(8,128)(2,1)} %bitcast.14, bf16[768,1024]{1,0:T(8,128)(2,1)} %collective-permute-done.other_hbm, f32[1024,1]{1,0:T(8,128)S(1)} %reshape.50.unit_ref, f32[1,768]{1,0:T(1,128)S(1)} %reshape.45.code_ref), custom_call_target="tpu_custom_call" | custom-call | flops 3221225472 | bytes 12582912 | tf_op jit(solution)/shard_map/score/pallas_call | solution.py:99
  46.1 9.3 %all-to-all-start.1 = ((f32[32,1,2304]{2,1,0:T(1,128)}), f32[32,1,2304]{2,1,0:T(1,128)S(1)}, u32[]{:S(2)}, u32[]{:S(2)}) async-start(f32[32,1,2304]{2,1,0:T(1,128)} %get-tuple-element.6), calls=%async_computation.1 | async-start | bytes 589824 | tf_op jit(solution)/shard_map/all_to_all | solution.py:346
  55.5 0.0 copy-done.3
  55.5 0.1 broadcast_in_dim.4
  55.6 0.1 reshape_reshape.3.half_ref
  55.7 0.1 pad_add_fusion.place_ref
  55.7 9.1 %all-to-all-done.1.heard_ref = f32[32,1,2304]{2,1,0:T(1,128)S(1)} async-done(((f32[32,1,2304]{2,1,0:T(1,128)}), f32[32,1,2304]{2,1,0:T(1,128)S(1)}, u32[]{:S(2)}, u32[]{:S(2)}) %all-to-all-start.1) | async-done | bytes 294944 | tf_op jit(solution)/shard_map/all_to_all | solution.py:346
  64.8 7.9 %gradient_term.1 = (f32[2,768]{1,0:T(2,128)S(1)}, bf16[1024,1024]{1,0:T(8,128)(2,1)S(1)}) custom-call(s32[2]{0:T(128)S(1)} %pad_add_fusion.place_ref, f32[32,1,2304]{2,1,0:T(1,128)S(1)} %all-to-all-done.1.heard_ref, f32[1,768]{1,0:T(1,128)S(1)} %reshape_reshape.3.half_ref, f32[1024,1536]{1,0:T(8,128)} %get-tuple-element.7.slope_hbm, ...), custom_call_target="tpu_custom_call" | custom-call | flops 3221225472 | bytes 12582912 | tf_op jit(solution)/shard_map/gradient_term/pallas_call | solution.py:226
  72.7 30.6 %all_to_all.30 = bf16[16,64,1024]{2,1,0:T(8,128)(2,1)S(1)} all-to-all(bf16[16,64,1024]{2,1,0:T(8,128)(2,1)S(1)} %bitcast.11), channel_id=1, replica_groups=mesh['z'=16,'y'=4,'x'=4,'c'=2] {'y','x'}, dimensions={0} | all-to-all | bytes 4194304 | tf_op jit(solution)/shard_map/all_to_all | solution.py:349
  103.2 0.4 reduce_sum.24
  103.6 28.3 %all_to_all.31 = bf16[16,8,512]{2,1,0:T(8,128)(2,1)S(1)} all-to-all(bf16[16,8,512]{2,1,0:T(8,128)(2,1)S(1)} %bitcast.12), channel_id=1, replica_groups=mesh['z'=16,'y'=4,'x'=4,'c'=2] {'z'}, dimensions={0} | all-to-all | bytes 262144 | tf_op jit(solution)/shard_map/all_to_all | solution.py:355
  132.0 17.1 %all_to_all.32.total_ref = bf16[16,8,512]{2,1,0:T(8,128)(2,1)S(1)} all-to-all(bf16[16,8,512]{2,1,0:T(8,128)(2,1)S(1)} %broadcast_in_dim.10), channel_id=1, replica_groups=mesh['z'=16,'y'=4,'x'=4,'c'=2] {'z'}, dimensions={0} | all-to-all | bytes 262144 | tf_op jit(solution)/shard_map/all_to_all | solution.py:28
  149.1 0.7 squares.1
  149.8 8.0 %all-to-all-start.5 = ((f32[32,1,128]{2,1,0:T(1,128)}), f32[32,1,128]{2,1,0:T(1,128)S(1)}, u32[]{:S(2)}, u32[]{:S(2)}) async-start(f32[32,1,128]{2,1,0:T(1,128)} %squares.1), calls=%async_computation.5 | async-start | bytes 32768 | tf_op jit(solution)/shard_map/all_to_all | solution.py:361
  157.9 0.7 reshape_squeeze.3
  158.5 6.2 %all-to-all-done.5.heard_ref = f32[32,1,128]{2,1,0:T(1,128)S(1)} async-done(((f32[32,1,128]{2,1,0:T(1,128)}), f32[32,1,128]{2,1,0:T(1,128)S(1)}, u32[]{:S(2)}, u32[]{:S(2)}) %all-to-all-start.5) | async-done | bytes 16416 | tf_op jit(solution)/shard_map/all_to_all | solution.py:361
  164.7 0.8 scaled.1
  (6 shorter events, 0.1 us)
Async XLA Ops:
  3.0 12.7 %copy-start.2 = (bf16[2048]{0:T(1024)(128)(2,1)S(1)}, bf16[2048]{0:T(1024)(128)(2,1)}, u32[]{:S(2)}) copy-start(bf16[2048]{0:T(1024)(128)(2,1)} %param.8) | copy-start | bytes 12292
  3.0 13.3 %copy-start = (s32[24,32]{1,0:T(8,128)S(1)}, s32[24,32]{1,0:T(8,128)}, u32[]{:S(2)}) copy-start(s32[24,32]{1,0:T(8,128)} %param.9) | copy-start | bytes 9220
  3.1 13.3 %copy-start.1 = (s32[24,32]{1,0:T(8,128)S(1)}, s32[24,32]{1,0:T(8,128)}, u32[]{:S(2)}) copy-start(s32[24,32]{1,0:T(8,128)} %param.10) | copy-start | bytes 9220
  3.1 33.0 %all-to-all-start = ((bf16[16,64,1024]{2,1,0:T(8,128)(2,1)}), bf16[16,64,1024]{2,1,0:T(8,128)(2,1)S(1)}, u32[]{:S(2)}, u32[]{:S(2)}) async-start(bf16[16,64,1024]{2,1,0:T(8,128)(2,1)} %copies.1), calls=%async_computation | async-start | bytes 4194304 | tf_op jit(solution)/shard_map/all_to_all | solution.py:334
  10.8 8.3 %collective-permute-start = (bf16[768,1024]{1,0:T(8,128)(2,1)}, bf16[768,1024]{1,0:T(8,128)(2,1)}, u32[]{:S(2)}, u32[]{:S(2)}) collective-permute-start(bf16[768,1024]{1,0:T(8,128)(2,1)} %bitcast.13), channel_id=1, source_target_pairs={{0,1},{1,0},{2,3},{3,2},{4,5},{5,4},{6,7},{7,6},{8,9},{9,8},{10,11... | collective-permute-start | bytes 4718600 | tf_op jit(solution)/shard_map/ppermute | solution.py:337
  36.1 19.4 %copy-start.3 = (f32[24]{0:T(128)S(1)}, f32[24]{0:T(128)}, u32[]{:S(2)}) copy-start(f32[24]{0:T(128)} %param.11) | copy-start | bytes 292
  46.1 18.6 %all-to-all-start.1 = ((f32[32,1,2304]{2,1,0:T(1,128)}), f32[32,1,2304]{2,1,0:T(1,128)S(1)}, u32[]{:S(2)}, u32[]{:S(2)}) async-start(f32[32,1,2304]{2,1,0:T(1,128)} %get-tuple-element.6), calls=%async_computation.1 | async-start | bytes 589824 | tf_op jit(solution)/shard_map/all_to_all | solution.py:346
  149.8 14.9 %all-to-all-start.5 = ((f32[32,1,128]{2,1,0:T(1,128)}), f32[32,1,128]{2,1,0:T(1,128)S(1)}, u32[]{:S(2)}, u32[]{:S(2)}) async-start(f32[32,1,128]{2,1,0:T(1,128)} %squares.1), calls=%async_computation.5 | async-start | bytes 32768 | tf_op jit(solution)/shard_map/all_to_all | solution.py:361

commit v7 on v6

--- a/solution.py
+++ b/solution.py
@@ -29,8 +29,8 @@
 
 
 def score_kernel(
-    weight_ref, own_hbm, other_hbm, unit_ref, code_ref, slope_hbm, message_ref,
-    rows_ref, slope_ref, part_ref, in_sems, out_sems,
+    weight_ref, own_hbm, other_hbm, unit_ref, code_ref, slope_hbm, message_hbm,
+    rows_ref, slope_ref, part_ref, message_ref, in_sems, out_sems,
 ):
     count = own_hbm.shape[0]
     units = weight_ref.shape[0]
@@ -85,8 +85,11 @@
     row = jnp.concatenate([part_ref[...], code_ref[...]], axis=1)
     for d in range(message_ref.shape[0]):
         message_ref[d] = row
+    send = pltpu.make_async_copy(message_ref, message_hbm, out_sems.at[chunks])
+    send.start()
     for n in range(chunks):
         put(n).wait()
+    send.wait()
 
 
 def score(weight, own, other, unit, code, devices):
@@ -99,17 +102,18 @@
     return pl.pallas_call(
         score_kernel,
         in_specs=[vmem, hbm, hbm, vmem, vmem],
-        out_specs=[hbm, vmem],
+        out_specs=[hbm, hbm],
         out_shape=[
             pltpu.HBM((units, 2 * count), f32),
-            jax.ShapeDtypeStruct((devices, 1, 3 * count), f32),
+            pltpu.HBM((devices, 1, 3 * count), f32),
         ],
         scratch_shapes=[
             pltpu.VMEM((chunks, cut, width), bf16),
             pltpu.VMEM((units, 2 * count), f32),
             pltpu.VMEM((1, 2 * count), f32),
+            pltpu.VMEM((devices, 1, 3 * count), f32),
             pltpu.SemaphoreType.DMA((chunks,)),
-            pltpu.SemaphoreType.DMA((chunks,)),
+            pltpu.SemaphoreType.DMA((chunks + 1,)),
         ],
         compiler_params=pltpu.CompilerParams(vmem_limit_bytes=40 * MIB),
         cost_estimate=pl.CostEstimate(
@@ -248,16 +252,25 @@
     )(place, heard, half, *in_hbm(slope, own, other))
 
 
-def copies_kernel(block_hbm, out_hbm, block_ref, in_sem, out_sems):
-    fetch = pltpu.make_async_copy(block_hbm, block_ref, in_sem)
-    fetch.start()
-    fetch.wait()
-    puts = [
-        pltpu.make_async_copy(block_ref, out_hbm.at[k], out_sems.at[k])
-        for k in range(out_hbm.shape[0])
+def copies_kernel(block_hbm, out_hbm, block_ref, in_sems, out_sems):
+    count, parts = out_hbm.shape[0], in_sems.shape[0]
+    size = block_hbm.shape[0] // parts
+    cuts = [pl.ds(n * size, size) for n in range(parts)]
+    fetches = [
+        pltpu.make_async_copy(block_hbm.at[cut, :], block_ref.at[cut, :], in_sems.at[n])
+        for n, cut in enumerate(cuts)
     ]
-    for put in puts:
-        put.start()
+    for fetch in fetches:
+        fetch.start()
+    puts = []
+    for n, cut in enumerate(cuts):
+        fetches[n].wait()
+        for k in range(count):
+            put = pltpu.make_async_copy(
+                block_ref.at[cut, :], out_hbm.at[k, cut, :], out_sems.at[n * count + k]
+            )
+            put.start()
+            puts.append(put)
     for put in puts:
         put.wait()
 
@@ -271,8 +284,8 @@
         out_shape=pltpu.HBM((count, *block.shape), block.dtype),
         scratch_shapes=[
             pltpu.VMEM(block.shape, block.dtype),
-            pltpu.SemaphoreType.DMA,
-            pltpu.SemaphoreType.DMA((count,)),
+            pltpu.SemaphoreType.DMA((2,)),
+            pltpu.SemaphoreType.DMA((2 * count,)),
         ],
         compiler_params=pltpu.CompilerParams(vmem_limit_bytes=16 * MIB),
         name="copies",

time: 166 us -> 166 us (level)
  no operation moved by 1% of the time
where the time goes in v7:
time: 166 us; the launch traced here: 165 us
  blocking collectives  76 us (46%)
  waiting for transfers between devices  34.9 us (21%)
  starting transfers between devices  30 us (18%)
  Pallas kernels  21.3 us (13%)
    all_to_all x1, blocking collectives, per_device(): lax.all_to_all(term.reshape(chips, owned_rows, width), CHIPS, split_axis=...  30.6 us
    all_to_all x1, blocking collectives, per_device(): lax.all_to_all(owned.reshape(planes, 8, width // across), 'z', split_axis...  28.3 us
    all_to_all x1, blocking collectives, spread(): return lax.all_to_all(copies, axis, split_axis=0, concat_axis=0, tiled=True)  17.1 us
    all_to_all x1, waiting for transfers between devices, per_device(): lax.all_to_all(copies(hidden_weight, chips), CHIPS, split_axis=0, concat_...  17 us
    pallas_call x1, Pallas kernels, score(): pl.pallas_call(score_kernel, in_specs=[vmem, hbm, hbm, vmem, vmem], out_s...  9.45 us
    all_to_all x1, starting transfers between devices, per_device(): lax.all_to_all(message, CAND, split_axis=0, concat_axis=0, tiled=True)  9.32 us
    all_to_all x1, waiting for transfers between devices, per_device(): lax.all_to_all(message, CAND, split_axis=0, concat_axis=0, tiled=True)  9.05 us
    all_to_all x1, starting transfers between devices, per_device(): lax.all_to_all(squares(total, chips * cores), CAND, split_axis=0, concat_...  8.03 us
  transfers between devices with their start and end apart: 4, of which 4 were waited for; matrix products, arithmetic and copies ran while one was open for 1% of the time, Pallas kernels for 0%

profile of v7, /device:TPU:1, one launch (start us, length us, event | category | flops | bytes accessed | tf_op | source)
XLA Modules:
  0.0 165.0 jit_solution(12990836817307682744)
XLA Ops:
  0.6 2.5 %copies.1 = bf16[16,64,1024]{2,1,0:T(8,128)(2,1)} custom-call(bf16[64,1024]{1,0:T(8,128)(2,1)} %block_hbm.1), custom_call_target="tpu_custom_call" | custom-call | tf_op jit(solution)/shard_map/copies/pallas_call | solution.py:280
  3.1 0.0 copy-start.2
  3.1 0.0 copy-start
  3.2 0.0 copy-start.1
  3.2 7.7 %all-to-all-start = ((bf16[16,64,1024]{2,1,0:T(8,128)(2,1)}), bf16[16,64,1024]{2,1,0:T(8,128)(2,1)S(1)}, u32[]{:S(2)}, u32[]{:S(2)}) async-start(bf16[16,64,1024]{2,1,0:T(8,128)(2,1)} %copies.1), calls=%async_computation | async-start | bytes 4194304 | tf_op jit(solution)/shard_map/all_to_all | solution.py:347
  10.9 4.9 %collective-permute-start = (bf16[768,1024]{1,0:T(8,128)(2,1)}, bf16[768,1024]{1,0:T(8,128)(2,1)}, u32[]{:S(2)}, u32[]{:S(2)}) collective-permute-start(bf16[768,1024]{1,0:T(8,128)(2,1)} %bitcast.13), channel_id=1, source_target_pairs={{0,1},{1,0},{2,3},{3,2},{4,5},{5,4},{6,7},{7,6},{8,9},{9,8},{10,11... | collective-permute-start | bytes 4718600 | tf_op jit(solution)/shard_map/ppermute | solution.py:350
  15.8 0.0 copy-done.2
  15.8 0.1 reshape.44
  15.9 0.5 reshape.50.unit_ref
  16.4 0.0 copy-done
  16.4 0.0 copy-done.1
  16.4 0.1 reshape.45.code_ref
  16.5 2.6 %collective-permute-done.other_hbm = bf16[768,1024]{1,0:T(8,128)(2,1)} collective-permute-done((bf16[768,1024]{1,0:T(8,128)(2,1)}, bf16[768,1024]{1,0:T(8,128)(2,1)}, u32[]{:S(2)}, u32[]{:S(2)}) %collective-permute-start) | collective-permute-done | bytes 1572896 | tf_op jit(solution)/shard_map/ppermute | solution.py:350
  19.2 17.0 %all-to-all-done = bf16[16,64,1024]{2,1,0:T(8,128)(2,1)S(1)} async-done(((bf16[16,64,1024]{2,1,0:T(8,128)(2,1)}), bf16[16,64,1024]{2,1,0:T(8,128)(2,1)S(1)}, u32[]{:S(2)}, u32[]{:S(2)}) %all-to-all-start) | async-done | bytes 2097184 | tf_op jit(solution)/shard_map/all_to_all | solution.py:347
  36.2 0.0 copy-start.3
  36.2 9.4 %score.1 = (f32[1024,1536]{1,0:T(8,128)}, f32[32,1,2304]{2,1,0:T(1,128)}) custom-call(bf16[1024,1024]{1,0:T(8,128)(2,1)S(1)} %bitcast.10, bf16[768,1024]{1,0:T(8,128)(2,1)} %bitcast.14, bf16[768,1024]{1,0:T(8,128)(2,1)} %collective-permute-done.other_hbm, f32[1024,1]{1,0:T(8,128)S(1)} %reshape.50.unit_ref, f32[1,768]{1,0:T(1,128)S(1)} %reshape.45.code_ref), custom_call_target="tpu_custom_call" | custom-call | flops 3221225472 | bytes 12582912 | tf_op jit(solution)/shard_map/score/pallas_call | solution.py:102
  45.6 9.3 %all-to-all-start.1 = ((f32[32,1,2304]{2,1,0:T(1,128)}), f32[32,1,2304]{2,1,0:T(1,128)S(1)}, u32[]{:S(2)}, u32[]{:S(2)}) async-start(f32[32,1,2304]{2,1,0:T(1,128)} %get-tuple-element.6), calls=%async_computation.1 | async-start | bytes 589824 | tf_op jit(solution)/shard_map/all_to_all | solution.py:359
  55.0 0.0 copy-done.3
  55.0 0.1 broadcast_in_dim.4
  55.1 0.1 reshape_reshape.3.half_ref
  55.1 0.1 pad_add_fusion.place_ref
  55.2 9.0 %all-to-all-done.1.heard_ref = f32[32,1,2304]{2,1,0:T(1,128)S(1)} async-done(((f32[32,1,2304]{2,1,0:T(1,128)}), f32[32,1,2304]{2,1,0:T(1,128)S(1)}, u32[]{:S(2)}, u32[]{:S(2)}) %all-to-all-start.1) | async-done | bytes 294944 | tf_op jit(solution)/shard_map/all_to_all | solution.py:359
  64.3 7.9 %gradient_term.1 = (f32[2,768]{1,0:T(2,128)S(1)}, bf16[1024,1024]{1,0:T(8,128)(2,1)S(1)}) custom-call(s32[2]{0:T(128)S(1)} %pad_add_fusion.place_ref, f32[32,1,2304]{2,1,0:T(1,128)S(1)} %all-to-all-done.1.heard_ref, f32[1,768]{1,0:T(1,128)S(1)} %reshape_reshape.3.half_ref, f32[1024,1536]{1,0:T(8,128)} %get-tuple-element.7.slope_hbm, ...), custom_call_target="tpu_custom_call" | custom-call | flops 3221225472 | bytes 12582912 | tf_op jit(solution)/shard_map/gradient_term/pallas_call | solution.py:230
  72.2 30.6 %all_to_all.30 = bf16[16,64,1024]{2,1,0:T(8,128)(2,1)S(1)} all-to-all(bf16[16,64,1024]{2,1,0:T(8,128)(2,1)S(1)} %bitcast.11), channel_id=1, replica_groups=mesh['z'=16,'y'=4,'x'=4,'c'=2] {'y','x'}, dimensions={0} | all-to-all | bytes 4194304 | tf_op jit(solution)/shard_map/all_to_all | solution.py:362
  102.7 0.4 reduce_sum.24
  103.1 28.3 %all_to_all.31 = bf16[16,8,512]{2,1,0:T(8,128)(2,1)S(1)} all-to-all(bf16[16,8,512]{2,1,0:T(8,128)(2,1)S(1)} %bitcast.12), channel_id=1, replica_groups=mesh['z'=16,'y'=4,'x'=4,'c'=2] {'z'}, dimensions={0} | all-to-all | bytes 262144 | tf_op jit(solution)/shard_map/all_to_all | solution.py:368
  131.5 17.1 %all_to_all.32.total_ref = bf16[16,8,512]{2,1,0:T(8,128)(2,1)S(1)} all-to-all(bf16[16,8,512]{2,1,0:T(8,128)(2,1)S(1)} %broadcast_in_dim.10), channel_id=1, replica_groups=mesh['z'=16,'y'=4,'x'=4,'c'=2] {'z'}, dimensions={0} | all-to-all | bytes 262144 | tf_op jit(solution)/shard_map/all_to_all | solution.py:28
  148.6 0.7 squares.1
  149.3 8.0 %all-to-all-start.5 = ((f32[32,1,128]{2,1,0:T(1,128)}), f32[32,1,128]{2,1,0:T(1,128)S(1)}, u32[]{:S(2)}, u32[]{:S(2)}) async-start(f32[32,1,128]{2,1,0:T(1,128)} %squares.1), calls=%async_computation.5 | async-start | bytes 32768 | tf_op jit(solution)/shard_map/all_to_all | solution.py:374
  157.4 0.7 reshape_squeeze.3
  158.0 6.2 %all-to-all-done.5.heard_ref = f32[32,1,128]{2,1,0:T(1,128)S(1)} async-done(((f32[32,1,128]{2,1,0:T(1,128)}), f32[32,1,128]{2,1,0:T(1,128)S(1)}, u32[]{:S(2)}, u32[]{:S(2)}) %all-to-all-start.5) | async-done | bytes 16416 | tf_op jit(solution)/shard_map/all_to_all | solution.py:374
  164.2 0.8 scaled.1
  (6 shorter events, 0.1 us)
Async XLA Ops:
  3.1 12.7 %copy-start.2 = (bf16[2048]{0:T(1024)(128)(2,1)S(1)}, bf16[2048]{0:T(1024)(128)(2,1)}, u32[]{:S(2)}) copy-start(bf16[2048]{0:T(1024)(128)(2,1)} %param.8) | copy-start | bytes 12292
  3.1 13.3 %copy-start = (s32[24,32]{1,0:T(8,128)S(1)}, s32[24,32]{1,0:T(8,128)}, u32[]{:S(2)}) copy-start(s32[24,32]{1,0:T(8,128)} %param.9) | copy-start | bytes 9220
  3.2 13.3 %copy-start.1 = (s32[24,32]{1,0:T(8,128)S(1)}, s32[24,32]{1,0:T(8,128)}, u32[]{:S(2)}) copy-start(s32[24,32]{1,0:T(8,128)} %param.10) | copy-start | bytes 9220
  3.2 33.0 %all-to-all-start = ((bf16[16,64,1024]{2,1,0:T(8,128)(2,1)}), bf16[16,64,1024]{2,1,0:T(8,128)(2,1)S(1)}, u32[]{:S(2)}, u32[]{:S(2)}) async-start(bf16[16,64,1024]{2,1,0:T(8,128)(2,1)} %copies.1), calls=%async_computation | async-start | bytes 4194304 | tf_op jit(solution)/shard_map/all_to_all | solution.py:347
  10.9 8.3 %collective-permute-start = (bf16[768,1024]{1,0:T(8,128)(2,1)}, bf16[768,1024]{1,0:T(8,128)(2,1)}, u32[]{:S(2)}, u32[]{:S(2)}) collective-permute-start(bf16[768,1024]{1,0:T(8,128)(2,1)} %bitcast.13), channel_id=1, source_target_pairs={{0,1},{1,0},{2,3},{3,2},{4,5},{5,4},{6,7},{7,6},{8,9},{9,8},{10,11... | collective-permute-start | bytes 4718600 | tf_op jit(solution)/shard_map/ppermute | solution.py:350
  36.2 18.8 %copy-start.3 = (f32[24]{0:T(128)S(1)}, f32[24]{0:T(128)}, u32[]{:S(2)}) copy-start(f32[24]{0:T(128)} %param.11) | copy-start | bytes 292
  45.6 18.6 %all-to-all-start.1 = ((f32[32,1,2304]{2,1,0:T(1,128)}), f32[32,1,2304]{2,1,0:T(1,128)S(1)}, u32[]{:S(2)}, u32[]{:S(2)}) async-start(f32[32,1,2304]{2,1,0:T(1,128)} %get-tuple-element.6), calls=%async_computation.1 | async-start | bytes 589824 | tf_op jit(solution)/shard_map/all_to_all | solution.py:359
  149.3 14.9 %all-to-all-start.5 = ((f32[32,1,128]{2,1,0:T(1,128)}), f32[32,1,128]{2,1,0:T(1,128)S(1)}, u32[]{:S(2)}, u32[]{:S(2)}) async-start(f32[32,1,128]{2,1,0:T(1,128)} %squares.1), calls=%async_computation.5 | async-start | bytes 32768 | tf_op jit(solution)/shard_map/all_to_all | solution.py:374

commit v8 on v7

--- a/solution.py
+++ b/solution.py
@@ -11,7 +11,7 @@
 EPS = 1e-06
 GELU_A = 0.7978845608028654
 GELU_B = 0.044715
-CHIPS = ("y", "x")
+CHIPS = ("x", "y")
 CAND = ("y", "x", "c")
 MIB = 1 << 20
 LANES = 128
@@ -349,7 +349,12 @@
     ).reshape(chips * owned_rows, width)
     other = lax.ppermute(own, "c", [(0, 1), (1, 0)])
     unit = lax.dynamic_index_in_dim(
-        score_weight.reshape(chips, cores, owned_rows), core, 1, keepdims=False
+        score_weight.reshape(
+            lax.axis_size("y"), lax.axis_size("x"), cores, owned_rows
+        ).transpose(1, 0, 2, 3),
+        core,
+        2,
+        keepdims=False,
     ).reshape(chips * owned_rows, 1).astype(f32)
     code = (8 * rank_pos + relevance).astype(f32).reshape(1, groups * local)
     half = jnp.repeat(0.5 / ideal_dcg, local).reshape(1, groups * local)

time: 166 us -> 164 us (0.988)
  blocking collectives: 76 us -> 73 us
where the time goes in v8:
time: 164 us
  blocking collectives  73 us (45%)
  waiting for transfers between devices  34.9 us (21%)
  starting transfers between devices  31.5 us (19%)
  Pallas kernels  21.3 us (13%)
    all_to_all x1, blocking collectives, per_device(): lax.all_to_all(term.reshape(chips, owned_rows, width), CHIPS, split_axis=...  30.1 us
    all_to_all x1, blocking collectives, per_device(): lax.all_to_all(owned.reshape(planes, 8, width // across), 'z', split_axis...  27.1 us
    all_to_all x1, waiting for transfers between devices, per_device(): lax.all_to_all(copies(hidden_weight, chips), CHIPS, split_axis=0, concat_...  17.2 us
    all_to_all x1, blocking collectives, spread(): return lax.all_to_all(copies, axis, split_axis=0, concat_axis=0, tiled=True)  15.8 us
    all_to_all x1, starting transfers between devices, per_device(): lax.all_to_all(squares(total, chips * cores), CAND, split_axis=0, concat_...  9.68 us
    pallas_call x1, Pallas kernels, score(): pl.pallas_call(score_kernel, in_specs=[vmem, hbm, hbm, vmem, vmem], out_s...  9.44 us
    all_to_all x1, starting transfers between devices, per_device(): lax.all_to_all(message, CAND, split_axis=0, concat_axis=0, tiled=True)  9.22 us
    all_to_all x1, waiting for transfers between devices, per_device(): lax.all_to_all(message, CAND, split_axis=0, concat_axis=0, tiled=True)  8.93 us
  transfers between devices with their start and end apart: 4, of which 4 were waited for; matrix products, arithmetic and copies ran while one was open for 1% of the time, Pallas kernels for 0%

profile of v8, /device:TPU:1, one launch (start us, length us, event | category | flops | bytes accessed | tf_op | source)
XLA Modules:
  0.0 163.5 jit_solution(6901273000413311163)
XLA Ops:
  0.6 2.5 %copies.1 = bf16[16,64,1024]{2,1,0:T(8,128)(2,1)} custom-call(bf16[64,1024]{1,0:T(8,128)(2,1)} %block_hbm.1), custom_call_target="tpu_custom_call" | custom-call | tf_op jit(solution)/shard_map/copies/pallas_call | solution.py:280
  3.1 0.0 copy-start.2
  3.1 0.0 copy-start
  3.2 0.0 copy-start.1
  3.2 7.7 %all-to-all-start = ((bf16[16,64,1024]{2,1,0:T(8,128)(2,1)}), bf16[16,64,1024]{2,1,0:T(8,128)(2,1)S(1)}, u32[]{:S(2)}, u32[]{:S(2)}) async-start(bf16[16,64,1024]{2,1,0:T(8,128)(2,1)} %copies.1), calls=%async_computation | async-start | bytes 4194304 | tf_op jit(solution)/shard_map/all_to_all | solution.py:347
  10.9 4.9 %collective-permute-start = (bf16[768,1024]{1,0:T(8,128)(2,1)}, bf16[768,1024]{1,0:T(8,128)(2,1)}, u32[]{:S(2)}, u32[]{:S(2)}) collective-permute-start(bf16[768,1024]{1,0:T(8,128)(2,1)} %bitcast.17), channel_id=1, source_target_pairs={{0,1},{1,0},{2,3},{3,2},{4,5},{5,4},{6,7},{7,6},{8,9},{9,8},{10,11... | collective-permute-start | bytes 4718600 | tf_op jit(solution)/shard_map/ppermute | solution.py:350
  15.8 0.0 copy-done.2
  15.8 0.1 reshape.44
  15.9 0.5 reshape.50.unit_ref
  16.4 0.0 copy-done
  16.4 0.0 copy-done.1
  16.4 0.1 reshape.45.code_ref
  16.5 2.6 %collective-permute-done.other_hbm = bf16[768,1024]{1,0:T(8,128)(2,1)} collective-permute-done((bf16[768,1024]{1,0:T(8,128)(2,1)}, bf16[768,1024]{1,0:T(8,128)(2,1)}, u32[]{:S(2)}, u32[]{:S(2)}) %collective-permute-start) | collective-permute-done | bytes 1572896 | tf_op jit(solution)/shard_map/ppermute | solution.py:350
  19.1 17.2 %all-to-all-done = bf16[16,64,1024]{2,1,0:T(8,128)(2,1)S(1)} async-done(((bf16[16,64,1024]{2,1,0:T(8,128)(2,1)}), bf16[16,64,1024]{2,1,0:T(8,128)(2,1)S(1)}, u32[]{:S(2)}, u32[]{:S(2)}) %all-to-all-start) | async-done | bytes 2097184 | tf_op jit(solution)/shard_map/all_to_all | solution.py:347
  36.3 0.0 copy-start.3
  36.3 9.4 %score.1 = (f32[1024,1536]{1,0:T(8,128)}, f32[32,1,2304]{2,1,0:T(1,128)}) custom-call(bf16[1024,1024]{1,0:T(8,128)(2,1)S(1)} %bitcast.14, bf16[768,1024]{1,0:T(8,128)(2,1)} %bitcast.18, bf16[768,1024]{1,0:T(8,128)(2,1)} %collective-permute-done.other_hbm, f32[1024,1]{1,0:T(8,128)S(1)} %reshape.50.unit_ref, f32[1,768]{1,0:T(1,128)S(1)} %reshape.45.code_ref), custom_call_target="tpu_custom_call" | custom-call | flops 3221225472 | bytes 12582912 | tf_op jit(solution)/shard_map/score/pallas_call | solution.py:102
  45.8 9.2 %all-to-all-start.1 = ((f32[32,1,2304]{2,1,0:T(1,128)}), f32[32,1,2304]{2,1,0:T(1,128)S(1)}, u32[]{:S(2)}, u32[]{:S(2)}) async-start(f32[32,1,2304]{2,1,0:T(1,128)} %get-tuple-element.6), calls=%async_computation.1 | async-start | bytes 589824 | tf_op jit(solution)/shard_map/all_to_all | solution.py:364
  55.0 0.0 copy-done.3
  55.0 0.1 broadcast_in_dim.4
  55.1 0.1 reshape_reshape.3.half_ref
  55.2 0.1 pad_add_fusion.place_ref
  55.2 8.9 %all-to-all-done.1.heard_ref = f32[32,1,2304]{2,1,0:T(1,128)S(1)} async-done(((f32[32,1,2304]{2,1,0:T(1,128)}), f32[32,1,2304]{2,1,0:T(1,128)S(1)}, u32[]{:S(2)}, u32[]{:S(2)}) %all-to-all-start.1) | async-done | bytes 294944 | tf_op jit(solution)/shard_map/all_to_all | solution.py:364
  64.2 7.9 %gradient_term.1 = (f32[2,768]{1,0:T(2,128)S(1)}, bf16[1024,1024]{1,0:T(8,128)(2,1)S(1)}) custom-call(s32[2]{0:T(128)S(1)} %pad_add_fusion.place_ref, f32[32,1,2304]{2,1,0:T(1,128)S(1)} %all-to-all-done.1.heard_ref, f32[1,768]{1,0:T(1,128)S(1)} %reshape_reshape.3.half_ref, f32[1024,1536]{1,0:T(8,128)} %get-tuple-element.7.slope_hbm, ...), custom_call_target="tpu_custom_call" | custom-call | flops 3221225472 | bytes 12582912 | tf_op jit(solution)/shard_map/gradient_term/pallas_call | solution.py:230
  72.1 30.1 %all_to_all.30 = bf16[16,64,1024]{2,1,0:T(8,128)(2,1)S(1)} all-to-all(bf16[16,64,1024]{2,1,0:T(8,128)(2,1)S(1)} %bitcast.15), channel_id=1, replica_groups=mesh['z'=16,'y'=4,'x'=4,'c'=2] {'x','y'}, dimensions={0} | all-to-all | bytes 4194304 | tf_op jit(solution)/shard_map/all_to_all | solution.py:367
  102.2 0.4 reduce_sum.24
  102.6 27.1 %all_to_all.31 = bf16[16,8,512]{2,1,0:T(8,128)(2,1)S(1)} all-to-all(bf16[16,8,512]{2,1,0:T(8,128)(2,1)S(1)} %bitcast.16), channel_id=1, replica_groups=mesh['z'=16,'y'=4,'x'=4,'c'=2] {'z'}, dimensions={0} | all-to-all | bytes 262144 | tf_op jit(solution)/shard_map/all_to_all | solution.py:373
  129.7 15.8 %all_to_all.32.total_ref = bf16[16,8,512]{2,1,0:T(8,128)(2,1)S(1)} all-to-all(bf16[16,8,512]{2,1,0:T(8,128)(2,1)S(1)} %broadcast_in_dim.10), channel_id=1, replica_groups=mesh['z'=16,'y'=4,'x'=4,'c'=2] {'z'}, dimensions={0} | all-to-all | bytes 262144 | tf_op jit(solution)/shard_map/all_to_all | solution.py:28
  145.5 0.7 squares.1
  146.2 9.7 %all-to-all-start.5 = ((f32[32,1,128]{2,1,0:T(1,128)}), f32[32,1,128]{2,1,0:T(1,128)S(1)}, u32[]{:S(2)}, u32[]{:S(2)}) async-start(f32[32,1,128]{2,1,0:T(1,128)} %squares.1), calls=%async_computation.5 | async-start | bytes 32768 | tf_op jit(solution)/shard_map/all_to_all | solution.py:379
  155.9 0.7 reshape_squeeze.3
  156.6 6.2 %all-to-all-done.5.heard_ref = f32[32,1,128]{2,1,0:T(1,128)S(1)} async-done(((f32[32,1,128]{2,1,0:T(1,128)}), f32[32,1,128]{2,1,0:T(1,128)S(1)}, u32[]{:S(2)}, u32[]{:S(2)}) %all-to-all-start.5) | async-done | bytes 16416 | tf_op jit(solution)/shard_map/all_to_all | solution.py:379
  162.8 0.8 scaled.1
  (7 shorter events, 0.1 us)
Async XLA Ops:
  3.1 12.7 %copy-start.2 = (bf16[2048]{0:T(1024)(128)(2,1)S(1)}, bf16[2048]{0:T(1024)(128)(2,1)}, u32[]{:S(2)}) copy-start(bf16[2048]{0:T(1024)(128)(2,1)} %param.8) | copy-start | bytes 12292
  3.1 13.3 %copy-start = (s32[24,32]{1,0:T(8,128)S(1)}, s32[24,32]{1,0:T(8,128)}, u32[]{:S(2)}) copy-start(s32[24,32]{1,0:T(8,128)} %param.9) | copy-start | bytes 9220
  3.2 13.3 %copy-start.1 = (s32[24,32]{1,0:T(8,128)S(1)}, s32[24,32]{1,0:T(8,128)}, u32[]{:S(2)}) copy-start(s32[24,32]{1,0:T(8,128)} %param.10) | copy-start | bytes 9220
  3.2 33.2 %all-to-all-start = ((bf16[16,64,1024]{2,1,0:T(8,128)(2,1)}), bf16[16,64,1024]{2,1,0:T(8,128)(2,1)S(1)}, u32[]{:S(2)}, u32[]{:S(2)}) async-start(bf16[16,64,1024]{2,1,0:T(8,128)(2,1)} %copies.1), calls=%async_computation | async-start | bytes 4194304 | tf_op jit(solution)/shard_map/all_to_all | solution.py:347
  10.9 8.3 %collective-permute-start = (bf16[768,1024]{1,0:T(8,128)(2,1)}, bf16[768,1024]{1,0:T(8,128)(2,1)}, u32[]{:S(2)}, u32[]{:S(2)}) collective-permute-start(bf16[768,1024]{1,0:T(8,128)(2,1)} %bitcast.17), channel_id=1, source_target_pairs={{0,1},{1,0},{2,3},{3,2},{4,5},{5,4},{6,7},{7,6},{8,9},{9,8},{10,11... | collective-permute-start | bytes 4718600 | tf_op jit(solution)/shard_map/ppermute | solution.py:350
  36.3 18.7 %copy-start.3 = (f32[24]{0:T(128)S(1)}, f32[24]{0:T(128)}, u32[]{:S(2)}) copy-start(f32[24]{0:T(128)} %param.11) | copy-start | bytes 292
  45.8 18.4 %all-to-all-start.1 = ((f32[32,1,2304]{2,1,0:T(1,128)}), f32[32,1,2304]{2,1,0:T(1,128)S(1)}, u32[]{:S(2)}, u32[]{:S(2)}) async-start(f32[32,1,2304]{2,1,0:T(1,128)} %get-tuple-element.6), calls=%async_computation.1 | async-start | bytes 589824 | tf_op jit(solution)/shard_map/all_to_all | solution.py:364
  146.2 16.6 %all-to-all-start.5 = ((f32[32,1,128]{2,1,0:T(1,128)}), f32[32,1,128]{2,1,0:T(1,128)S(1)}, u32[]{:S(2)}, u32[]{:S(2)}) async-start(f32[32,1,128]{2,1,0:T(1,128)} %squares.1), calls=%async_computation.5 | async-start | bytes 32768 | tf_op jit(solution)/shard_map/all_to_all | solution.py:379

commit v9 on v8

--- a/solution.py
+++ b/solution.py
@@ -13,6 +13,7 @@
 GELU_B = 0.044715
 CHIPS = ("x", "y")
 CAND = ("y", "x", "c")
+EVERY = ("x", "y", "c")
 MIB = 1 << 20
 LANES = 128
 f32 = jnp.float32
@@ -341,7 +342,7 @@
     chips = lax.axis_size("y") * lax.axis_size("x")
     planes = lax.axis_size("z")
     core = lax.axis_index("c")
-    chip = lax.axis_index("y") * lax.axis_size("x") + lax.axis_index("x")
+    chip = lax.axis_index("x") * lax.axis_size("y") + lax.axis_index("y")
     own = embeddings.reshape(groups * local, width)
 
     weight = lax.all_to_all(
@@ -361,7 +362,7 @@
     place = jnp.stack([chip, core]).astype(jnp.int32)
 
     slope, message = score(weight, own, other, unit, code, chips * cores)
-    heard = lax.all_to_all(message, CAND, split_axis=0, concat_axis=0, tiled=True)
+    heard = lax.all_to_all(message, EVERY, split_axis=0, concat_axis=0, tiled=True)
     lam, term = gradient_term(heard, half, place, slope, own, other)
     lambdas = lam[0].reshape(groups, local)
     terms = lax.all_to_all(
@@ -377,7 +378,7 @@
     total = spread(piece, "z", planes)
     entries = owned_rows * width * chips * cores
     square = lax.all_to_all(
-        squares(total, chips * cores), CAND, split_axis=0, concat_axis=0, tiled=True
+        squares(total, chips * cores), EVERY, split_axis=0, concat_axis=0, tiled=True
     )
     return scaled(total, square, owned_rows, width, entries), lambdas
 

time: 164 us -> 164 us (level)
  no operation moved by 1% of the time
where the time goes in v9:
time: 164 us; the launch traced here: 163 us
  blocking collectives  72.8 us (44%)
  waiting for transfers between devices  35 us (21%)
  starting transfers between devices  31.4 us (19%)
  Pallas kernels  21.3 us (13%)
    all_to_all x1, blocking collectives, per_device(): lax.all_to_all(term.reshape(chips, owned_rows, width), CHIPS, split_axis=...  30 us
    all_to_all x1, blocking collectives, per_device(): lax.all_to_all(owned.reshape(planes, 8, width // across), 'z', split_axis...  27 us
    all_to_all x1, waiting for transfers between devices, per_device(): lax.all_to_all(copies(hidden_weight, chips), CHIPS, split_axis=0, concat_...  17.2 us
    all_to_all x1, blocking collectives, spread(): return lax.all_to_all(copies, axis, split_axis=0, concat_axis=0, tiled=True)  15.8 us
    all_to_all x1, starting transfers between devices, per_device(): lax.all_to_all(squares(total, chips * cores), EVERY, split_axis=0, concat...  9.53 us
    pallas_call x1, Pallas kernels, score(): pl.pallas_call(score_kernel, in_specs=[vmem, hbm, hbm, vmem, vmem], out_s...  9.44 us
    all_to_all x1, starting transfers between devices, per_device(): lax.all_to_all(message, EVERY, split_axis=0, concat_axis=0, tiled=True)  9.22 us
    all_to_all x1, waiting for transfers between devices, per_device(): lax.all_to_all(message, EVERY, split_axis=0, concat_axis=0, tiled=True)  9.03 us
  transfers between devices with their start and end apart: 4, of which 4 were waited for; matrix products, arithmetic and copies ran while one was open for 1% of the time, Pallas kernels for 0%

profile of v9, /device:TPU:1, one launch (start us, length us, event | category | flops | bytes accessed | tf_op | source)
XLA Modules:
  0.0 163.3 jit_solution(9878762331298594788)
XLA Ops:
  0.6 2.5 %copies.1 = bf16[16,64,1024]{2,1,0:T(8,128)(2,1)} custom-call(bf16[64,1024]{1,0:T(8,128)(2,1)} %block_hbm.1), custom_call_target="tpu_custom_call" | custom-call | tf_op jit(solution)/shard_map/copies/pallas_call | solution.py:281
  3.1 0.0 copy-start.2
  3.1 0.0 copy-start
  3.2 0.0 copy-start.1
  3.2 7.7 %all-to-all-start = ((bf16[16,64,1024]{2,1,0:T(8,128)(2,1)}), bf16[16,64,1024]{2,1,0:T(8,128)(2,1)S(1)}, u32[]{:S(2)}, u32[]{:S(2)}) async-start(bf16[16,64,1024]{2,1,0:T(8,128)(2,1)} %copies.1), calls=%async_computation | async-start | bytes 4194304 | tf_op jit(solution)/shard_map/all_to_all | solution.py:348
  10.9 4.9 %collective-permute-start = (bf16[768,1024]{1,0:T(8,128)(2,1)}, bf16[768,1024]{1,0:T(8,128)(2,1)}, u32[]{:S(2)}, u32[]{:S(2)}) collective-permute-start(bf16[768,1024]{1,0:T(8,128)(2,1)} %bitcast.17), channel_id=1, source_target_pairs={{0,1},{1,0},{2,3},{3,2},{4,5},{5,4},{6,7},{7,6},{8,9},{9,8},{10,11... | collective-permute-start | bytes 4718600 | tf_op jit(solution)/shard_map/ppermute | solution.py:351
  15.8 0.0 copy-done.2
  15.8 0.1 reshape.44
  15.9 0.5 reshape.50.unit_ref
  16.4 0.0 copy-done
  16.4 0.0 copy-done.1
  16.4 0.1 reshape.45.code_ref
  16.5 2.6 %collective-permute-done.other_hbm = bf16[768,1024]{1,0:T(8,128)(2,1)} collective-permute-done((bf16[768,1024]{1,0:T(8,128)(2,1)}, bf16[768,1024]{1,0:T(8,128)(2,1)}, u32[]{:S(2)}, u32[]{:S(2)}) %collective-permute-start) | collective-permute-done | bytes 1572896 | tf_op jit(solution)/shard_map/ppermute | solution.py:351
  19.1 17.2 %all-to-all-done = bf16[16,64,1024]{2,1,0:T(8,128)(2,1)S(1)} async-done(((bf16[16,64,1024]{2,1,0:T(8,128)(2,1)}), bf16[16,64,1024]{2,1,0:T(8,128)(2,1)S(1)}, u32[]{:S(2)}, u32[]{:S(2)}) %all-to-all-start) | async-done | bytes 2097184 | tf_op jit(solution)/shard_map/all_to_all | solution.py:348
  36.3 0.0 copy-start.3
  36.3 9.4 %score.1 = (f32[1024,1536]{1,0:T(8,128)}, f32[32,1,2304]{2,1,0:T(1,128)}) custom-call(bf16[1024,1024]{1,0:T(8,128)(2,1)S(1)} %bitcast.14, bf16[768,1024]{1,0:T(8,128)(2,1)} %bitcast.18, bf16[768,1024]{1,0:T(8,128)(2,1)} %collective-permute-done.other_hbm, f32[1024,1]{1,0:T(8,128)S(1)} %reshape.50.unit_ref, f32[1,768]{1,0:T(1,128)S(1)} %reshape.45.code_ref), custom_call_target="tpu_custom_call" | custom-call | flops 3221225472 | bytes 12582912 | tf_op jit(solution)/shard_map/score/pallas_call | solution.py:103
  45.8 9.2 %all-to-all-start.1 = ((f32[32,1,2304]{2,1,0:T(1,128)}), f32[32,1,2304]{2,1,0:T(1,128)S(1)}, u32[]{:S(2)}, u32[]{:S(2)}) async-start(f32[32,1,2304]{2,1,0:T(1,128)} %get-tuple-element.6), calls=%async_computation.1 | async-start | bytes 589824 | tf_op jit(solution)/shard_map/all_to_all | solution.py:365
  55.0 0.0 copy-done.3
  55.0 0.1 broadcast_in_dim.4
  55.1 0.1 reshape_reshape.3.half_ref
  55.2 0.1 pad_add_fusion.place_ref
  55.2 9.0 %all-to-all-done.1.heard_ref = f32[32,1,2304]{2,1,0:T(1,128)S(1)} async-done(((f32[32,1,2304]{2,1,0:T(1,128)}), f32[32,1,2304]{2,1,0:T(1,128)S(1)}, u32[]{:S(2)}, u32[]{:S(2)}) %all-to-all-start.1) | async-done | bytes 294944 | tf_op jit(solution)/shard_map/all_to_all | solution.py:365
  64.3 7.9 %gradient_term.1 = (f32[2,768]{1,0:T(2,128)S(1)}, bf16[1024,1024]{1,0:T(8,128)(2,1)S(1)}) custom-call(s32[2]{0:T(128)S(1)} %pad_add_fusion.place_ref, f32[32,1,2304]{2,1,0:T(1,128)S(1)} %all-to-all-done.1.heard_ref, f32[1,768]{1,0:T(1,128)S(1)} %reshape_reshape.3.half_ref, f32[1024,1536]{1,0:T(8,128)} %get-tuple-element.7.slope_hbm, ...), custom_call_target="tpu_custom_call" | custom-call | flops 3221225472 | bytes 12582912 | tf_op jit(solution)/shard_map/gradient_term/pallas_call | solution.py:231
  72.2 30.0 %all_to_all.30 = bf16[16,64,1024]{2,1,0:T(8,128)(2,1)S(1)} all-to-all(bf16[16,64,1024]{2,1,0:T(8,128)(2,1)S(1)} %bitcast.15), channel_id=1, replica_groups=mesh['z'=16,'y'=4,'x'=4,'c'=2] {'x','y'}, dimensions={0} | all-to-all | bytes 4194304 | tf_op jit(solution)/shard_map/all_to_all | solution.py:368
  102.2 0.4 reduce_sum.24
  102.6 27.0 %all_to_all.31 = bf16[16,8,512]{2,1,0:T(8,128)(2,1)S(1)} all-to-all(bf16[16,8,512]{2,1,0:T(8,128)(2,1)S(1)} %bitcast.16), channel_id=1, replica_groups=mesh['z'=16,'y'=4,'x'=4,'c'=2] {'z'}, dimensions={0} | all-to-all | bytes 262144 | tf_op jit(solution)/shard_map/all_to_all | solution.py:374
  129.6 15.8 %all_to_all.32.total_ref = bf16[16,8,512]{2,1,0:T(8,128)(2,1)S(1)} all-to-all(bf16[16,8,512]{2,1,0:T(8,128)(2,1)S(1)} %broadcast_in_dim.10), channel_id=1, replica_groups=mesh['z'=16,'y'=4,'x'=4,'c'=2] {'z'}, dimensions={0} | all-to-all | bytes 262144 | tf_op jit(solution)/shard_map/all_to_all | solution.py:29
  145.4 0.7 squares.1
  146.1 9.5 %all-to-all-start.5 = ((f32[32,1,128]{2,1,0:T(1,128)}), f32[32,1,128]{2,1,0:T(1,128)S(1)}, u32[]{:S(2)}, u32[]{:S(2)}) async-start(f32[32,1,128]{2,1,0:T(1,128)} %squares.1), calls=%async_computation.5 | async-start | bytes 32768 | tf_op jit(solution)/shard_map/all_to_all | solution.py:380
  155.7 0.7 reshape_squeeze.3
  156.4 6.2 %all-to-all-done.5.heard_ref = f32[32,1,128]{2,1,0:T(1,128)S(1)} async-done(((f32[32,1,128]{2,1,0:T(1,128)}), f32[32,1,128]{2,1,0:T(1,128)S(1)}, u32[]{:S(2)}, u32[]{:S(2)}) %all-to-all-start.5) | async-done | bytes 16416 | tf_op jit(solution)/shard_map/all_to_all | solution.py:380
  162.6 0.8 scaled.1
  (7 shorter events, 0.1 us)
Async XLA Ops:
  3.1 12.7 %copy-start.2 = (bf16[2048]{0:T(1024)(128)(2,1)S(1)}, bf16[2048]{0:T(1024)(128)(2,1)}, u32[]{:S(2)}) copy-start(bf16[2048]{0:T(1024)(128)(2,1)} %param.8) | copy-start | bytes 12292
  3.1 13.3 %copy-start = (s32[24,32]{1,0:T(8,128)S(1)}, s32[24,32]{1,0:T(8,128)}, u32[]{:S(2)}) copy-start(s32[24,32]{1,0:T(8,128)} %param.9) | copy-start | bytes 9220
  3.2 13.3 %copy-start.1 = (s32[24,32]{1,0:T(8,128)S(1)}, s32[24,32]{1,0:T(8,128)}, u32[]{:S(2)}) copy-start(s32[24,32]{1,0:T(8,128)} %param.10) | copy-start | bytes 9220
  3.2 33.2 %all-to-all-start = ((bf16[16,64,1024]{2,1,0:T(8,128)(2,1)}), bf16[16,64,1024]{2,1,0:T(8,128)(2,1)S(1)}, u32[]{:S(2)}, u32[]{:S(2)}) async-start(bf16[16,64,1024]{2,1,0:T(8,128)(2,1)} %copies.1), calls=%async_computation | async-start | bytes 4194304 | tf_op jit(solution)/shard_map/all_to_all | solution.py:348
  10.9 8.3 %collective-permute-start = (bf16[768,1024]{1,0:T(8,128)(2,1)}, bf16[768,1024]{1,0:T(8,128)(2,1)}, u32[]{:S(2)}, u32[]{:S(2)}) collective-permute-start(bf16[768,1024]{1,0:T(8,128)(2,1)} %bitcast.17), channel_id=1, source_target_pairs={{0,1},{1,0},{2,3},{3,2},{4,5},{5,4},{6,7},{7,6},{8,9},{9,8},{10,11... | collective-permute-start | bytes 4718600 | tf_op jit(solution)/shard_map/ppermute | solution.py:351
  36.3 18.7 %copy-start.3 = (f32[24]{0:T(128)S(1)}, f32[24]{0:T(128)}, u32[]{:S(2)}) copy-start(f32[24]{0:T(128)} %param.11) | copy-start | bytes 292
  45.8 18.5 %all-to-all-start.1 = ((f32[32,1,2304]{2,1,0:T(1,128)}), f32[32,1,2304]{2,1,0:T(1,128)S(1)}, u32[]{:S(2)}, u32[]{:S(2)}) async-start(f32[32,1,2304]{2,1,0:T(1,128)} %get-tuple-element.6), calls=%async_computation.1 | async-start | bytes 589824 | tf_op jit(solution)/shard_map/all_to_all | solution.py:365
  146.1 16.4 %all-to-all-start.5 = ((f32[32,1,128]{2,1,0:T(1,128)}), f32[32,1,128]{2,1,0:T(1,128)S(1)}, u32[]{:S(2)}, u32[]{:S(2)}) async-start(f32[32,1,128]{2,1,0:T(1,128)} %squares.1), calls=%async_computation.5 | async-start | bytes 32768 | tf_op jit(solution)/shard_map/all_to_all | solution.py:380
